TPU v7x, 32 devices: a whole 2x2x4 slice. The times are simulated.
32 devices in a mesh: group: 4 (over z), blk: 8 (over y, x, core).
Axes of the slice: x: 2, y: 2, z: 4, core: 2. Of those that a mesh axis runs over, the one named last changes fastest.
Arguments:
- image_a: float32 [3, 1024, 2048], P(None, 'group', 'blk'), may hold values from -6 to 6
- image_b: float32 [3, 1024, 2048], P(None, 'group', 'blk'), may hold values from -6 to 6
- initial: float32 [3, 1024, 2048], P(None, 'group', 'blk'), may hold values from -6 to 6
- coverage: int32 [4, 8], P('group', 'blk'), may hold values 0 or 1
- seam_label: int32 [4, 8], P('group', 'blk'), may hold values from 0 to 1
Outputs:
- blended: float32 [3, 1024, 2048], P(None, 'group', 'blk')
All inputs are finite; a program needn't handle non-finite values. No bound on the sum of `coverage` on one device may be relied on, other than what follows from the above.
Results may differ from a plain program's by a relative error of at most 0.00003.
Values sent between devices are 32-bit elements; how exact they have to be, the bound alone decides.
No kernel may reach another device: no remote copies, remote signals or barrier semaphores. Data moves between devices by JAX's collectives and lax.ppermute only.
A program may use at most 128 MiB of HBM per device.

v0:
```python
import jax
import jax.numpy as jnp
from jax import lax
from jax.sharding import PartitionSpec as P

BS = 256
LEVELS = 4
NU = 2
COARSE = 4


RELAX = 0.8


def padded_2(cells, sides, width):
    for axis, dim in sides:
        count = lax.axis_size(axis)
        ends = count - 1
        head = lax.slice_in_dim(cells, 0, width, axis=dim)
        tail = lax.slice_in_dim(cells, cells.shape[dim] - width, cells.shape[dim], axis=dim)
        cells = jnp.concatenate(
            [
                lax.ppermute(tail, axis, [(i, (i + 1) % count) for i in range(ends)]),
                cells,
                lax.ppermute(head, axis, [((i + 1) % count, i) for i in range(ends)]),
            ],
            axis=dim,
        )
    return cells


def beside_sum(padded):
    return padded[:, :-2, 1:-1] + padded[:, 2:, 1:-1] + padded[:, 1:-1, :-2] + padded[:, 1:-1, 2:]


def local_rim(field):
    return padded_2(field, (("group", 1), ("blk", 2)), 1)


def cell_map(table, span):
    return jnp.repeat(jnp.repeat(table, span, 0), span, 1)


def crop(field, margin):
    return field[:, margin:-margin, margin:-margin]


def smooth(approx, source, active, depth_index, sweeps):
    factor = 0.25**depth_index
    start = 0
    approx = RELAX * active * source / (4.0 * factor)
    start = 1
    for sweep in range(start, sweeps):
        approx = approx + RELAX * active * (
            source - factor * (4.0 * approx - beside_sum(local_rim(approx)))
        ) / (4.0 * factor)
    return approx


def shrink(field):
    chans, rows, cols = field.shape
    return field.reshape(chans, rows // 2, 2, cols // 2, 2).mean(axis=(2, 4))


def expand(field):
    return jnp.repeat(jnp.repeat(field, 2, 1), 2, 2)


def wide_sweep(approx_wide, source_wide, active_wide, factor):
    margin = (source_wide.shape[1] - approx_wide.shape[1]) // 2 + 1
    inner = crop(approx_wide, 1)
    source_in = crop(source_wide, margin)
    active_in = crop(active_wide, margin)
    return inner + RELAX * active_in * (
        source_in - factor * (4.0 * inner - beside_sum(approx_wide))
    ) / (4.0 * factor)


def deep_cycle(source, active, depth_index, coarser):
    factor = 0.25**depth_index
    chans = source.shape[0]
    if depth_index == LEVELS - 1:
        return smooth(None, source, active, depth_index, COARSE)
    joined = jnp.concatenate([source, active], 0)
    joined_wide = padded_2(joined, (("group", 1), ("blk", 2)), NU)
    source_wide = joined_wide[0:chans]
    active_wide = joined_wide[chans : chans + 1]
    approx_wide = RELAX * active_wide * source_wide / (4.0 * factor)
    approx_wide = wide_sweep(approx_wide, source_wide, active_wide, factor)
    leftover = active * (source - factor * (4.0 * crop(approx_wide, 1) - beside_sum(approx_wide)))
    approx = crop(approx_wide, 1)
    coarse_fix = coarser(shrink(leftover), depth_index + 1)
    approx = approx + active * expand(coarse_fix)
    approx_wide = padded_2(approx, (("group", 1), ("blk", 2)), NU)
    for sweep in range(NU):
        approx_wide = wide_sweep(approx_wide, source_wide, active_wide, factor)
    return approx_wide


def shards(image_a, image_b, initial, coverage, seam_label):
    stacked = jnp.concatenate([image_a, image_b, initial], 0)
    padded = padded_2(stacked, (("group", 1), ("blk", 2)), 1)
    laplace = 4.0 * stacked - beside_sum(padded)
    chans = image_a.shape[0]
    laplace_a = laplace[0:chans]
    laplace_b = laplace[chans : 2 * chans]
    laplace_x = laplace[2 * chans : 3 * chans]
    labels = cell_map(seam_label, BS)[None]
    guide = jnp.where(labels == 1, laplace_b, laplace_a)

    def active_at(depth_index):
        return cell_map(coverage, BS >> depth_index).astype(jnp.float32)[None]

    def local_cycle(source, active, depth_index):
        return deep_cycle(source, active, depth_index, coarser_local)

    def coarser_local(next_source, next_depth):
        return local_cycle(next_source, active_at(next_depth), next_depth)

    active_top = active_at(0)
    source = active_top * (guide - laplace_x)
    return initial + local_cycle(source, active_top, 0)


def solution(mesh):
    placed = (
        P(None, "group", "blk"),
        P(None, "group", "blk"),
        P(None, "group", "blk"),
        P("group", "blk"),
        P("group", "blk"),
    )
    return jax.shard_map(
        shards, mesh=mesh, in_specs=placed, out_specs=P(None, "group", "blk"), check_vma=False
    )
```

profile of v0, /device:TPU:12, one launch (start us, length us, event | category | flops | bytes accessed | tf_op | source)
XLA Modules:
  0.0 347.4 jit_solution(17166507432858309082)
XLA Ops:
  20.9 4.5 %collective-permute-start.3 = (f32[9,258,1]{1,2,0:T(1,128)S(1)}, f32[9,258,1]{1,2,0:T(1,128)S(1)}, u32[]{:S(2)}, u32[]{:S(2)}) collective-permute-start(f32[9,258,1]{1,2,0:T(1,128)S(1)} %get-tuple-element.6), channel_id=1, source_target_pairs={{1,0},{2,1},{3,2},{4,3},{5,4},{6,5},{7,6},{9,8},{10,9},{11,10},{12... | collective-permute-start | bytes 27872 | tf_op jit(solution)/shard_map/ppermute | solution.py:25
  26.9 6.7 %fusion.1 = f32[9,256,256]{1,2,0:T(8,128)S(1)} fusion(f32[9,258,1]{1,2,0:T(1,128)S(1)} %collective-permute-done.3, f32[9,1,256]{1,2,0:T(8,128)S(1)} %copy-done.6, f32[9,1,256]{1,2,0:T(8,128)S(1)} %copy-done.5, f32[3,256,256]{1,2,0:T(8,128)S(1)} %copy.42, f32[3,256,256]{1,2,0:T(8,128)} %copy-done.4, f32[3,256,256]{1,2,0:T(8,128)} %copy-done.3, ...), kind=kLoop, calls=%fused_computation.2 | loop fusion | flops 13565952 | bytes 4755600 | tf_op jit(solution)/shard_map/sub | solution.py:103
  39.9 10.4 %collective-permute-done.4 = f32[4,2,256]{1,2,0:T(8,128)S(1)} collective-permute-done((f32[4,2,256]{1,2,0:T(8,128)S(1)}, f32[4,2,256]{1,2,0:T(8,128)S(1)}, u32[]{:S(2)}, u32[]{:S(2)}) %collective-permute-start.4) | collective-permute-done | bytes 8224 | tf_op jit(solution)/shard_map/ppermute | solution.py:23
  55.6 4.5 %collective-permute-start.7 = (f32[4,260,2]{1,2,0:T(2,128)S(1)}, f32[4,260,2]{1,2,0:T(2,128)S(1)}, u32[]{:S(2)}, u32[]{:S(2)}) collective-permute-start(f32[4,260,2]{1,2,0:T(2,128)S(1)} %get-tuple-element.10), channel_id=1, source_target_pairs={{1,0},{2,1},{3,2},{4,3},{5,4},{6,5},{7,6},{9,8},{10,9},{11,10},{12... | collective-permute-start | bytes 24968 | tf_op jit(solution)/shard_map/ppermute | solution.py:25
  70.3 52.4 %reshape.45 = f32[3,128,2,128,2]{4,3,2,1,0:T(8,128)} reshape(f32[3,256,256]{2,1,0:T(8,128)} %copy.36) | data formatting | bytes 1572864 | tf_op jit(solution)/shard_map/reshape | solution.py:62
  122.7 19.3 %reduce_sum.27 = f32[3,128,128]{2,1,0:T(8,128)S(1)} reduce(f32[3,128,2,128,2]{4,3,2,1,0:T(8,128)} %reshape.45, f32[]{:T(128)} %constant.22.clone.1), dimensions={2,4}, to_apply=%region_0.1 | reduce | flops 147456 | bytes 983044 | tf_op jit(solution)/shard_map/reduce_sum | solution.py:62
  151.9 4.7 %collective-permute-start.11 = (f32[4,132,2]{2,1,0:T(8,128)S(1)}, f32[4,132,2]{2,1,0:T(8,128)S(1)}, u32[]{:S(2)}, u32[]{:S(2)}) collective-permute-start(f32[4,132,2]{2,1,0:T(8,128)S(1)} %get-tuple-element.18), channel_id=1, source_target_pairs={{1,0},{2,1},{3,2},{4,3},{5,4},{6,5},{7,6},{9,8},{10,9},{11,10},{12... | collective-permute-start | bytes 12680 | tf_op jit(solution)/shard_map/ppermute | solution.py:25
  156.6 3.9 %collective-permute-done.10 = f32[4,132,2]{2,1,0:T(8,128)S(1)} collective-permute-done((f32[4,132,2]{2,1,0:T(8,128)S(1)}, f32[4,132,2]{2,1,0:T(8,128)S(1)}, u32[]{:S(2)}, u32[]{:S(2)}) %collective-permute-start.10) | collective-permute-done | bytes 4256 | tf_op jit(solution)/shard_map/ppermute | solution.py:23
  163.4 14.8 %reshape.46 = f32[3,64,2,64,2]{4,3,2,1,0:T(8,128)} reshape(f32[3,128,128]{2,1,0:T(8,128)} %fusion.50) | data formatting | bytes 393216 | tf_op jit(solution)/shard_map/reshape | solution.py:62
  178.2 6.3 %reduce_sum.28 = f32[3,64,64]{2,1,0:T(8,128)S(1)} reduce(f32[3,64,2,64,2]{4,3,2,1,0:T(8,128)} %reshape.46, f32[]{:T(128)} %constant.22.clone.1), dimensions={2,4}, to_apply=%region_1.2 | reduce | flops 36864 | bytes 245764 | tf_op jit(solution)/shard_map/reduce_sum | solution.py:62
  186.4 3.9 %collective-permute-start.13 = (f32[4,2,64]{2,1,0:T(2,128)S(1)}, f32[4,2,64]{2,1,0:T(2,128)S(1)}, u32[]{:S(2)}, u32[]{:S(2)}) collective-permute-start(f32[4,2,64]{2,1,0:T(2,128)S(1)} %get-tuple-element.32), channel_id=1, source_target_pairs={{8,0},{16,8},{24,16},{9,1},{17,9},{25,17},{10,2},{18,10},{26,18},{... | collective-permute-start | bytes 6152 | tf_op jit(solution)/shard_map/ppermute | solution.py:25
  194.6 4.5 %collective-permute-start.15 = (f32[4,68,2]{2,1,0:T(8,128)}, f32[4,68,2]{2,1,0:T(8,128)}, u32[]{:S(2)}, u32[]{:S(2)}) collective-permute-start(f32[4,68,2]{2,1,0:T(8,128)} %get-tuple-element.26), channel_id=1, source_target_pairs={{1,0},{2,1},{3,2},{4,3},{5,4},{6,5},{7,6},{9,8},{10,9},{11,10},{12... | collective-permute-start | bytes 6536 | tf_op jit(solution)/shard_map/ppermute | solution.py:25
  204.9 5.1 %reshape.47 = f32[3,32,2,32,2]{4,3,2,1,0:T(8,128)} reshape(f32[3,64,64]{2,1,0:T(8,128)} %fusion.78) | data formatting | bytes 98304 | tf_op jit(solution)/shard_map/reshape | solution.py:62
  215.7 3.9 %collective-permute-start.17 = (f32[3,1,32]{2,1,0:T(1,128)S(1)}, f32[3,1,32]{2,1,0:T(1,128)S(1)}, u32[]{:S(2)}, u32[]{:S(2)}) collective-permute-start(f32[3,1,32]{2,1,0:T(1,128)S(1)} %get-tuple-element.44), channel_id=1, source_target_pairs={{8,0},{16,8},{24,16},{9,1},{17,9},{25,17},{10,2},{18,10},{26,18},{... | collective-permute-start | bytes 1160 | tf_op jit(solution)/shard_map/ppermute | solution.py:25
  223.9 4.5 %collective-permute-start.19 = (f32[3,34,1]{2,1,0:T(8,128)}, f32[3,34,1]{2,1,0:T(8,128)}, u32[]{:S(2)}, u32[]{:S(2)}) collective-permute-start(f32[3,34,1]{2,1,0:T(8,128)} %get-tuple-element.38), channel_id=1, source_target_pairs={{1,0},{2,1},{3,2},{4,3},{5,4},{6,5},{7,6},{9,8},{10,9},{11,10},{12... | collective-permute-start | bytes 1232 | tf_op jit(solution)/shard_map/ppermute | solution.py:25
  233.7 3.9 %collective-permute-start.21 = (f32[3,1,32]{2,1,0:T(1,128)S(1)}, f32[3,1,32]{2,1,0:T(1,128)S(1)}, u32[]{:S(2)}, u32[]{:S(2)}) collective-permute-start(f32[3,1,32]{2,1,0:T(1,128)S(1)} %get-tuple-element.42), channel_id=1, source_target_pairs={{8,0},{16,8},{24,16},{9,1},{17,9},{25,17},{10,2},{18,10},{26,18},{... | collective-permute-start | bytes 1160 | tf_op jit(solution)/shard_map/ppermute | solution.py:25
  241.2 4.5 %collective-permute-start.23 = (f32[3,34,1]{2,1,0:T(8,128)S(1)}, f32[3,34,1]{2,1,0:T(8,128)S(1)}, u32[]{:S(2)}, u32[]{:S(2)}) collective-permute-start(f32[3,34,1]{2,1,0:T(8,128)S(1)} %get-tuple-element.36), channel_id=1, source_target_pairs={{1,0},{2,1},{3,2},{4,3},{5,4},{6,5},{7,6},{9,8},{10,9},{11,10},{12... | collective-permute-start | bytes 1232 | tf_op jit(solution)/shard_map/ppermute | solution.py:25
  250.5 3.9 %collective-permute-start.25 = (f32[3,1,32]{2,1,0:T(1,128)S(1)}, f32[3,1,32]{2,1,0:T(1,128)S(1)}, u32[]{:S(2)}, u32[]{:S(2)}) collective-permute-start(f32[3,1,32]{2,1,0:T(1,128)S(1)} %get-tuple-element.40), channel_id=1, source_target_pairs={{8,0},{16,8},{24,16},{9,1},{17,9},{25,17},{10,2},{18,10},{26,18},{... | collective-permute-start | bytes 1160 | tf_op jit(solution)/shard_map/ppermute | solution.py:25
  258.0 4.5 %collective-permute-start.27 = (f32[3,34,1]{2,1,0:T(8,128)S(1)}, f32[3,34,1]{2,1,0:T(8,128)S(1)}, u32[]{:S(2)}, u32[]{:S(2)}) collective-permute-start(f32[3,34,1]{2,1,0:T(8,128)S(1)} %get-tuple-element.34), channel_id=1, source_target_pairs={{1,0},{2,1},{3,2},{4,3},{5,4},{6,5},{7,6},{9,8},{10,9},{11,10},{12... | collective-permute-start | bytes 1232 | tf_op jit(solution)/shard_map/ppermute | solution.py:25
  272.8 3.9 %collective-permute-start.29 = (f32[3,2,64]{2,1,0:T(2,128)S(1)}, f32[3,2,64]{2,1,0:T(2,128)S(1)}, u32[]{:S(2)}, u32[]{:S(2)}) collective-permute-start(f32[3,2,64]{2,1,0:T(2,128)S(1)} %get-tuple-element.30), channel_id=1, source_target_pairs={{8,0},{16,8},{24,16},{9,1},{17,9},{25,17},{10,2},{18,10},{26,18},{... | collective-permute-start | bytes 4616 | tf_op jit(solution)/shard_map/ppermute | solution.py:25
  280.4 4.5 %collective-permute-start.31 = (f32[3,68,2]{2,1,0:T(8,128)S(1)}, f32[3,68,2]{2,1,0:T(8,128)S(1)}, u32[]{:S(2)}, u32[]{:S(2)}) collective-permute-start(f32[3,68,2]{2,1,0:T(8,128)S(1)} %get-tuple-element.28), channel_id=1, source_target_pairs={{1,0},{2,1},{3,2},{4,3},{5,4},{6,5},{7,6},{9,8},{10,9},{11,10},{12... | collective-permute-start | bytes 4904 | tf_op jit(solution)/shard_map/ppermute | solution.py:25
  303.0 4.8 %collective-permute-start.35 = (f32[3,132,2]{2,1,0:T(8,128)S(1)}, f32[3,132,2]{2,1,0:T(8,128)S(1)}, u32[]{:S(2)}, u32[]{:S(2)}) collective-permute-start(f32[3,132,2]{2,1,0:T(8,128)S(1)} %get-tuple-element.20), channel_id=1, source_target_pairs={{1,0},{2,1},{3,2},{4,3},{5,4},{6,5},{7,6},{9,8},{10,9},{11,10},{12... | collective-permute-start | bytes 9512 | tf_op jit(solution)/shard_map/ppermute | solution.py:25
  321.8 3.9 %collective-permute-start.37 = (f32[3,2,256]{1,2,0:T(8,128)S(1)}, f32[3,2,256]{1,2,0:T(8,128)S(1)}, u32[]{:S(2)}, u32[]{:S(2)}) collective-permute-start(f32[3,2,256]{1,2,0:T(8,128)S(1)} %get-tuple-element.14), channel_id=1, source_target_pairs={{8,0},{16,8},{24,16},{9,1},{17,9},{25,17},{10,2},{18,10},{26,18},{... | collective-permute-start | bytes 18440 | tf_op jit(solution)/shard_map/ppermute | solution.py:25
  333.5 5.7 %collective-permute-start.39 = (f32[3,260,2]{1,2,0:T(2,128)S(1)}, f32[3,260,2]{1,2,0:T(2,128)S(1)}, u32[]{:S(2)}, u32[]{:S(2)}) collective-permute-start(f32[3,260,2]{1,2,0:T(2,128)S(1)} %get-tuple-element.12), channel_id=1, source_target_pairs={{1,0},{2,1},{3,2},{4,3},{5,4},{6,5},{7,6},{9,8},{10,9},{11,10},{12... | collective-permute-start | bytes 18728 | tf_op jit(solution)/shard_map/ppermute | solution.py:25
  (200 shorter events, 155.6 us)
Async XLA Ops:
  5.7 7.5 %collective-permute-start = (f32[9,1,256]{2,1,0:T(1,128)S(1)}, f32[9,1,256]{2,1,0:T(1,128)S(1)}, u32[]{:S(2)}, u32[]{:S(2)}) collective-permute-start(f32[9,1,256]{2,1,0:T(1,128)S(1)} %copy.30), channel_id=1, source_target_pairs={{0,8},{8,16},{16,24},{1,9},{9,17},{17,25},{2,10},{10,18},{18,26},{... | collective-permute-start | bytes 27656 | tf_op jit(solution)/shard_map/ppermute | solution.py:23
  19.0 7.8 %collective-permute-start.2 = (f32[9,258,1]{1,2,0:T(1,128)S(1)}, f32[9,258,1]{1,2,0:T(1,128)S(1)}, u32[]{:S(2)}, u32[]{:S(2)}) collective-permute-start(f32[9,258,1]{1,2,0:T(1,128)S(1)} %get-tuple-element.5), channel_id=1, source_target_pairs={{0,1},{1,2},{2,3},{3,4},{4,5},{5,6},{6,7},{8,9},{9,10},{10,11},{11... | collective-permute-start | bytes 27872 | tf_op jit(solution)/shard_map/ppermute | solution.py:23
  33.9 16.4 %collective-permute-start.4 = (f32[4,2,256]{1,2,0:T(8,128)S(1)}, f32[4,2,256]{1,2,0:T(8,128)S(1)}, u32[]{:S(2)}, u32[]{:S(2)}) collective-permute-start(f32[4,2,256]{1,2,0:T(8,128)S(1)} %get-tuple-element.15), channel_id=1, source_target_pairs={{0,8},{8,16},{16,24},{1,9},{9,17},{17,25},{2,10},{10,18},{18,26},{... | collective-permute-start | bytes 24584 | tf_op jit(solution)/shard_map/ppermute | solution.py:23
  37.4 16.1 %collective-permute-start.5 = (f32[4,2,256]{1,2,0:T(8,128)S(1)}, f32[4,2,256]{1,2,0:T(8,128)S(1)}, u32[]{:S(2)}, u32[]{:S(2)}) collective-permute-start(f32[4,2,256]{1,2,0:T(8,128)S(1)} %get-tuple-element.16), channel_id=1, source_target_pairs={{8,0},{16,8},{24,16},{9,1},{17,9},{25,17},{10,2},{18,10},{26,18},{... | collective-permute-start | bytes 24584 | tf_op jit(solution)/shard_map/ppermute | solution.py:25
  53.7 6.5 %collective-permute-start.6 = (f32[4,260,2]{1,2,0:T(2,128)S(1)}, f32[4,260,2]{1,2,0:T(2,128)S(1)}, u32[]{:S(2)}, u32[]{:S(2)}) collective-permute-start(f32[4,260,2]{1,2,0:T(2,128)S(1)} %get-tuple-element.9), channel_id=1, source_target_pairs={{0,1},{1,2},{2,3},{3,4},{4,5},{5,6},{6,7},{8,9},{9,10},{10,11},{11... | collective-permute-start | bytes 24968 | tf_op jit(solution)/shard_map/ppermute | solution.py:23
  149.9 10.6 %collective-permute-start.10 = (f32[4,132,2]{2,1,0:T(8,128)S(1)}, f32[4,132,2]{2,1,0:T(8,128)S(1)}, u32[]{:S(2)}, u32[]{:S(2)}) collective-permute-start(f32[4,132,2]{2,1,0:T(8,128)S(1)} %get-tuple-element.17), channel_id=1, source_target_pairs={{0,1},{1,2},{2,3},{3,4},{4,5},{5,6},{6,7},{8,9},{9,10},{10,11},{11... | collective-permute-start | bytes 12680 | tf_op jit(solution)/shard_map/ppermute | solution.py:23
  151.9 8.7 %collective-permute-start.11 = (f32[4,132,2]{2,1,0:T(8,128)S(1)}, f32[4,132,2]{2,1,0:T(8,128)S(1)}, u32[]{:S(2)}, u32[]{:S(2)}) collective-permute-start(f32[4,132,2]{2,1,0:T(8,128)S(1)} %get-tuple-element.18), channel_id=1, source_target_pairs={{1,0},{2,1},{3,2},{4,3},{5,4},{6,5},{7,6},{9,8},{10,9},{11,10},{12... | collective-permute-start | bytes 12680 | tf_op jit(solution)/shard_map/ppermute | solution.py:25
  192.7 7.7 %collective-permute-start.14 = (f32[4,68,2]{2,1,0:T(8,128)}, f32[4,68,2]{2,1,0:T(8,128)}, u32[]{:S(2)}, u32[]{:S(2)}) collective-permute-start(f32[4,68,2]{2,1,0:T(8,128)} %get-tuple-element.25), channel_id=1, source_target_pairs={{0,1},{1,2},{2,3},{3,4},{4,5},{5,6},{6,7},{8,9},{9,10},{10,11},{11... | collective-permute-start | bytes 6536 | tf_op jit(solution)/shard_map/ppermute | solution.py:23
  194.6 7.5 %collective-permute-start.15 = (f32[4,68,2]{2,1,0:T(8,128)}, f32[4,68,2]{2,1,0:T(8,128)}, u32[]{:S(2)}, u32[]{:S(2)}) collective-permute-start(f32[4,68,2]{2,1,0:T(8,128)} %get-tuple-element.26), channel_id=1, source_target_pairs={{1,0},{2,1},{3,2},{4,3},{5,4},{6,5},{7,6},{9,8},{10,9},{11,10},{12... | collective-permute-start | bytes 6536 | tf_op jit(solution)/shard_map/ppermute | solution.py:25
  222.0 6.7 %collective-permute-start.18 = (f32[3,34,1]{2,1,0:T(8,128)}, f32[3,34,1]{2,1,0:T(8,128)}, u32[]{:S(2)}, u32[]{:S(2)}) collective-permute-start(f32[3,34,1]{2,1,0:T(8,128)} %get-tuple-element.37), channel_id=1, source_target_pairs={{0,1},{1,2},{2,3},{3,4},{4,5},{5,6},{6,7},{8,9},{9,10},{10,11},{11... | collective-permute-start | bytes 1232 | tf_op jit(solution)/shard_map/ppermute | solution.py:23
  223.9 6.7 %collective-permute-start.19 = (f32[3,34,1]{2,1,0:T(8,128)}, f32[3,34,1]{2,1,0:T(8,128)}, u32[]{:S(2)}, u32[]{:S(2)}) collective-permute-start(f32[3,34,1]{2,1,0:T(8,128)} %get-tuple-element.38), channel_id=1, source_target_pairs={{1,0},{2,1},{3,2},{4,3},{5,4},{6,5},{7,6},{9,8},{10,9},{11,10},{12... | collective-permute-start | bytes 1232 | tf_op jit(solution)/shard_map/ppermute | solution.py:25
  239.3 6.5 %collective-permute-start.22 = (f32[3,34,1]{2,1,0:T(8,128)S(1)}, f32[3,34,1]{2,1,0:T(8,128)S(1)}, u32[]{:S(2)}, u32[]{:S(2)}) collective-permute-start(f32[3,34,1]{2,1,0:T(8,128)S(1)} %get-tuple-element.35), channel_id=1, source_target_pairs={{0,1},{1,2},{2,3},{3,4},{4,5},{5,6},{6,7},{8,9},{9,10},{10,11},{11... | collective-permute-start | bytes 1232 | tf_op jit(solution)/shard_map/ppermute | solution.py:23
  241.2 6.4 %collective-permute-start.23 = (f32[3,34,1]{2,1,0:T(8,128)S(1)}, f32[3,34,1]{2,1,0:T(8,128)S(1)}, u32[]{:S(2)}, u32[]{:S(2)}) collective-permute-start(f32[3,34,1]{2,1,0:T(8,128)S(1)} %get-tuple-element.36), channel_id=1, source_target_pairs={{1,0},{2,1},{3,2},{4,3},{5,4},{6,5},{7,6},{9,8},{10,9},{11,10},{12... | collective-permute-start | bytes 1232 | tf_op jit(solution)/shard_map/ppermute | solution.py:25
  256.0 6.5 %collective-permute-start.26 = (f32[3,34,1]{2,1,0:T(8,128)S(1)}, f32[3,34,1]{2,1,0:T(8,128)S(1)}, u32[]{:S(2)}, u32[]{:S(2)}) collective-permute-start(f32[3,34,1]{2,1,0:T(8,128)S(1)} %get-tuple-element.33), channel_id=1, source_target_pairs={{0,1},{1,2},{2,3},{3,4},{4,5},{5,6},{6,7},{8,9},{9,10},{10,11},{11... | collective-permute-start | bytes 1232 | tf_op jit(solution)/shard_map/ppermute | solution.py:23
  258.0 6.4 %collective-permute-start.27 = (f32[3,34,1]{2,1,0:T(8,128)S(1)}, f32[3,34,1]{2,1,0:T(8,128)S(1)}, u32[]{:S(2)}, u32[]{:S(2)}) collective-permute-start(f32[3,34,1]{2,1,0:T(8,128)S(1)} %get-tuple-element.34), channel_id=1, source_target_pairs={{1,0},{2,1},{3,2},{4,3},{5,4},{6,5},{7,6},{9,8},{10,9},{11,10},{12... | collective-permute-start | bytes 1232 | tf_op jit(solution)/shard_map/ppermute | solution.py:25
  278.5 7.0 %collective-permute-start.30 = (f32[3,68,2]{2,1,0:T(8,128)S(1)}, f32[3,68,2]{2,1,0:T(8,128)S(1)}, u32[]{:S(2)}, u32[]{:S(2)}) collective-permute-start(f32[3,68,2]{2,1,0:T(8,128)S(1)} %get-tuple-element.27), channel_id=1, source_target_pairs={{0,1},{1,2},{2,3},{3,4},{4,5},{5,6},{6,7},{8,9},{9,10},{10,11},{11... | collective-permute-start | bytes 4904 | tf_op jit(solution)/shard_map/ppermute | solution.py:23
  280.4 6.9 %collective-permute-start.31 = (f32[3,68,2]{2,1,0:T(8,128)S(1)}, f32[3,68,2]{2,1,0:T(8,128)S(1)}, u32[]{:S(2)}, u32[]{:S(2)}) collective-permute-start(f32[3,68,2]{2,1,0:T(8,128)S(1)} %get-tuple-element.28), channel_id=1, source_target_pairs={{1,0},{2,1},{3,2},{4,3},{5,4},{6,5},{7,6},{9,8},{10,9},{11,10},{12... | collective-permute-start | bytes 4904 | tf_op jit(solution)/shard_map/ppermute | solution.py:25
  293.4 6.0 %collective-permute-start.32 = (f32[3,2,128]{2,1,0:T(2,128)S(1)}, f32[3,2,128]{2,1,0:T(2,128)S(1)}, u32[]{:S(2)}, u32[]{:S(2)}) collective-permute-start(f32[3,2,128]{2,1,0:T(2,128)S(1)} %get-tuple-element.21), channel_id=1, source_target_pairs={{0,8},{8,16},{16,24},{1,9},{9,17},{17,25},{2,10},{10,18},{18,26},{... | collective-permute-start | bytes 9224 | tf_op jit(solution)/shard_map/ppermute | solution.py:23
  301.1 8.7 %collective-permute-start.34 = (f32[3,132,2]{2,1,0:T(8,128)S(1)}, f32[3,132,2]{2,1,0:T(8,128)S(1)}, u32[]{:S(2)}, u32[]{:S(2)}) collective-permute-start(f32[3,132,2]{2,1,0:T(8,128)S(1)} %get-tuple-element.19), channel_id=1, source_target_pairs={{0,1},{1,2},{2,3},{3,4},{4,5},{5,6},{6,7},{8,9},{9,10},{10,11},{11... | collective-permute-start | bytes 9512 | tf_op jit(solution)/shard_map/ppermute | solution.py:23
  303.0 7.8 %collective-permute-start.35 = (f32[3,132,2]{2,1,0:T(8,128)S(1)}, f32[3,132,2]{2,1,0:T(8,128)S(1)}, u32[]{:S(2)}, u32[]{:S(2)}) collective-permute-start(f32[3,132,2]{2,1,0:T(8,128)S(1)} %get-tuple-element.20), channel_id=1, source_target_pairs={{1,0},{2,1},{3,2},{4,3},{5,4},{6,5},{7,6},{9,8},{10,9},{11,10},{12... | collective-permute-start | bytes 9512 | tf_op jit(solution)/shard_map/ppermute | solution.py:25
  319.9 9.7 %collective-permute-start.36 = (f32[3,2,256]{1,2,0:T(8,128)S(1)}, f32[3,2,256]{1,2,0:T(8,128)S(1)}, u32[]{:S(2)}, u32[]{:S(2)}) collective-permute-start(f32[3,2,256]{1,2,0:T(8,128)S(1)} %get-tuple-element.13), channel_id=1, source_target_pairs={{0,8},{8,16},{16,24},{1,9},{9,17},{17,25},{2,10},{10,18},{18,26},{... | collective-permute-start | bytes 18440 | tf_op jit(solution)/shard_map/ppermute | solution.py:23
  321.8 9.7 %collective-permute-start.37 = (f32[3,2,256]{1,2,0:T(8,128)S(1)}, f32[3,2,256]{1,2,0:T(8,128)S(1)}, u32[]{:S(2)}, u32[]{:S(2)}) collective-permute-start(f32[3,2,256]{1,2,0:T(8,128)S(1)} %get-tuple-element.14), channel_id=1, source_target_pairs={{8,0},{16,8},{24,16},{9,1},{17,9},{25,17},{10,2},{18,10},{26,18},{... | collective-permute-start | bytes 18440 | tf_op jit(solution)/shard_map/ppermute | solution.py:25
  331.6 7.7 %collective-permute-start.38 = (f32[3,260,2]{1,2,0:T(2,128)S(1)}, f32[3,260,2]{1,2,0:T(2,128)S(1)}, u32[]{:S(2)}, u32[]{:S(2)}) collective-permute-start(f32[3,260,2]{1,2,0:T(2,128)S(1)} %get-tuple-element.11), channel_id=1, source_target_pairs={{0,1},{1,2},{2,3},{3,4},{4,5},{5,6},{6,7},{8,9},{9,10},{10,11},{11... | collective-permute-start | bytes 18728 | tf_op jit(solution)/shard_map/ppermute | solution.py:23
  333.5 7.1 %collective-permute-start.39 = (f32[3,260,2]{1,2,0:T(2,128)S(1)}, f32[3,260,2]{1,2,0:T(2,128)S(1)}, u32[]{:S(2)}, u32[]{:S(2)}) collective-permute-start(f32[3,260,2]{1,2,0:T(2,128)S(1)} %get-tuple-element.12), channel_id=1, source_target_pairs={{1,0},{2,1},{3,2},{4,3},{5,4},{6,5},{7,6},{9,8},{10,9},{11,10},{12... | collective-permute-start | bytes 18728 | tf_op jit(solution)/shard_map/ppermute | solution.py:25
  (40 other events, 283.9 us)
where the time goes:
time: 353 us; the launch traced here: 347 us
  starting transfers between devices  125 us (35%)
  local copies, waits for them, and re-layouts  108 us (31%)
  other arithmetic  59.2 us (17%)
  waiting for transfers between devices  53.1 us (15%)
    ppermute x20, starting transfers between devices, padded_2(): lax.ppermute(head, axis, [((i + 1) % count, i) for i in range(ends)])  82.8 us
    reshape x3, local copies, waits for them, and re-layouts, shrink(): return field.reshape(chans, rows // 2, 2, cols // 2, 2).mean(axis=(2, 4))  72.2 us
    ppermute x20, starting transfers between devices, padded_2(): lax.ppermute(tail, axis, [(i, (i + 1) % count) for i in range(ends)])  41.9 us
    ppermute x20, waiting for transfers between devices, padded_2(): lax.ppermute(head, axis, [((i + 1) % count, i) for i in range(ends)])  31 us
    reduce_sum x3, other arithmetic, shrink(): return field.reshape(chans, rows // 2, 2, cols // 2, 2).mean(axis=(2, 4))  28.6 us
    ppermute x20, waiting for transfers between devices, padded_2(): lax.ppermute(tail, axis, [(i, (i + 1) % count) for i in range(ends)])  22.1 us
    mul x6, local copies, waits for them, and re-layouts, deep_cycle(): approx = approx + active * expand(coarse_fix)  9.56 us
  transfers between devices with their start and end apart: 40, of which 26 were waited for; matrix products, arithmetic and copies ran while one was open for 1% of the time, Pallas kernels for 0%

commit v1 on v0

v1 whole, which is shorter than its diff:
```python
import functools

import jax
import jax.numpy as jnp
from jax import lax
from jax.experimental import pallas as pl
from jax.experimental.pallas import tpu as pltpu
from jax.sharding import PartitionSpec as P

LEVELS = 4
NU = 2
COARSE = 4
RELAX = 0.8

LANES = 128
HALO = 64
SPREAD = 18


def source_reach():
    need = 0
    for _ in range(LEVELS - 1):
        need = -(-(need + NU) // 2)
    need += COARSE - 1
    for _ in range(LEVELS - 1):
        need = 2 * need + NU
    return need


REACH = source_reach()
STRIP = REACH + 2
assert STRIP % 8 == 0 and STRIP <= HALO
A_LEFT, B_LEFT, ACT_LEFT, LAB_LEFT = 60, 61, 62, 63
A_RIGHT, B_RIGHT, ACT_RIGHT, LAB_RIGHT = 64, 65, 66, 67


def lane_ids(rows):
    return lax.broadcasted_iota(jnp.int32, (rows, LANES), 1)


def roll(tile, shift):
    return pltpu.roll(tile, shift % LANES, 1)


def spread_cell(tile, lane):
    return jnp.broadcast_to(tile[:, lane : lane + 1], tile.shape)


def prepare(a_ref, b_ref, x_ref, cover_ref, label_ref, source_ref, column_ref, even_ref, odd_ref, da, db):
    chans, rows, cols = a_ref.shape
    tiles = cols // LANES
    active = cover_ref[0, 0].astype(jnp.float32)
    marked = label_ref[0, 0].astype(jnp.float32)
    second = label_ref[0, 0] == 1
    on_even = lax.rem(lax.axis_index("group"), 2) == 0
    zero_row = jnp.zeros((8, LANES), jnp.float32)
    step = 32
    ids = lane_ids(step)
    for k in range(tiles):
        for buf in (da, db):
            buf[k, 0:8, :] = zero_row
            buf[k, rows + 8 : rows + 16, :] = zero_row

    def flags(n):
        out = jnp.where((ids[:n] == ACT_LEFT) | (ids[:n] == ACT_RIGHT), active, 0.0)
        return jnp.where((ids[:n] == LAB_LEFT) | (ids[:n] == LAB_RIGHT), marked, out)

    flag_lanes = flags(step)

    def channel(c, _):
        for k in range(tiles):
            at = pl.ds(k * LANES, LANES)
            for r in range(0, rows, step):
                x = x_ref[c, r : r + step, at]
                da[k, 8 + r : 8 + r + step, :] = a_ref[c, r : r + step, at] - x
                db[k, 8 + r : 8 + r + step, :] = b_ref[c, r : r + step, at] - x

        def pick(k, low, n):
            return jnp.where(second, db[k, low : low + n, :], da[k, low : low + n, :])

        for r in range(0, rows, step):
            mids = [pick(k, 8 + r, step) for k in range(tiles)]
            rights = [roll(t, 1) for t in mids]
            lefts = [roll(t, -1) for t in mids]
            found = []
            for k in range(tiles):
                below = jnp.where(ids == 0, rights[k - 1] if k else 0.0, rights[k])
                above = jnp.where(ids == LANES - 1, lefts[k + 1] if k + 1 < tiles else 0.0, lefts[k])
                beside = pick(k, 7 + r, step) + pick(k, 9 + r, step) + below + above
                found.append(active * (RELAX * mids[k] - 0.25 * RELAX * beside))
                source_ref[c, k, HALO + r : HALO + r + step, :] = found[k]
            first_a, first_b = da[0, 8 + r : 8 + r + step, :], db[0, 8 + r : 8 + r + step, :]
            last_a, last_b = da[tiles - 1, 8 + r : 8 + r + step, :], db[tiles - 1, 8 + r : 8 + r + step, :]
            cells = flag_lanes
            cells = jnp.where(ids == A_LEFT, spread_cell(first_a, 0), cells)
            cells = jnp.where(ids == B_LEFT, spread_cell(first_b, 0), cells)
            cells = jnp.where(ids == A_RIGHT, spread_cell(last_a, LANES - 1), cells)
            cells = jnp.where(ids == B_RIGHT, spread_cell(last_b, LANES - 1), cells)
            cells = jnp.where(ids < REACH, found[0], cells)
            cells = jnp.where(ids >= LANES - REACH, found[tiles - 1], cells)
            column_ref[c, HALO + r : HALO + r + step, :] = cells
        return 0

    lax.fori_loop(0, chans, channel, 0)

    def message(out, top):
        low = HALO if top else HALO + rows - STRIP
        line = 8 if top else 8 + rows - 1
        spot = STRIP - 2 if top else 0
        packed = zero_row
        eight = ids[:8]
        for t in range(STRIP // 8):
            for c in range(chans):
                lane = SPREAD * t + 6 * c
                moved = roll(column_ref[c, low + 8 * t : low + 8 * t + 8, :], lane - A_LEFT)
                packed = jnp.where((eight >= lane) & (eight < lane + 6), moved, packed)
        out[0, chans * STRIP :, :] = packed
        marks = jnp.where(eight < LANES // 2, active, marked)
        for k in range(1, tiles):
            out[k, chans * STRIP :, :] = marks
        for c in range(chans):
            for k in range(tiles):
                out[k, c * STRIP : (c + 1) * STRIP, :] = source_ref[c, k, low : low + STRIP, :]
                at = pl.ds(k * LANES, LANES)
                row = line - 8
                x = x_ref[c, row : row + 1, at]
                out[k, c * STRIP + spot : c * STRIP + spot + 1, :] = a_ref[c, row : row + 1, at] - x
                out[k, c * STRIP + spot + 1 : c * STRIP + spot + 2, :] = b_ref[c, row : row + 1, at] - x

    @pl.when(on_even)
    def _():
        message(even_ref, False)
        message(odd_ref, True)

    @pl.when(jnp.logical_not(on_even))
    def _():
        message(even_ref, True)
        message(odd_ref, False)


def join_rows(source_in, column_in, sent_even, sent_odd, got_even, got_odd, source_ref, column_ref, even_ref, odd_ref):
    chans, tiles, height, _ = source_ref.shape
    rows = height - 2 * HALO
    tail = chans * STRIP
    row_even = lax.rem(lax.axis_index("group"), 2) == 0
    col_even = lax.rem(lax.axis_index("blk"), 2) == 0
    ids = lane_ids(STRIP)
    one = lane_ids(1)

    def cells_of(c, low, n):
        left, right = source_ref[c, 0, low : low + n, :], source_ref[c, tiles - 1, low : low + n, :]
        return left, right

    def side(top, got, mine):
        low = HALO - STRIP if top else HALO + rows
        their_spot = 0 if top else STRIP - 2
        my_spot = STRIP - 2 if top else 0
        edge = HALO if top else HALO + rows - 1
        other = edge - 1 if top else edge + 1
        packed = got[0, tail:, :]
        marks = got[1, tail:, :]
        their_active, their_mark = spread_cell(marks, 0), spread_cell(marks, LANES // 2)
        own_row = column_ref[0, HALO : HALO + 8, :]
        my_active, my_mark = spread_cell(own_row, ACT_LEFT), spread_cell(own_row, LAB_LEFT)
        eight = ids[:8]
        flags = jnp.where((eight == ACT_LEFT) | (eight == ACT_RIGHT), their_active, their_mark)
        for c in range(chans):
            for k in range(tiles):
                source_ref[c, k, low : low + STRIP, :] = got[k, c * STRIP : (c + 1) * STRIP, :]
                their_a = got[k, c * STRIP + their_spot : c * STRIP + their_spot + 1, :]
                their_b = got[k, c * STRIP + their_spot + 1 : c * STRIP + their_spot + 2, :]
                my_a = mine[k, c * STRIP + my_spot : c * STRIP + my_spot + 1, :]
                my_b = mine[k, c * STRIP + my_spot + 1 : c * STRIP + my_spot + 2, :]
                for_mine = 0.25 * RELAX * my_active[:1] * jnp.where(my_mark[:1] == 1.0, their_b, their_a)
                for_theirs = 0.25 * RELAX * their_active[:1] * jnp.where(their_mark[:1] == 1.0, my_b, my_a)
                source_ref[c, k, edge : edge + 1, :] = source_ref[c, k, edge : edge + 1, :] - for_mine
                source_ref[c, k, other : other + 1, :] = source_ref[c, k, other : other + 1, :] - for_theirs
            for t in range(STRIP // 8):
                cells = roll(packed, A_LEFT - SPREAD * t - 6 * c)
                keep = (eight < ACT_LEFT) | (eight == A_RIGHT) | (eight == B_RIGHT)
                cells = jnp.where(keep, cells, flags)
                left, right = cells_of(c, low + 8 * t, 8)
                cells = jnp.where(eight < REACH, left, cells)
                cells = jnp.where(eight >= LANES - REACH, right, cells)
                column_ref[c, low + 8 * t : low + 8 * t + 8, :] = cells
            left, right = cells_of(c, edge, 1)
            cells = column_ref[c, edge : edge + 1, :]
            cells = jnp.where(one < REACH, left, cells)
            column_ref[c, edge : edge + 1, :] = jnp.where(one >= LANES - REACH, right, cells)

    @pl.when(row_even)
    def _():
        side(True, got_odd, sent_odd)
        side(False, got_even, sent_even)

    @pl.when(jnp.logical_not(row_even))
    def _():
        side(True, got_even, sent_even)
        side(False, got_odd, sent_odd)

    first = HALO - STRIP
    half = even_ref.shape[1]
    low_half = lane_ids(half) < LANES // 2

    def pack(out, right):
        for c in range(chans):
            upper = column_ref[c, first : first + half, :]
            lower = column_ref[c, first + half : first + 2 * half, :]
            if right:
                out[c] = jnp.where(low_half, roll(upper, LANES // 2), lower)
            else:
                out[c] = jnp.where(low_half, upper, roll(lower, LANES // 2))

    @pl.when(col_even)
    def _():
        pack(even_ref, True)
        pack(odd_ref, False)

    @pl.when(jnp.logical_not(col_even))
    def _():
        pack(even_ref, False)
        pack(odd_ref, True)


def bands(height, depth):
    halo = HALO >> depth
    return ((0, halo), (halo, height - halo), (height - halo, height))


def cycle(source_in, column_in, got_even, got_odd, x_ref, out_ref, side, *bufs):
    chans, own_tiles, height, _ = source_in.shape
    rows = height - 2 * HALO
    tiles = own_tiles + 1
    first = HALO - STRIP
    half = got_even.shape[1]
    col_even = lax.rem(lax.axis_index("blk"), 2) == 0
    levels = [bufs[5 * d : 5 * d + 5] for d in range(LEVELS)]

    low_half = lane_ids(half) < LANES // 2
    for c in range(chans):
        even, odd = got_even[c], got_odd[c]
        right = jnp.where(col_even, even, odd)
        left = jnp.where(col_even, odd, even)
        side[c, first : first + half, :] = jnp.where(low_half, right, roll(left, LANES // 2))
        side[c, first + half : first + 2 * half, :] = jnp.where(low_half, roll(right, LANES // 2), left)

    eight = lane_ids(8)
    in_low = eight < LANES // 2
    scale_mid, scale_side, mark_mid, mark_side = [], [], [], []
    for low, _ in ((HALO - 8, 0), (HALO, 0), (HALO + rows, 0)):
        mid, beside = column_in[0, low : low + 8, :], side[0, low : low + 8, :]
        scale_mid.append(spread_cell(mid, ACT_LEFT) * (0.25 * RELAX))
        mark_mid.append(spread_cell(mid, LAB_LEFT) == 1.0)
        scale_side.append(jnp.where(in_low, spread_cell(beside, ACT_LEFT), spread_cell(beside, ACT_RIGHT)) * (0.25 * RELAX))
        mark_side.append(jnp.where(in_low, spread_cell(beside, LAB_RIGHT), spread_cell(beside, LAB_LEFT)) == 1.0)

    def wide(mask, n):
        return jnp.broadcast_to(mask[:1], (n, LANES))

    def scales(band, n):
        return [wide(scale_mid[band], n)] * own_tiles + [wide(scale_side[band], n)]

    def pieces(depth, low, high, step):
        for band, (start, end) in enumerate(bands(height >> depth, depth)):
            start, end = max(start, low), min(end, high)
            while start < end:
                n = min(step, end - start)
                yield band, start, n
                start += n

    def swept(src, add, depth, band, r, n, keep=None):
        shift = 1 << depth
        ids = lane_ids(n)
        mids = [src[k, 8 + r : 8 + r + n, :] for k in range(tiles)]
        rights = [roll(t, shift) for t in mids]
        lefts = [roll(t, -shift) for t in mids]
        scale = scales(band, n)
        found = []
        for k in range(keep or tiles):
            below = jnp.where(ids < shift, rights[k - 1], rights[k])
            above = jnp.where(ids >= LANES - shift, lefts[(k + 1) % tiles], lefts[k])
            beside = (src[k, 7 + r : 7 + r + n, :] + src[k, 9 + r : 9 + r + n, :]) + (below + above)
            found.append(scale[k] * (mids[k] + beside) + add[k, 8 + r : 8 + r + n, :])
        return mids, found

    def restrict(rest, out, depth, low, high):
        shift = 1 << depth
        for r in range(low // 2, high // 2, 32):
            n = min(32, high // 2 - r)
            even = (lane_ids(n) & shift) == 0
            for k in range(tiles):
                total = rest[k, pl.ds(8 + 2 * r, n, stride=2), :] + rest[k, pl.ds(9 + 2 * r, n, stride=2), :]
                other = jnp.where(even, roll(total, -shift), roll(total, shift))
                out[k, 8 + r : 8 + r + n, :] = total + other

    def prolong(fix, out, depth, low, high):
        for band, r, n in pieces(depth + 1, low, high, 32):
            scale = scales(band, n)
            for k in range(tiles):
                value = fix[k, 8 + r : 8 + r + n, :] * (scale[k] * (4.0 / RELAX))
                out[k, pl.ds(8 + 2 * r, n, stride=2), :] = value
                out[k, pl.ds(9 + 2 * r, n, stride=2), :] = value

    def cycle_of(depth, low, high):
        src, one, two, rest, extra = levels[depth]
        step = 32
        if depth == LEVELS - 1:
            held = src
            for sweep in range(1, COARSE):
                into = (one, two)[sweep % 2]
                for band, r, n in pieces(depth, low, high, step):
                    _, found = swept(held, src, depth, band, r, n)
                    for k in range(tiles):
                        into[k, 8 + r : 8 + r + n, :] = found[k]
                held = into
            return held
        for band, r, n in pieces(depth, low, high, step):
            _, found = swept(src, src, depth, band, r, n)
            for k in range(tiles):
                one[k, 8 + r : 8 + r + n, :] = found[k]
        for band, r, n in pieces(depth, low, high, step):
            mids, found = swept(one, src, depth, band, r, n)
            for k in range(tiles):
                rest[k, 8 + r : 8 + r + n, :] = found[k] - mids[k]
        restrict(rest, levels[depth + 1][0], depth, low, high)
        fix = cycle_of(depth + 1, 0, height >> (depth + 1))
        if depth == 0:
            low, high = HALO - 8, HALO + rows + 8
        prolong(fix, extra, depth, low // 2, high // 2)
        for band, r, n in pieces(depth, low, high, step):
            for k in range(tiles):
                two[k, 8 + r : 8 + r + n, :] = one[k, 8 + r : 8 + r + n, :] + extra[k, 8 + r : 8 + r + n, :]
        for band, r, n in pieces(depth, low, high, step):
            _, found = swept(two, src, depth, band, r, n)
            for k in range(tiles):
                one[k, 8 + r : 8 + r + n, :] = found[k]
        if depth == 0:
            return one
        for band, r, n in pieces(depth, low, high, step):
            _, found = swept(one, src, depth, band, r, n)
            for k in range(tiles):
                two[k, 8 + r : 8 + r + n, :] = found[k]
        return two

    def channel(c, _):
        src = levels[0][0]
        for band, r, n in pieces(0, first, height - first, 32):
            ids = lane_ids(n)
            column, beside = column_in[c, r : r + n, :], side[c, r : r + n, :]
            theirs = jnp.where(wide(mark_mid[band], n), roll(beside, -1), beside)
            mine = jnp.where(wide(mark_side[band], n), roll(column, -1), column)
            scale = scales(band, n)
            for k in range(own_tiles):
                value = source_in[c, k, r : r + n, :]
                if k == 0:
                    value = value - jnp.where(ids == 0, scale[k] * roll(theirs, -A_RIGHT), 0.0)
                if k == own_tiles - 1:
                    value = value - jnp.where(ids == LANES - 1, scale[k] * roll(theirs, LANES - 1 - A_LEFT), 0.0)
                src[k, 8 + r : 8 + r + n, :] = value
            value = jnp.where((ids < REACH) | (ids >= LANES - REACH), beside, 0.0)
            value = value - jnp.where(ids == 0, scale[own_tiles] * roll(mine, -A_RIGHT), 0.0)
            value = value - jnp.where(ids == LANES - 1, scale[own_tiles] * roll(mine, LANES - 1 - A_LEFT), 0.0)
            src[own_tiles, 8 + r : 8 + r + n, :] = value
        one = cycle_of(0, first, height - first)
        for r in range(HALO, HALO + rows, 32):
            _, found = swept(one, src, 0, 1, r, 32, own_tiles)
            for k in range(own_tiles):
                at = pl.ds(k * LANES, LANES)
                out_ref[c, r - HALO : r - HALO + 32, at] = x_ref[c, r - HALO : r - HALO + 32, at] + found[k]
        return 0

    lax.fori_loop(0, chans, channel, 0)


def swaps(count, odd):
    pairs = [(i, i + 1) for i in range(odd, count - 1, 2)]
    return pairs + [(j, i) for i, j in pairs]


def shards(image_a, image_b, initial, coverage, seam_label):
    chans, rows, cols = image_a.shape
    tiles = cols // LANES
    height = rows + 2 * HALO
    vmem = pl.BlockSpec(memory_space=pltpu.VMEM)
    smem = pl.BlockSpec(memory_space=pltpu.SMEM)
    sds = functools.partial(jax.ShapeDtypeStruct, dtype=jnp.float32)
    params = pltpu.CompilerParams(vmem_limit_bytes=48 * 1024 * 1024)
    group, blk = lax.axis_size("group"), lax.axis_size("blk")
    central = sds((chans, tiles, height, LANES))
    column = sds((chans, height, LANES))
    upright = sds((tiles, chans * STRIP + 8, LANES))
    beside = sds((chans, (rows + 2 * STRIP) // 2, LANES))

    source, columns, sent_even, sent_odd = pl.pallas_call(
        prepare,
        out_shape=(central, column, upright, upright),
        in_specs=[vmem, vmem, vmem, smem, smem],
        out_specs=(vmem,) * 4,
        scratch_shapes=[pltpu.VMEM((tiles, rows + 16, LANES), jnp.float32)] * 2,
        compiler_params=params,
        name="prepare",
    )(image_a, image_b, initial, coverage, seam_label)
    got_even = lax.ppermute(sent_even, "group", swaps(group, 0))
    got_odd = lax.ppermute(sent_odd, "group", swaps(group, 1))

    source, columns, sent_even, sent_odd = pl.pallas_call(
        join_rows,
        out_shape=(central, column, beside, beside),
        in_specs=[vmem] * 6,
        out_specs=(vmem,) * 4,
        input_output_aliases={0: 0, 1: 1},
        compiler_params=params,
        name="join_rows",
    )(source, columns, sent_even, sent_odd, got_even, got_odd)
    got_even = lax.ppermute(sent_even, "blk", swaps(blk, 0))
    got_odd = lax.ppermute(sent_odd, "blk", swaps(blk, 1))

    scratch = [pltpu.VMEM((chans, height, LANES), jnp.float32)]
    for depth in range(LEVELS):
        scratch += [pltpu.VMEM((tiles + 1, (height >> depth) + 16, LANES), jnp.float32)] * 5
    return pl.pallas_call(
        cycle,
        out_shape=sds((chans, rows, cols)),
        in_specs=[vmem] * 5,
        out_specs=vmem,
        scratch_shapes=scratch,
        compiler_params=params,
        name="cycle",
    )(source, columns, got_even, got_odd, initial)


def solution(mesh):
    placed = (
        P(None, "group", "blk"),
        P(None, "group", "blk"),
        P(None, "group", "blk"),
        P("group", "blk"),
        P("group", "blk"),
    )
    return jax.shard_map(
        shards, mesh=mesh, in_specs=placed, out_specs=P(None, "group", "blk"), check_vma=False
    )
```

time: 353 us -> 40.3 us (0.11); the launches traced: 347 us -> 39.5 us
  starting transfers between devices: 125 us -> 8.62 us
  local copies, waits for them, and re-layouts: 108 us -> 3.4 us
  other arithmetic: 59.2 us -> 0 us
  waiting for transfers between devices: 53.1 us -> 12.4 us
  Pallas kernels: 0 us -> 13.8 us
    ppermute x40 -> x4, starting transfers between devices: 125 us -> 8.62 us  [the longest x1 4.59 us: shards(): got_odd = lax.ppermute(sent_odd, 'group', swaps(group, 1))]
    reshape x3 -> x0, local copies, waits for them, and re-layouts: 72.2 us -> none  [shrink(): return field.reshape(chans, rows // 2, 2, cols // 2, 2).mean(axis=(2, 4))]
    ppermute x40 -> x4, waiting for transfers between devices: 53.1 us -> 12.4 us  [the longest x1 8.1 us: shards(): got_odd = lax.ppermute(sent_odd, 'blk', swaps(blk, 1))]
    reduce_sum x3 -> x0, other arithmetic: 28.6 us -> none  [shrink(): return field.reshape(chans, rows // 2, 2, cols // 2, 2).mean(axis=(2, 4))]
    pallas_call x0 -> x3, Pallas kernels: none -> 13.8 us  [the longest x1 12.2 us: shards(): pl.pallas_call(cycle, out_shape=sds((chans, rows, cols)), in_specs=[vmem]...]
    add x12 -> x0, other arithmetic: 13.5 us -> none  [the longest x6 5.49 us: wide_sweep(): inner + RELAX * active_in * (source_in - factor * (4.0 * inner - beside_s...]
    mul x7 -> x0, local copies, waits for them, and re-layouts: 11.9 us -> none  [the longest x6 9.56 us: deep_cycle(): approx = approx + active * expand(coarse_fix)]
    slice x19 -> x0, local copies, waits for them, and re-layouts: 7.42 us -> none  [the longest x18 5.79 us: padded_2(): lax.slice_in_dim(cells, cells.shape[dim] - width, cells.shape[dim], axis=...]
  transfers between devices with their start and end apart: 40 -> 4, of which waited for: 26 -> 3; matrix products, arithmetic and copies ran while one was open for 1% -> 0% of each run, Pallas kernels for 0% -> 0%
where the time goes in v1:
time: 40.3 us; the launch traced here: 39.5 us
  Pallas kernels  13.8 us (34%)
  waiting for transfers between devices  12.4 us (31%)
  starting transfers between devices  8.62 us (21%)
  local copies, waits for them, and re-layouts  3.4 us (8%)
  between operations  1.35 us (3%)
    pallas_call x1, Pallas kernels, shards(): pl.pallas_call(cycle, out_shape=sds((chans, rows, cols)), in_specs=[vmem]...  12.2 us
    ppermute x1, waiting for transfers between devices, shards(): got_odd = lax.ppermute(sent_odd, 'blk', swaps(blk, 1))  8.1 us
    ppermute x1, starting transfers between devices, shards(): got_odd = lax.ppermute(sent_odd, 'group', swaps(group, 1))  4.59 us
    ppermute x1, starting transfers between devices, shards(): got_odd = lax.ppermute(sent_odd, 'blk', swaps(blk, 1))  3.43 us
    unnamed x8, local copies, waits for them, and re-layouts  3.4 us
    ppermute x1, waiting for transfers between devices, shards(): got_odd = lax.ppermute(sent_odd, 'group', swaps(group, 1))  3.02 us
    pallas_call x1, Pallas kernels, shards(): pl.pallas_call(prepare, out_shape=(central, column, upright, upright), in...  1.24 us
    ppermute x1, waiting for transfers between devices, shards(): got_even = lax.ppermute(sent_even, 'group', swaps(group, 0))  1.23 us
  transfers between devices with their start and end apart: 4, of which 3 were waited for; matrix products, arithmetic and copies ran while one was open for 0% of the time, Pallas kernels for 0%

profile of v1, /device:TPU:12, one launch (start us, length us, event | category | flops | bytes accessed | tf_op | source)
XLA Modules:
  0.0 39.5 jit_solution(12118009355270602389)
XLA Ops:
  1.3 0.0 copy-start
  1.3 1.1 %copy-done = f32[3,256,256]{2,1,0:T(8,128)S(1)} copy-done((f32[3,256,256]{2,1,0:T(8,128)S(1)}, f32[3,256,256]{2,1,0:T(8,128)}, u32[]{:S(2)}) %copy-start) | copy-done | bytes 786456
  2.4 0.0 copy-start.2
  2.4 1.1 %copy-done.2 = f32[3,256,256]{2,1,0:T(8,128)S(1)} copy-done((f32[3,256,256]{2,1,0:T(8,128)S(1)}, f32[3,256,256]{2,1,0:T(8,128)}, u32[]{:S(2)}) %copy-start.2) | copy-done | bytes 786456
  3.6 0.0 copy-start.3
  3.6 1.1 %copy-done.3 = f32[3,256,256]{2,1,0:T(8,128)S(1)} copy-done((f32[3,256,256]{2,1,0:T(8,128)S(1)}, f32[3,256,256]{2,1,0:T(8,128)}, u32[]{:S(2)}) %copy-start.3) | copy-done | bytes 786456
  4.7 1.2 %prepare.1 = (f32[3,2,384,128]{3,2,1,0:T(8,128)S(1)}, f32[3,384,128]{2,1,0:T(8,128)S(1)}, f32[2,176,128]{2,1,0:T(8,128)S(1)}, f32[2,176,128]{2,1,0:T(8,128)S(1)}) custom-call(f32[3,256,256]{2,1,0:T(8,128)S(1)} %copy-done.2, f32[3,256,256]{2,1,0:T(8,128)S(1)} %copy-done.3, f32[3,256,256]{2,1,0:T(8,128)S(1)} %copy-done, s32[1,1]{1,0:T(1,128)S(6)} %copy.10.cover_ref, ...), custom_call_target="tpu_custom_call" | custom-call | tf_op jit(solution)/shard_map/prepare/pallas_call | solution.py:394
  5.9 0.5 %collective-permute-start = (f32[2,176,128]{2,1,0:T(8,128)S(1)}, f32[2,176,128]{2,1,0:T(8,128)S(1)}, u32[]{:S(2)}, u32[]{:S(2)}) collective-permute-start(f32[2,176,128]{2,1,0:T(8,128)S(1)} %get-tuple-element.15.sent_even), channel_id=1, source_target_pairs={{0,8},{16,24},{8,0},{24,16},{1,9},{17,25},{9,1},{25,17},{2,10},{18... | collective-permute-start | bytes 540680 | tf_op jit(solution)/shard_map/ppermute | solution.py:403
  6.5 4.6 %collective-permute-start.1 = (f32[2,176,128]{2,1,0:T(8,128)S(1)}, f32[2,176,128]{2,1,0:T(8,128)S(1)}, u32[]{:S(2)}, u32[]{:S(2)}) collective-permute-start(f32[2,176,128]{2,1,0:T(8,128)S(1)} %get-tuple-element.16.sent_odd), channel_id=1, source_target_pairs={{8,16},{16,8},{9,17},{17,9},{10,18},{18,10},{11,19},{19,11},{12,20... | collective-permute-start | bytes 540680 | tf_op jit(solution)/shard_map/ppermute | solution.py:404
  11.1 1.2 %collective-permute-done.got_even = f32[2,176,128]{2,1,0:T(8,128)S(1)} collective-permute-done((f32[2,176,128]{2,1,0:T(8,128)S(1)}, f32[2,176,128]{2,1,0:T(8,128)S(1)}, u32[]{:S(2)}, u32[]{:S(2)}) %collective-permute-start) | collective-permute-done | bytes 180256 | tf_op jit(solution)/shard_map/ppermute | solution.py:403
  12.3 3.0 %collective-permute-done.1.got_odd = f32[2,176,128]{2,1,0:T(8,128)S(1)} collective-permute-done((f32[2,176,128]{2,1,0:T(8,128)S(1)}, f32[2,176,128]{2,1,0:T(8,128)S(1)}, u32[]{:S(2)}, u32[]{:S(2)}) %collective-permute-start.1) | collective-permute-done | bytes 180256 | tf_op jit(solution)/shard_map/ppermute | solution.py:404
  15.3 0.0 copy-start.1
  15.3 0.4 join_rows.1
  15.7 0.1 collective-permute-start.2
  15.8 3.4 %collective-permute-start.3 = (f32[3,184,128]{2,1,0:T(8,128)S(1)}, f32[3,184,128]{2,1,0:T(8,128)S(1)}, u32[]{:S(2)}, u32[]{:S(2)}) collective-permute-start(f32[3,184,128]{2,1,0:T(8,128)S(1)} %get-tuple-element.20), channel_id=1, source_target_pairs={{1,2},{3,4},{5,6},{2,1},{4,3},{6,5},{9,10},{11,12},{13,14},{10,9},... | collective-permute-start | bytes 847880 | tf_op jit(solution)/shard_map/ppermute | solution.py:416
  19.2 0.0 collective-permute-done.2.got_even
  19.3 8.1 %collective-permute-done.3.got_odd = f32[3,184,128]{2,1,0:T(8,128)S(1)} collective-permute-done((f32[3,184,128]{2,1,0:T(8,128)S(1)}, f32[3,184,128]{2,1,0:T(8,128)S(1)}, u32[]{:S(2)}, u32[]{:S(2)}) %collective-permute-start.3) | collective-permute-done | bytes 282656 | tf_op jit(solution)/shard_map/ppermute | solution.py:416
  27.3 0.0 copy-done.1
  27.3 12.2 %cycle.1 = f32[3,256,256]{2,1,0:T(8,128)} custom-call(f32[3,2,384,128]{3,2,1,0:T(8,128)S(1)} %get-tuple-element.17.source_in, f32[3,384,128]{2,1,0:T(8,128)S(1)} %get-tuple-element.18.column_in, f32[3,184,128]{2,1,0:T(8,128)S(1)} %collective-permute-done.2.got_even, f32[3,184,128]{2,1,0:T(8,128)S(1)} %collective-permute-done.3.got_odd, ...), custom_call_target="tpu_custom_call" | custom-call | tf_op jit(solution)/shard_map/cycle/pallas_call | solution.py:421
Async XLA Ops:
  1.3 1.1 %copy-start = (f32[3,256,256]{2,1,0:T(8,128)S(1)}, f32[3,256,256]{2,1,0:T(8,128)}, u32[]{:S(2)}) copy-start(f32[3,256,256]{2,1,0:T(8,128)} %x_ref.3) | copy-start | bytes 2359300
  2.4 1.1 %copy-start.2 = (f32[3,256,256]{2,1,0:T(8,128)S(1)}, f32[3,256,256]{2,1,0:T(8,128)}, u32[]{:S(2)}) copy-start(f32[3,256,256]{2,1,0:T(8,128)} %a_ref.1) | copy-start | bytes 2359300
  3.6 1.1 %copy-start.3 = (f32[3,256,256]{2,1,0:T(8,128)S(1)}, f32[3,256,256]{2,1,0:T(8,128)}, u32[]{:S(2)}) copy-start(f32[3,256,256]{2,1,0:T(8,128)} %b_ref.1) | copy-start | bytes 2359300
  5.9 6.4 %collective-permute-start = (f32[2,176,128]{2,1,0:T(8,128)S(1)}, f32[2,176,128]{2,1,0:T(8,128)S(1)}, u32[]{:S(2)}, u32[]{:S(2)}) collective-permute-start(f32[2,176,128]{2,1,0:T(8,128)S(1)} %get-tuple-element.15.sent_even), channel_id=1, source_target_pairs={{0,8},{16,24},{8,0},{24,16},{1,9},{17,25},{9,1},{25,17},{2,10},{18... | collective-permute-start | bytes 540680 | tf_op jit(solution)/shard_map/ppermute | solution.py:403
  6.5 8.9 %collective-permute-start.1 = (f32[2,176,128]{2,1,0:T(8,128)S(1)}, f32[2,176,128]{2,1,0:T(8,128)S(1)}, u32[]{:S(2)}, u32[]{:S(2)}) collective-permute-start(f32[2,176,128]{2,1,0:T(8,128)S(1)} %get-tuple-element.16.sent_odd), channel_id=1, source_target_pairs={{8,16},{16,8},{9,17},{17,9},{10,18},{18,10},{11,19},{19,11},{12,20... | collective-permute-start | bytes 540680 | tf_op jit(solution)/shard_map/ppermute | solution.py:404
  15.3 12.0 %copy-start.1 = (f32[3,256,256]{2,1,0:T(8,128)S(1)}, f32[3,256,256]{2,1,0:T(8,128)}, u32[]{:S(2)}) copy-start(f32[3,256,256]{2,1,0:T(8,128)} %x_ref.3) | copy-start | bytes 2359300
  15.7 3.5 %collective-permute-start.2 = (f32[3,184,128]{2,1,0:T(8,128)S(1)}, f32[3,184,128]{2,1,0:T(8,128)S(1)}, u32[]{:S(2)}, u32[]{:S(2)}) collective-permute-start(f32[3,184,128]{2,1,0:T(8,128)S(1)} %get-tuple-element.19), channel_id=1, source_target_pairs={{0,1},{2,3},{4,5},{6,7},{1,0},{3,2},{5,4},{7,6},{8,9},{10,11},{12,... | collective-permute-start | bytes 847880 | tf_op jit(solution)/shard_map/ppermute | solution.py:415
  15.8 11.5 %collective-permute-start.3 = (f32[3,184,128]{2,1,0:T(8,128)S(1)}, f32[3,184,128]{2,1,0:T(8,128)S(1)}, u32[]{:S(2)}, u32[]{:S(2)}) collective-permute-start(f32[3,184,128]{2,1,0:T(8,128)S(1)} %get-tuple-element.20), channel_id=1, source_target_pairs={{1,2},{3,4},{5,6},{2,1},{4,3},{6,5},{9,10},{11,12},{13,14},{10,9},... | collective-permute-start | bytes 847880 | tf_op jit(solution)/shard_map/ppermute | solution.py:416

commit v2 on v0

v2 whole, which is shorter than its diff:
```python
import functools

import jax
import jax.numpy as jnp
from jax import lax
from jax.experimental import pallas as pl
from jax.experimental.pallas import tpu as pltpu
from jax.sharding import PartitionSpec as P

LEVELS = 4
NU = 2
COARSE = 4
RELAX = 0.8
NEAR = 0.25 * RELAX

LANES = 128
HALF = LANES // 2
HALO = 64
STEP = 96


def source_reach():
    need = 0
    for _ in range(LEVELS - 1):
        need = -(-(need + NU) // 2)
    need += COARSE - 1
    for _ in range(LEVELS - 1):
        need = 2 * need + NU
    return need


REACH = source_reach()
STRIP = REACH + 2
assert STRIP % 8 == 0 and STRIP <= HALO
FIRST = HALO - STRIP
RIM = 8
SEAM = 6


def lane_ids(rows):
    return lax.broadcasted_iota(jnp.int32, (rows, LANES), 1)


def roll(tile, shift):
    return pltpu.roll(tile, shift % LANES, 1)


def spans(low, high, step=STEP):
    while low < high:
        yield low, min(step, high - low)
        low += step


def even_at(axis):
    return lax.rem(lax.axis_index(axis), 2) == 0


def own_source(mids, ups, downs, active):
    tiles = len(mids)
    rights = [roll(t, 1) for t in mids]
    lefts = [roll(t, -1) for t in mids]
    ids = lane_ids(mids[0].shape[0])
    found = []
    for k in range(tiles):
        before = jnp.where(ids == 0, rights[k - 1] if k else 0.0, rights[k])
        after = jnp.where(ids == LANES - 1, lefts[k + 1] if k + 1 < tiles else 0.0, lefts[k])
        beside = (ups[k] + downs[k]) + (before + after)
        found.append(active * (RELAX * mids[k] - NEAR * beside))
    return found


def staggered(items, begin, end, depth):
    waiting = []
    for item in items:
        waiting.append((item, begin(item)))
        if len(waiting) > depth:
            end(*waiting.pop(0))
    for each in waiting:
        end(*each)


def turn(src, shift, r, n):
    tiles = range(src.shape[0])
    return [roll(src[k, r : r + n, :], shift) for k in tiles], [roll(src[k, r : r + n, :], -shift) for k in tiles]


def swept(src, add, scale, shift, r, n, ring, turned, keep=None):
    tiles = src.shape[0]
    ids = lane_ids(n)
    mids = [src[k, r : r + n, :] for k in range(tiles)]
    rights, lefts = turned
    found = []
    for k in range(keep or tiles):
        before, after = rights[k], lefts[k]
        if tiles > 1 or not ring:
            before = jnp.where(ids < shift, rights[k - 1] if ring or k else 0.0, before)
            after = jnp.where(ids >= LANES - shift, lefts[(k + 1) % tiles] if ring or k + 1 < tiles else 0.0, after)
        beside = (src[k, r - 1 : r - 1 + n, :] + src[k, r + 1 : r + 1 + n, :]) + (before + after)
        more = add(k, r - 8, n) if callable(add) else add[k, r : r + n, :]
        found.append(scale[k] * (mids[k] + beside) + more)
    return mids, found


def restricted(rest, k, r, n, shift):
    total = rest[k, pl.ds(r, n, stride=2), :] + rest[k, pl.ds(r + 1, n, stride=2), :]
    even = (lane_ids(n) & shift) == 0
    return total + jnp.where(even, roll(total, -shift), roll(total, shift))


def strips(a_ref, b_ref, x_ref, cover_ref, label_ref, even_ref, odd_ref, picked, other_a, other_b, built):
    chans, rows, cols = a_ref.shape
    tiles = cols // LANES
    active = cover_ref[0, 0].astype(jnp.float32)
    marked = label_ref[0, 0].astype(jnp.float32)
    second = label_ref[0, 0] == 1
    eight = lane_ids(8)

    top = pl.program_id(0) == 0
    low = jnp.where(top, 0, rows - STRIP)
    line = jnp.where(top, 0, rows - 1)
    spot = jnp.where(top, STRIP - 2, 0)
    for k in range(tiles):
        for edge in (7, 8 + rows):
            picked[k, edge : edge + 1, :] = jnp.zeros((1, LANES), jnp.float32)
    packed = jnp.zeros((8, LANES), jnp.float32)
    for c in range(chans):
        for k in range(tiles):
            at = pl.ds(k * LANES, LANES)
            for r, n in spans(0, rows):
                x = x_ref[c, r : r + n, at]
                from_a, from_b = a_ref[c, r : r + n, at] - x, b_ref[c, r : r + n, at] - x
                other_a[k, r : r + n, :], other_b[k, r : r + n, :] = from_a, from_b
                picked[k, 8 + r : 8 + r + n, :] = jnp.where(second, from_b, from_a)
        start = pl.multiple_of(low, 8)
        parts = [[picked[k, pl.ds(start + 8 + s, STRIP), :] for k in range(tiles)] for s in (0, -1, 1)]
        for k, found in enumerate(own_source(*parts, active)):
            built[k, c * STRIP : (c + 1) * STRIP, :] = found
        for k in range(tiles):
            built[k, pl.ds(c * STRIP + spot, 1), :] = other_a[k, pl.ds(line, 1), :]
            built[k, pl.ds(c * STRIP + spot + 1, 1), :] = other_b[k, pl.ds(line, 1), :]
        for t in range(STRIP // 8):
            lane = 4 * (chans * t + c)
            at = pl.ds(start + 8 * t, 8)
            packed = jnp.where(eight == lane, roll(other_a[0, at, :], lane), packed)
            packed = jnp.where(eight == lane + 1, roll(other_b[0, at, :], lane + 1), packed)
            packed = jnp.where(eight == lane + 2, roll(other_a[tiles - 1, at, :], lane + 3), packed)
            packed = jnp.where(eight == lane + 3, roll(other_b[tiles - 1, at, :], lane + 4), packed)
    built[0, chans * STRIP :, :] = packed
    for k in range(1, tiles):
        built[k, chans * STRIP :, :] = jnp.where(eight < HALF, active, marked)

    by_odd = top == even_at("group")

    @pl.when(by_odd)
    def _():
        odd_ref[...] = built[...]

    @pl.when(jnp.logical_not(by_odd))
    def _():
        even_ref[...] = built[...]


def inside(a_ref, b_ref, x_ref, cover_ref, label_ref, source_ref, once_ref, seam_ref, coarse_ref, da, db, rest):
    chans, rows, cols = a_ref.shape
    tiles = cols // LANES
    active = cover_ref[0, 0].astype(jnp.float32)
    second = label_ref[0, 0] == 1
    for k in range(tiles):
        for buf in (da, db):
            buf[k, 0:8, :] = jnp.zeros((8, LANES), jnp.float32)
            buf[k, rows + 8 : rows + 16, :] = jnp.zeros((8, LANES), jnp.float32)
    scale = [active * NEAR] * tiles
    top, end = HALO, HALO + rows

    def pick(k, low, n):
        return jnp.where(second, db[k, low : low + n, :], da[k, low : low + n, :])

    def channel(c, _):
        for k in range(tiles):
            at = pl.ds(k * LANES, LANES)
            for r, n in spans(0, rows):
                x = x_ref[c, r : r + n, at]
                da[k, 8 + r : 8 + r + n, :] = a_ref[c, r : r + n, at] - x
                db[k, 8 + r : 8 + r + n, :] = b_ref[c, r : r + n, at] - x
        for r, n in spans(0, rows):
            parts = [[pick(k, 8 + s + r, n) for k in range(tiles)] for s in (0, -1, 1)]
            found = own_source(*parts, active)
            for k in range(tiles):
                source_ref[c, k, top + r : top + r + n, :] = found[k]
            ids = lane_ids(n)
            seam = jnp.where(ids < SEAM, found[0], roll(found[tiles - 1], HALF))
            at = pl.ds(8 + r, n)
            seam = jnp.where(ids == HALF, roll(da[tiles - 1, at, :], HALF + 1), seam)
            seam = jnp.where(ids == HALF + 1, roll(db[tiles - 1, at, :], HALF + 2), seam)
            seam = jnp.where(ids == LANES - 1, roll(da[0, at, :], -1), seam)
            seam_ref[c, top + r : top + r + n, :] = jnp.where(ids == LANES - 2, roll(db[0, at, :], -2), seam)
        source, once = source_ref.at[c], once_ref.at[c]

        def first(piece, turned):
            r, n = piece
            _, found = swept(source, source, scale, 1, r, n, False, turned)
            for k in range(tiles):
                once_ref[c, k, r : r + n, :] = found[k]

        def second_sweep(piece, turned):
            r, n = piece
            mids, found = swept(once, source, scale, 1, r, n, False, turned)
            for k in range(tiles):
                rest[k, r : r + n, :] = found[k] - mids[k]

        staggered(spans(top, end), lambda piece: turn(source, 1, *piece), first, 0)
        staggered(spans(top, end), lambda piece: turn(once, 1, *piece), second_sweep, 0)
        for r, n in spans(top // 2, end // 2):
            for k in range(tiles):
                coarse_ref[c, k, r : r + n, :] = restricted(rest, k, 2 * r, n, 1)
        return 0

    lax.fori_loop(0, chans, channel, 0)


def seam_units(chans, height):
    tiles_of = (height - 2 * FIRST) // 8
    for unit in range(chans * tiles_of):
        yield unit // tiles_of, FIRST + 8 * (unit % tiles_of), unit // 16, 8 * (unit % 16)


def message_rows(chans, height):
    quarter = height // 2
    cells = (chans // 2 * quarter + chans % 2 * quarter // 2) // 2
    units = -(-chans * ((height - 2 * FIRST) // 8) // 16) * 8
    return cells, units


def column_rows(chans, height):
    quarter = height // 2
    places = [(c, r, c + 1, r) for c in range(0, chans - 1, 2) for r in range(0, quarter, 8)]
    if chans % 2:
        places += [(chans - 1, r, chans - 1, r + quarter // 2) for r in range(0, quarter // 2, 8)]
    return places


def join_rows(
    source_in, once_in, seam_in, coarse_in, sent_even, sent_odd, got_even, got_odd, cover_ref, label_ref,
    source_ref, once_ref, seam_ref, coarse_ref, even_ref, odd_ref, rest, marks_ref, upper_got, lower_got, lines, left_out, right_out,
):
    chans, tiles, height, _ = source_ref.shape
    rows = height - 2 * HALO
    tail = chans * STRIP
    row_even, col_even = even_at("group"), even_at("blk")
    active = cover_ref[0, 0].astype(jnp.float32)
    marked = label_ref[0, 0].astype(jnp.float32)
    eight = lane_ids(8)

    def take(top, got):
        low = FIRST if top else HALO + rows
        their_spot = 0 if top else STRIP - 2
        my_spot = 0 if top else 2
        edge = HALO if top else HALO + rows - 1
        other = edge - 1 if top else edge + 1
        packed = got[0, tail:, :]
        marks = got[1, tail:, :]
        their_active = jnp.broadcast_to(marks[0:1, 0:1], (1, LANES))
        their_mark = jnp.broadcast_to(marks[0:1, HALF : HALF + 1], (1, LANES))
        band = 0 if top else 2
        marks_ref[band : band + 1, :] = their_active
        marks_ref[band + 3 : band + 4, :] = their_mark
        for c in range(chans):
            for k in range(tiles):
                source_ref[c, k, low : low + STRIP, :] = got[k, c * STRIP : (c + 1) * STRIP, :]
                their_a = got[k, c * STRIP + their_spot : c * STRIP + their_spot + 1, :]
                their_b = got[k, c * STRIP + their_spot + 1 : c * STRIP + their_spot + 2, :]
                my_a = lines[k, 4 * c + my_spot : 4 * c + my_spot + 1, :]
                my_b = lines[k, 4 * c + my_spot + 1 : 4 * c + my_spot + 2, :]
                for_mine = NEAR * active * jnp.where(marked == 1.0, their_b, their_a)
                for_theirs = NEAR * their_active * jnp.where(their_mark == 1.0, my_b, my_a)
                source_ref[c, k, edge : edge + 1, :] = source_ref[c, k, edge : edge + 1, :] - for_mine
                source_ref[c, k, other : other + 1, :] = source_ref[c, k, other : other + 1, :] - for_theirs
            for t in range(STRIP // 8):
                lane = 4 * (chans * t + c)
                last = roll(packed, HALF - lane - 2)
                once_a, once_b = roll(packed, LANES - 1 - lane), roll(packed, LANES - 2 - lane - 1)
                cells = jnp.where(eight == LANES - 1, once_a, jnp.where(eight == LANES - 2, once_b, last))
                r = low + 8 * t
                cells = jnp.where(eight < SEAM, source_ref[c, 0, r : r + 8, :], cells)
                end = roll(source_ref[c, tiles - 1, r : r + 8, :], HALF)
                seam_ref[c, r : r + 8, :] = jnp.where((eight >= HALF - SEAM) & (eight < HALF), end, cells)
            r = edge // 8 * 8
            cells = jnp.where(eight < SEAM, source_ref[c, 0, r : r + 8, :], seam_ref[c, r : r + 8, :])
            end = roll(source_ref[c, tiles - 1, r : r + 8, :], HALF)
            seam_ref[c, r : r + 8, :] = jnp.where((eight >= HALF - SEAM) & (eight < HALF), end, cells)

    def arrange(upper, lower, mine_up, mine_low):
        upper_got[...] = upper[...]
        lower_got[...] = lower[...]
        for c in range(chans):
            for k in range(tiles):
                lines[k, 4 * c : 4 * c + 2, :] = mine_up[k, (c + 1) * STRIP - 2 : (c + 1) * STRIP, :]
                lines[k, 4 * c + 2 : 4 * c + 4, :] = mine_low[k, c * STRIP : c * STRIP + 2, :]

    @pl.when(row_even)
    def _():
        arrange(got_odd, got_even, sent_odd, sent_even)

    @pl.when(jnp.logical_not(row_even))
    def _():
        arrange(got_even, got_odd, sent_even, sent_odd)

    take(True, upper_got)
    take(False, lower_got)
    marks_ref[1:2, :] = jnp.full((1, LANES), active)
    marks_ref[4:5, :] = jnp.full((1, LANES), marked)
    marks_ref[6:8, :] = jnp.zeros((2, LANES), jnp.float32)

    edges = ((FIRST, HALO, 0), (HALO, HALO + RIM, 1), (HALO + rows - RIM, HALO + rows, 1), (HALO + rows, height - FIRST, 2))
    spots = [(c, band, r, n) for c in range(chans) for low, high, band in edges for r, n in spans(low, high)]
    for stage in range(2):
        held = (source_ref, once_ref)[stage]

        def edge_sweep(spot, turned):
            c, band, r, n = spot
            scale = [jnp.broadcast_to(marks_ref[band : band + 1, :] * NEAR, (n, LANES))] * tiles
            mids, found = swept(held.at[c], source_ref.at[c], scale, 1, r, n, False, turned)
            for k in range(tiles):
                if stage == 0:
                    once_ref[c, k, r : r + n, :] = found[k]
                else:
                    rest[c, k, r : r + n, :] = found[k] - mids[k]

        staggered(spots, lambda spot: turn(held.at[spot[0]], 1, *spot[2:]), edge_sweep, 0)
    for c in range(chans):
        for low, high in ((FIRST, HALO + RIM), (HALO + rows - RIM, height - FIRST)):
            for k in range(tiles):
                coarse_ref[c, k, low // 2 : high // 2, :] = restricted(rest.at[c], k, low, (high - low) // 2, 1)
            zeros = jnp.zeros((FIRST // 2, LANES), jnp.float32)
        for k in range(tiles):
            coarse_ref[c, k, 0 : FIRST // 2, :] = zeros
            coarse_ref[c, k, (height - FIRST) // 2 : height // 2, :] = zeros

    cells, units = message_rows(chans, height)
    first_half = eight < HALF
    even_lane = (eight & 1) == 0

    def edge_cells(c, r):
        return jnp.where(first_half, coarse_ref[c, 0, r : r + 8, :], coarse_ref[c, tiles - 1, r : r + 8, :])

    def joined(place):
        c, r, d, s = place
        return jnp.where(even_lane, edge_cells(c, r), edge_cells(d, s))

    def pack(left, right):
        places = column_rows(chans, height)
        for t in range(cells // 8):
            upper, lower = joined(places[t]), joined(places[t + cells // 8])
            left[8 * t : 8 * t + 8, :] = jnp.where(first_half, upper, roll(lower, HALF))
            right[8 * t : 8 * t + 8, :] = jnp.where(first_half, roll(upper, HALF), lower)
        lefts = rights = jnp.zeros((8, LANES), jnp.float32)
        last = None
        for c, r, tile, lane in [*seam_units(chans, height), (None, None, -1, 0)]:
            if tile != last and last is not None:
                at = cells + 8 * last
                left[at : at + 8, :], right[at : at + 8, :] = lefts, rights
            last = tile
            if c is None:
                break
            value = seam_ref[c, r : r + 8, :]
            spot = (eight >= lane) & (eight < lane + 8)
            lefts = jnp.where(spot, roll(value, lane + 2), lefts)
            rights = jnp.where(spot, roll(value, lane - (HALF - SEAM)), rights)
        for out in (left, right):
            out[cells + units : cells + units + 8, :] = marks_ref[...]

    pack(left_out, right_out)

    @pl.when(col_even)
    def _():
        odd_ref[...] = left_out[...]
        even_ref[...] = right_out[...]

    @pl.when(jnp.logical_not(col_even))
    def _():
        even_ref[...] = left_out[...]
        odd_ref[...] = right_out[...]


def cycle(
    source_in, once_in, seam_in, coarse_in, sent_even, got_even, got_odd, x_ref, out_ref,
    right_ref, left_ref, seam_source, seam_once, seam_rest, fine, fine_two, *bufs,
):
    chans, own_tiles, height, _ = source_in.shape
    rows = height - 2 * HALO
    tiles = own_tiles + 1
    cells, units = message_rows(chans, height)
    col_even = even_at("blk")
    eight = lane_ids(8)

    @pl.when(col_even)
    def _():
        right_ref[...] = got_even[...]
        left_ref[...] = got_odd[...]

    @pl.when(jnp.logical_not(col_even))
    def _():
        right_ref[...] = got_odd[...]
        left_ref[...] = got_even[...]

    at = cells + units

    def mark(ref, row):
        return jnp.broadcast_to(ref[at + row : at + row + 1, :], (8, LANES))

    own = [mark(sent_even, i) for i in range(6)]
    right = [mark(right_ref, i) for i in range(6)]
    left = [mark(left_ref, i) for i in range(6)]
    quarter3 = eight < HALF + HALF // 2
    first_half = eight < HALF

    def mixed(i):
        return jnp.where(first_half, own[i], jnp.where(quarter3, right[i], left[i]))

    seam_scale = [mixed(i) * NEAR for i in range(3)]
    seam_mark = [mixed(i + 3) == 1.0 for i in range(3)]
    own_scale = [own[i] * NEAR for i in range(3)]
    side_scale = [jnp.where(first_half, right[i], left[i]) * NEAR for i in range(3)]

    def wide(mask, n):
        return jnp.broadcast_to(mask[:1], (n, LANES))

    def over_rows(kinds, depth, r, n):
        full, halo = height >> depth, HALO >> depth
        ends = ((0, halo), (halo, full - halo), (full - halo, full))
        parts = [(max(a, r), min(b, r + n), kind) for (a, b), kind in zip(ends, kinds)]
        parts = [wide(kind, b - a) for a, b, kind in parts if b > a]
        return parts[0] if len(parts) == 1 else jnp.concatenate(parts, axis=0)

    def scales(depth, r, n):
        return [over_rows(own_scale, depth, r, n)] * own_tiles + [over_rows(side_scale, depth, r, n)]

    inner = (eight < SEAM) | ((eight >= HALF - SEAM) & (eight < HALF))
    outer = ((eight >= HALF) & (eight < HALF + SEAM)) | (eight >= LANES - SEAM)
    from_near = (eight == 0) | (eight == HALF - 1)
    from_own = (eight == HALF) | (eight == LANES - 1)
    up_one = (eight == HALF - 1) | (eight == LANES - 1)
    near_b = (eight == HALF - 2) | (eight == 1)
    right_unit = (eight >= HALF - 2) & (eight < HALF + SEAM)
    def unpack(unit):
        c, r, tile, lane = unit
        rights = roll(right_ref[cells + 8 * tile : cells + 8 * tile + 8, :], HALF - 2 - lane)
        lefts = roll(left_ref[cells + 8 * tile : cells + 8 * tile + 8, :], LANES - SEAM - lane)
        return rights, lefts

    def keep_near(unit, turned):
        c, r, _, _ = unit
        seam_rest[c, 0, r : r + 8, :] = jnp.where(right_unit, *turned)

    def second_cells(unit):
        c, r, _, _ = unit
        cells_b = jnp.where(near_b, seam_rest[c, 0, r : r + 8, :], seam_in[c, r : r + 8, :])
        return roll(cells_b, 1), roll(cells_b, -1)

    def put_seam(unit, turned):
        c, r, _, _ = unit
        band = 0 if r < HALO else 1 if r < HALO + rows else 2
        near, mine = seam_rest[c, 0, r : r + 8, :], seam_in[c, r : r + 8, :]
        value = jnp.where(inner, mine, jnp.where(outer, near, 0.0))
        border = jnp.where(seam_mark[band], jnp.where(up_one, *turned), jnp.where(from_near, near, mine))
        border = jnp.where(from_near | from_own, border, 0.0)
        seam_source[c, 0, r : r + 8, :] = value - seam_scale[band] * border

    units_of = list(seam_units(chans, height))
    staggered(units_of, unpack, keep_near, 24)
    staggered(units_of, second_cells, put_seam, 24)
    spots = [(c, r, n) for c in range(chans) for r, n in spans(FIRST, height - FIRST, 2 * STEP)]

    def seam_first(spot, turned):
        c, r, n = spot
        source = seam_source.at[c]
        _, found = swept(source, source, [over_rows(seam_scale, 0, r, n)], 1, r, n, True, turned)
        seam_once[c, 0, r : r + n, :] = found[0]

    def seam_second(spot, turned):
        c, r, n = spot
        scale = [over_rows(seam_scale, 0, r, n)]
        mids, found = swept(seam_once.at[c], seam_source.at[c], scale, 1, r, n, True, turned)
        seam_rest[c, 0, r : r + n, :] = found[0] - mids[0]

    staggered(spots, lambda spot: turn(seam_source.at[spot[0]], 1, *spot[1:]), seam_first, 0)
    staggered(spots, lambda spot: turn(seam_once.at[spot[0]], 1, *spot[1:]), seam_second, 0)

    one_src, one_once, one_two = bufs[0:3]
    half_rows = height // 2
    eights = lane_ids(8)
    even_lane = (eights & 1) == 0
    places = column_rows(chans, height)
    for t, (c, r, d, s) in enumerate(places):
        low, upper = (8 * t, True) if t < cells // 8 else (8 * t - cells, False)
        from_right, from_left = right_ref[low : low + 8, :], left_ref[low : low + 8, :]
        if upper:
            value = jnp.where(first_half, from_right, roll(from_left, HALF))
        else:
            value = jnp.where(first_half, roll(from_right, HALF), from_left)
        one_src[c, own_tiles, 8 + r : 16 + r, :] = jnp.where(even_lane, value, roll(value, 1))
        one_src[d, own_tiles, 8 + s : 16 + s, :] = jnp.where(even_lane, roll(value, -1), value)
    for c in range(chans):
        for r, n in spans(0, half_rows):
            for k in range(own_tiles):
                one_src[c, k, 8 + r : 8 + r + n, :] = coarse_in[c, k, r : r + n, :]
        for r, n in spans(FIRST // 2, half_rows - FIRST // 2):
            ids = lane_ids(n)
            seam = restricted(seam_rest.at[c], 0, 2 * r, n, 1)
            turned = roll(seam, HALF)
            at = pl.ds(8 + r, n)
            one_src[c, 0, at, :] = jnp.where(ids < 4, seam, one_src[c, 0, at, :])
            one_src[c, own_tiles - 1, at, :] = jnp.where(ids >= LANES - 4, turned, one_src[c, own_tiles - 1, at, :])
            side = jnp.where(ids < 4, turned, one_src[c, own_tiles, at, :])
            one_src[c, own_tiles, at, :] = jnp.where(ids >= LANES - 4, seam, side)

    def smooth(src, once, fields, depth, into, minus=False):
        def one_sweep(spot, turned):
            f, r, n = spot
            mids, found = swept(once.at[f], src.at[f], scales(depth, r, n), 1 << depth, 8 + r, n, True, turned)
            for k in range(tiles):
                into[f, k, 8 + r : 8 + r + n, :] = found[k] - mids[k] if minus else found[k]

        spots = [(f, r, n) for f in range(fields) for r, n in spans(0, height >> depth)]
        staggered(spots, lambda spot: turn(once.at[spot[0]], 1 << depth, 8 + spot[1], spot[2]), one_sweep, 0)

    def expand(fix, fields, depth, out, low, high, spread):
        for f in range(fields):
            for r, n in spans(low, high):
                scale = scales(depth + 1, r, n)
                for k in range(tiles):
                    value = fix[0 if spread else f, k, 8 + r : 8 + r + n, :]
                    if spread:
                        value = spread(value, f)
                    value = value * (scale[k] * (1.0 / NEAR))
                    out[f, k, pl.ds(8 + 2 * r, n, stride=2), :] = value
                    out[f, k, pl.ds(9 + 2 * r, n, stride=2), :] = value

    def add_fix(once, two, fields, depth, into):
        for f in range(fields):
            for r, n in spans(0, height >> depth):
                for k in range(tiles):
                    at = pl.ds(8 + r, n)
                    into[f, k, at, :] = once[f, k, at, :] + two[f, k, at, :]

    assert chans <= 4 and LEVELS >= 3

    def spread_channel(value, f):
        ids = lane_ids(value.shape[0])
        odd = (ids & 1) == 1
        pair = jnp.where(odd, value, roll(value, -1)) if f & 1 else jnp.where(odd, roll(value, 1), value)
        high = (ids & 2) == 2
        return jnp.where(high, pair, roll(pair, -2)) if f & 2 else jnp.where(high, roll(pair, 2), pair)

    def level(depth):
        src, once, two = bufs[3 * (depth - 1) : 3 * depth]
        fields = chans if depth == 1 else 1
        if depth == LEVELS - 1:
            held = src
            for sweep in range(1, COARSE):
                into = (once, two)[sweep % 2]
                smooth(src, held, fields, depth, into)
                held = into
            return held
        smooth(src, src, fields, depth, once)
        smooth(src, once, fields, depth, two, True)
        below = bufs[3 * depth]
        shift = 1 << depth
        for r, n in spans(0, height >> (depth + 1)):
            ids = lane_ids(n) & 3
            for k in range(tiles):
                value = None
                for f in range(fields):
                    total = restricted(two.at[f], k, 8 + 2 * r, n, shift)
                    value = total if value is None else jnp.where(ids == f, total, value)
                below[0, k, 8 + r : 8 + r + n, :] = value
        fix = level(depth + 1)
        expand(fix, fields, depth, two, 0, height >> (depth + 1), spread_channel if depth == 1 else None)
        add_fix(once, two, fields, depth, once)
        smooth(src, once, fields, depth, two)
        smooth(src, two, fields, depth, once)
        return once

    fix = level(1)
    low, high = HALO - RIM, HALO + rows + RIM

    def fine_source(c):
        def tile(k, r, n):
            ids = lane_ids(n)
            seam = seam_source[c, 0, r : r + n, :]
            if k == own_tiles:
                return jnp.where(ids < HALF, roll(seam, HALF), seam)
            value = source_in[c, k, r : r + n, :]
            if k == 0:
                value = jnp.where(ids == 0, seam, value)
            if k == own_tiles - 1:
                value = jnp.where(ids == LANES - 1, roll(seam, HALF), value)
            return value

        return tile

    def finish(c, _):
        for r, n in spans(low // 2, high // 2):
            scale = scales(1, r, n)
            for k in range(tiles):
                value = fix[c, k, 8 + r : 8 + r + n, :] * (scale[k] * (1.0 / NEAR))
                fine[k, pl.ds(8 + 2 * r, n, stride=2), :] = value
                fine[k, pl.ds(9 + 2 * r, n, stride=2), :] = value
        for r, n in spans(low, high):
            ids = lane_ids(n)
            seam = seam_once[c, 0, r : r + n, :]
            turned = roll(seam, HALF)
            at = pl.ds(8 + r, n)
            for k in range(own_tiles):
                value = once_in[c, k, r : r + n, :]
                if k == 0:
                    value = jnp.where(ids < 2, seam, value)
                if k == own_tiles - 1:
                    value = jnp.where(ids >= LANES - 2, turned, value)
                fine[k, at, :] = fine[k, at, :] + value
            fine[own_tiles, at, :] = fine[own_tiles, at, :] + jnp.where(ids < HALF, turned, seam)
        add = fine_source(c)

        def first(piece, turned):
            r, n = piece
            _, found = swept(fine, add, scales(0, r, n), 1, 8 + r, n, True, turned)
            for k in range(tiles):
                fine_two[k, 8 + r : 8 + r + n, :] = found[k]

        def last(piece, turned):
            r, n = piece
            _, found = swept(fine_two, add, scales(0, r, n), 1, 8 + r, n, True, turned, own_tiles)
            for k in range(own_tiles):
                at = pl.ds(k * LANES, LANES)
                out_ref[c, r - HALO : r - HALO + n, at] = x_ref[c, r - HALO : r - HALO + n, at] + found[k]

        staggered(spans(low, high), lambda piece: turn(fine, 1, 8 + piece[0], piece[1]), first, 0)
        staggered(spans(HALO, HALO + rows), lambda piece: turn(fine_two, 1, 8 + piece[0], piece[1]), last, 0)
        return 0

    lax.fori_loop(0, chans, finish, 0)


def swaps(count, odd):
    pairs = [(i, i + 1) for i in range(odd, count - 1, 2)]
    return pairs + [(j, i) for i, j in pairs]


def shards(image_a, image_b, initial, coverage, seam_label):
    chans, rows, cols = image_a.shape
    tiles = cols // LANES
    height = rows + 2 * HALO
    vmem = pl.BlockSpec(memory_space=pltpu.VMEM)
    smem = pl.BlockSpec(memory_space=pltpu.SMEM)
    f32 = jnp.float32
    sds = functools.partial(jax.ShapeDtypeStruct, dtype=f32)
    params = pltpu.CompilerParams(vmem_limit_bytes=40 * 1024 * 1024)
    group, blk = lax.axis_size("group"), lax.axis_size("blk")
    central = sds((chans, tiles, height, LANES))
    column = sds((chans, height, LANES))
    coarse = sds((chans, tiles, height // 2, LANES))
    upright = sds((tiles, chans * STRIP + 8, LANES))
    beside = sds((sum(message_rows(chans, height)) + 8, LANES))

    last = rows // HALO - 1
    block = pl.BlockSpec((chans, HALO, cols), lambda i: (0, i * last, 0))
    whole = pl.BlockSpec(upright.shape, lambda i: (0, 0, 0))
    sent_even, sent_odd = pl.pallas_call(
        strips,
        grid=(2,),
        out_shape=(upright, upright),
        in_specs=[block, block, block, smem, smem],
        out_specs=(whole, whole),
        scratch_shapes=[pltpu.VMEM((tiles, HALO + 16, LANES), f32)] + [pltpu.VMEM((tiles, HALO, LANES), f32)] * 2
        + [pltpu.VMEM(upright.shape, f32)],
        compiler_params=params,
        name="strips",
    )(image_a, image_b, initial, coverage, seam_label)
    got_even = lax.ppermute(sent_even, "group", swaps(group, 0))
    got_odd = lax.ppermute(sent_odd, "group", swaps(group, 1))

    source, once, seam, coarser = pl.pallas_call(
        inside,
        out_shape=(central, central, column, coarse),
        in_specs=[vmem, vmem, vmem, smem, smem],
        out_specs=(vmem,) * 4,
        scratch_shapes=[pltpu.VMEM((tiles, rows + 16, LANES), f32)] * 2 + [pltpu.VMEM((tiles, height, LANES), f32)],
        compiler_params=params,
        cost_estimate=pl.CostEstimate(flops=200_000_000, bytes_accessed=4_000_000, transcendentals=0),
        name="inside",
    )(image_a, image_b, initial, coverage, seam_label)

    source, once, seam, coarser, sent_even, sent_odd = pl.pallas_call(
        join_rows,
        out_shape=(central, central, column, coarse, beside, beside),
        in_specs=[vmem] * 8 + [smem] * 2,
        out_specs=(vmem,) * 6,
        input_output_aliases={0: 0, 1: 1, 2: 2, 3: 3},
        scratch_shapes=[pltpu.VMEM(central.shape, f32), pltpu.VMEM((8, LANES), f32)]
        + [pltpu.VMEM(upright.shape, f32)] * 2
        + [pltpu.VMEM((tiles, 4 * chans, LANES), f32)]
        + [pltpu.VMEM(beside.shape, f32)] * 2,
        compiler_params=params,
        name="join_rows",
    )(source, once, seam, coarser, sent_even, sent_odd, got_even, got_odd, coverage, seam_label)
    got_even = lax.ppermute(sent_even, "blk", swaps(blk, 0))
    got_odd = lax.ppermute(sent_odd, "blk", swaps(blk, 1))

    scratch = [pltpu.VMEM(beside.shape, f32)] * 2 + [pltpu.VMEM((chans, 1, height, LANES), f32)] * 3
    scratch += [pltpu.VMEM((tiles + 1, height + 16, LANES), f32)] * 2
    for depth in range(1, LEVELS):
        fields = chans if depth == 1 else 1
        scratch += [pltpu.VMEM((fields, tiles + 1, (height >> depth) + 16, LANES), f32)] * 3
    return pl.pallas_call(
        cycle,
        out_shape=sds((chans, rows, cols)),
        in_specs=[vmem] * 8,
        out_specs=vmem,
        scratch_shapes=scratch,
        compiler_params=params,
        name="cycle",
    )(source, once, seam, coarser, sent_even, got_even, got_odd, initial)


def solution(mesh):
    placed = (
        P(None, "group", "blk"),
        P(None, "group", "blk"),
        P(None, "group", "blk"),
        P("group", "blk"),
        P("group", "blk"),
    )
    return jax.shard_map(
        shards, mesh=mesh, in_specs=placed, out_specs=P(None, "group", "blk"), check_vma=False
    )
```

time: 353 us -> 35.1 us (0.10); the launches traced: 347 us -> 34.7 us
  starting transfers between devices: 125 us -> 8.69 us
  local copies, waits for them, and re-layouts: 108 us -> 3.4 us
  other arithmetic: 59.2 us -> 0 us
  waiting for transfers between devices: 53.1 us -> 5.1 us
  Pallas kernels: 0 us -> 16.2 us
    ppermute x40 -> x4, starting transfers between devices: 125 us -> 8.69 us  [the longest x1 4.6 us: shards(): got_odd = lax.ppermute(sent_odd, 'group', swaps(group, 1))]
    reshape x3 -> x0, local copies, waits for them, and re-layouts: 72.2 us -> none  [shrink(): return field.reshape(chans, rows // 2, 2, cols // 2, 2).mean(axis=(2, 4))]
    ppermute x40 -> x4, waiting for transfers between devices: 53.1 us -> 5.1 us  [the longest x1 3.75 us: shards(): got_odd = lax.ppermute(sent_odd, 'blk', swaps(blk, 1))]
    reduce_sum x3 -> x0, other arithmetic: 28.6 us -> none  [shrink(): return field.reshape(chans, rows // 2, 2, cols // 2, 2).mean(axis=(2, 4))]
    pallas_call x0 -> x4, Pallas kernels: none -> 16.2 us  [the longest x1 11.2 us: shards(): pl.pallas_call(cycle, out_shape=sds((chans, rows, cols)), in_specs=[vmem]...]
    add x12 -> x0, other arithmetic: 13.5 us -> none  [the longest x6 5.49 us: wide_sweep(): inner + RELAX * active_in * (source_in - factor * (4.0 * inner - beside_s...]
    mul x7 -> x0, local copies, waits for them, and re-layouts: 11.9 us -> none  [the longest x6 9.56 us: deep_cycle(): approx = approx + active * expand(coarse_fix)]
    slice x19 -> x0, local copies, waits for them, and re-layouts: 7.42 us -> none  [the longest x18 5.79 us: padded_2(): lax.slice_in_dim(cells, cells.shape[dim] - width, cells.shape[dim], axis=...]
  transfers between devices with their start and end apart: 40 -> 4, of which waited for: 26 -> 2; matrix products, arithmetic and copies ran while one was open for 1% -> 0% of each run, Pallas kernels for 0% -> 8%
where the time goes in v2:
time: 35.1 us; the launch traced here: 34.7 us
  Pallas kernels  16.2 us (46%)
  starting transfers between devices  8.69 us (25%)
  waiting for transfers between devices  5.1 us (15%)
  local copies, waits for them, and re-layouts  3.4 us (10%)
  between operations  1.36 us (4%)
    pallas_call x1, Pallas kernels, shards(): pl.pallas_call(cycle, out_shape=sds((chans, rows, cols)), in_specs=[vmem]...  11.2 us
    ppermute x1, starting transfers between devices, shards(): got_odd = lax.ppermute(sent_odd, 'group', swaps(group, 1))  4.6 us
    ppermute x1, waiting for transfers between devices, shards(): got_odd = lax.ppermute(sent_odd, 'blk', swaps(blk, 1))  3.75 us
    unnamed x8, local copies, waits for them, and re-layouts  3.4 us
    pallas_call x1, Pallas kernels, shards(): pl.pallas_call(inside, out_shape=(central, central, column, coarse), in_s...  2.89 us
    ppermute x1, starting transfers between devices, shards(): got_odd = lax.ppermute(sent_odd, 'blk', swaps(blk, 1))  1.94 us
    ppermute x1, starting transfers between devices, shards(): got_even = lax.ppermute(sent_even, 'blk', swaps(blk, 0))  1.64 us
    ppermute x1, waiting for transfers between devices, shards(): got_odd = lax.ppermute(sent_odd, 'group', swaps(group, 1))  1.35 us
  transfers between devices with their start and end apart: 4, of which 2 were waited for; matrix products, arithmetic and copies ran while one was open for 0% of the time, Pallas kernels for 8%

profile of v2, /device:TPU:12, one launch (start us, length us, event | category | flops | bytes accessed | tf_op | source)
XLA Modules:
  0.0 34.7 jit_solution(13599707395907078504)
XLA Ops:
  1.3 0.0 copy-start
  1.3 1.1 %copy-done = f32[3,256,256]{2,1,0:T(8,128)S(1)} copy-done((f32[3,256,256]{2,1,0:T(8,128)S(1)}, f32[3,256,256]{2,1,0:T(8,128)}, u32[]{:S(2)}) %copy-start) | copy-done | bytes 786456
  2.4 0.0 copy-start.2
  2.4 1.1 %copy-done.2 = f32[3,256,256]{2,1,0:T(8,128)S(1)} copy-done((f32[3,256,256]{2,1,0:T(8,128)S(1)}, f32[3,256,256]{2,1,0:T(8,128)}, u32[]{:S(2)}) %copy-start.2) | copy-done | bytes 786456
  3.6 0.0 copy-start.3
  3.6 1.1 %copy-done.3 = f32[3,256,256]{2,1,0:T(8,128)S(1)} copy-done((f32[3,256,256]{2,1,0:T(8,128)S(1)}, f32[3,256,256]{2,1,0:T(8,128)}, u32[]{:S(2)}) %copy-start.3) | copy-done | bytes 786456
  4.7 0.8 %strips.1 = (f32[2,176,128]{2,1,0:T(8,128)S(1)}, f32[2,176,128]{2,1,0:T(8,128)S(1)}) custom-call(f32[3,256,256]{2,1,0:T(8,128)S(1)} %copy-done.2, f32[3,256,256]{2,1,0:T(8,128)S(1)} %copy-done.3, f32[3,256,256]{2,1,0:T(8,128)S(1)} %copy-done, s32[1,1]{1,0:T(1,128)S(6)} %copy.14.cover_ref, s32[1,1]{1,0:T(1,128)S(6)} %copy.15.label_ref), custom_call_target="tpu_custom_call" | custom-call | tf_op jit(solution)/shard_map/strips/pallas_call | solution.py:668
  5.5 0.5 %collective-permute-start = (f32[2,176,128]{2,1,0:T(8,128)S(1)}, f32[2,176,128]{2,1,0:T(8,128)S(1)}, u32[]{:S(2)}, u32[]{:S(2)}) collective-permute-start(f32[2,176,128]{2,1,0:T(8,128)S(1)} %get-tuple-element.21.sent_even), channel_id=1, source_target_pairs={{0,8},{16,24},{8,0},{24,16},{1,9},{17,25},{9,1},{25,17},{2,10},{18... | collective-permute-start | bytes 540680 | tf_op jit(solution)/shard_map/ppermute | solution.py:679
  6.0 4.6 %collective-permute-start.1 = (f32[2,176,128]{2,1,0:T(8,128)S(1)}, f32[2,176,128]{2,1,0:T(8,128)S(1)}, u32[]{:S(2)}, u32[]{:S(2)}) collective-permute-start(f32[2,176,128]{2,1,0:T(8,128)S(1)} %get-tuple-element.22.sent_odd), channel_id=1, source_target_pairs={{8,16},{16,8},{9,17},{17,9},{10,18},{18,10},{11,19},{19,11},{12,20... | collective-permute-start | bytes 540680 | tf_op jit(solution)/shard_map/ppermute | solution.py:680
  10.6 2.9 %inside.1 = (f32[3,2,384,128]{3,2,1,0:T(8,128)S(1)}, f32[3,2,384,128]{3,2,1,0:T(8,128)S(1)}, f32[3,384,128]{2,1,0:T(8,128)S(1)}, f32[3,2,192,128]{3,2,1,0:T(8,128)S(1)}) custom-call(f32[3,256,256]{2,1,0:T(8,128)S(1)} %copy-done.2, f32[3,256,256]{2,1,0:T(8,128)S(1)} %copy-done.3, f32[3,256,256]{2,1,0:T(8,128)S(1)} %copy-done, s32[1,1]{1,0:T(1,128)S(6)} %copy.14.cover_ref, ...), custom_call_target="tpu_custom_call" | custom-call | flops 200000000 | bytes 4000000 | tf_op jit(solution)/shard_map/inside/pallas_call | solution.py:682
  13.5 0.0 collective-permute-done.got_even
  13.5 1.3 %collective-permute-done.1.got_odd = f32[2,176,128]{2,1,0:T(8,128)S(1)} collective-permute-done((f32[2,176,128]{2,1,0:T(8,128)S(1)}, f32[2,176,128]{2,1,0:T(8,128)S(1)}, u32[]{:S(2)}, u32[]{:S(2)}) %collective-permute-start.1) | collective-permute-done | bytes 180256 | tf_op jit(solution)/shard_map/ppermute | solution.py:680
  14.9 0.0 copy-start.1
  14.9 1.3 %join_rows.1 = (f32[3,2,384,128]{3,2,1,0:T(8,128)S(1)}, f32[3,2,384,128]{3,2,1,0:T(8,128)S(1)}, f32[3,384,128]{2,1,0:T(8,128)S(1)}, f32[3,2,192,128]{3,2,1,0:T(8...) custom-call(f32[3,2,384,128]{3,2,1,0:T(8,128)S(1)} %get-tuple-elemen, ...), custom_call_target="tpu_custom_call", output_to_operand_aliasing={{0}: (0, {}), {1}: (1, {}), {2}: (2, {}), {3}: (3, {})} | custom-call | tf_op jit(solution)/shard_map/join_rows/pallas_call | solution.py:693
  16.2 1.9 %collective-permute-start.3 = (f32[224,128]{1,0:T(8,128)S(1)}, f32[224,128]{1,0:T(8,128)S(1)}, u32[]{:S(2)}, u32[]{:S(2)}) collective-permute-start(f32[224,128]{1,0:T(8,128)S(1)} %get-tuple-element.28), channel_id=1, source_target_pairs={{1,2},{3,4},{5,6},{2,1},{4,3},{6,5},{9,10},{11,12},{13,14},{10,9},... | collective-permute-start | bytes 344072 | tf_op jit(solution)/shard_map/ppermute | solution.py:707
  18.1 1.6 %collective-permute-start.2 = (f32[224,128]{1,0:T(8,128)S(1)}, f32[224,128]{1,0:T(8,128)S(1)}, u32[]{:S(2)}, u32[]{:S(2)}) collective-permute-start(f32[224,128]{1,0:T(8,128)S(1)} %get-tuple-element.27.sent_even), channel_id=1, source_target_pairs={{0,1},{2,3},{4,5},{6,7},{1,0},{3,2},{5,4},{7,6},{8,9},{10,11},{12,... | collective-permute-start | bytes 344072 | tf_op jit(solution)/shard_map/ppermute | solution.py:706
  19.7 3.7 %collective-permute-done.3.got_odd = f32[224,128]{1,0:T(8,128)S(1)} collective-permute-done((f32[224,128]{1,0:T(8,128)S(1)}, f32[224,128]{1,0:T(8,128)S(1)}, u32[]{:S(2)}, u32[]{:S(2)}) %collective-permute-start.3) | collective-permute-done | bytes 114720 | tf_op jit(solution)/shard_map/ppermute | solution.py:707
  23.5 0.0 collective-permute-done.2.got_even
  23.5 0.0 copy-done.1
  23.5 11.2 %cycle.1 = f32[3,256,256]{2,1,0:T(8,128)} custom-call(f32[3,2,384,128]{3,2,1,0:T(8,128)S(1)} %get-tuple-element.23.source_in, f32[3,2,384,128]{3,2,1,0:T(8,128)S(1)} %get-tuple-element.24.once_in, f32[3,384,128]{2,1,0:T(8,128)S(1)} %get-tuple-element.25.seam_in, f32[3,2,192,128]{3,2,1,0:T(8,128)S(1)} %get-tuple-element.26.coarse_in, ...), custom_call_target="tpu_custom_call" | custom-call | tf_op jit(solution)/shard_map/cycle/pallas_call | solution.py:714
Async XLA Ops:
  1.3 1.1 %copy-start = (f32[3,256,256]{2,1,0:T(8,128)S(1)}, f32[3,256,256]{2,1,0:T(8,128)}, u32[]{:S(2)}) copy-start(f32[3,256,256]{2,1,0:T(8,128)} %x_ref.5) | copy-start | bytes 2359300
  2.4 1.1 %copy-start.2 = (f32[3,256,256]{2,1,0:T(8,128)S(1)}, f32[3,256,256]{2,1,0:T(8,128)}, u32[]{:S(2)}) copy-start(f32[3,256,256]{2,1,0:T(8,128)} %a_ref.3) | copy-start | bytes 2359300
  3.6 1.1 %copy-start.3 = (f32[3,256,256]{2,1,0:T(8,128)S(1)}, f32[3,256,256]{2,1,0:T(8,128)}, u32[]{:S(2)}) copy-start(f32[3,256,256]{2,1,0:T(8,128)} %b_ref.3) | copy-start | bytes 2359300
  5.5 8.0 %collective-permute-start = (f32[2,176,128]{2,1,0:T(8,128)S(1)}, f32[2,176,128]{2,1,0:T(8,128)S(1)}, u32[]{:S(2)}, u32[]{:S(2)}) collective-permute-start(f32[2,176,128]{2,1,0:T(8,128)S(1)} %get-tuple-element.21.sent_even), channel_id=1, source_target_pairs={{0,8},{16,24},{8,0},{24,16},{1,9},{17,25},{9,1},{25,17},{2,10},{18... | collective-permute-start | bytes 540680 | tf_op jit(solution)/shard_map/ppermute | solution.py:679
  6.0 8.9 %collective-permute-start.1 = (f32[2,176,128]{2,1,0:T(8,128)S(1)}, f32[2,176,128]{2,1,0:T(8,128)S(1)}, u32[]{:S(2)}, u32[]{:S(2)}) collective-permute-start(f32[2,176,128]{2,1,0:T(8,128)S(1)} %get-tuple-element.22.sent_odd), channel_id=1, source_target_pairs={{8,16},{16,8},{9,17},{17,9},{10,18},{18,10},{11,19},{19,11},{12,20... | collective-permute-start | bytes 540680 | tf_op jit(solution)/shard_map/ppermute | solution.py:680
  14.9 8.6 %copy-start.1 = (f32[3,256,256]{2,1,0:T(8,128)S(1)}, f32[3,256,256]{2,1,0:T(8,128)}, u32[]{:S(2)}) copy-start(f32[3,256,256]{2,1,0:T(8,128)} %x_ref.5) | copy-start | bytes 2359300
  16.2 7.3 %collective-permute-start.3 = (f32[224,128]{1,0:T(8,128)S(1)}, f32[224,128]{1,0:T(8,128)S(1)}, u32[]{:S(2)}, u32[]{:S(2)}) collective-permute-start(f32[224,128]{1,0:T(8,128)S(1)} %get-tuple-element.28), channel_id=1, source_target_pairs={{1,2},{3,4},{5,6},{2,1},{4,3},{6,5},{9,10},{11,12},{13,14},{10,9},... | collective-permute-start | bytes 344072 | tf_op jit(solution)/shard_map/ppermute | solution.py:707
  18.1 5.4 %collective-permute-start.2 = (f32[224,128]{1,0:T(8,128)S(1)}, f32[224,128]{1,0:T(8,128)S(1)}, u32[]{:S(2)}, u32[]{:S(2)}) collective-permute-start(f32[224,128]{1,0:T(8,128)S(1)} %get-tuple-element.27.sent_even), channel_id=1, source_target_pairs={{0,1},{2,3},{4,5},{6,7},{1,0},{3,2},{5,4},{7,6},{8,9},{10,11},{12,... | collective-permute-start | bytes 344072 | tf_op jit(solution)/shard_map/ppermute | solution.py:706

commit v3 on v2

--- a/solution.py
+++ b/solution.py
@@ -107,57 +107,83 @@
     return total + jnp.where(even, roll(total, -shift), roll(total, shift))
 
 
-def strips(a_ref, b_ref, x_ref, cover_ref, label_ref, even_ref, odd_ref, picked, other_a, other_b, built):
-    chans, rows, cols = a_ref.shape
+def strips(
+    a_hbm, b_hbm, x_hbm, cover_ref, label_ref, even_ref, odd_ref,
+    a_both, b_both, x_both, picked, other_a, other_b, built, sems,
+):
+    chans, block, cols = a_hbm.shape
+    rows = HALO
     tiles = cols // LANES
     active = cover_ref[0, 0].astype(jnp.float32)
     marked = label_ref[0, 0].astype(jnp.float32)
     second = label_ref[0, 0] == 1
     eight = lane_ids(8)
 
-    top = pl.program_id(0) == 0
-    low = jnp.where(top, 0, rows - STRIP)
-    line = jnp.where(top, 0, rows - 1)
-    spot = jnp.where(top, STRIP - 2, 0)
-    for k in range(tiles):
-        for edge in (7, 8 + rows):
-            picked[k, edge : edge + 1, :] = jnp.zeros((1, LANES), jnp.float32)
-    packed = jnp.zeros((8, LANES), jnp.float32)
-    for c in range(chans):
+
+    def fetches(step):
+        low = pl.multiple_of(step * (block - HALO), 8)
+        pairs = ((a_hbm, a_both), (b_hbm, b_both), (x_hbm, x_both))
+        return [
+            pltpu.make_async_copy(src.at[:, pl.ds(low, HALO), :], dst.at[step], sems.at[i, step])
+            for i, (src, dst) in enumerate(pairs)
+        ]
+
+    for step in range(2):
+        for fetch in fetches(step):
+            fetch.start()
+
+    def one_side(step, _):
+        for fetch in fetches(step):
+            fetch.wait()
+        message(step, a_both.at[step], b_both.at[step], x_both.at[step])
+        return 0
+
+    def message(step, a_ref, b_ref, x_ref):
+        top = step == 0
+        low = jnp.where(top, 0, rows - STRIP)
+        line = jnp.where(top, 0, rows - 1)
+        spot = jnp.where(top, STRIP - 2, 0)
         for k in range(tiles):
-            at = pl.ds(k * LANES, LANES)
-            for r, n in spans(0, rows):
-                x = x_ref[c, r : r + n, at]
-                from_a, from_b = a_ref[c, r : r + n, at] - x, b_ref[c, r : r + n, at] - x
-                other_a[k, r : r + n, :], other_b[k, r : r + n, :] = from_a, from_b
-                picked[k, 8 + r : 8 + r + n, :] = jnp.where(second, from_b, from_a)
-        start = pl.multiple_of(low, 8)
-        parts = [[picked[k, pl.ds(start + 8 + s, STRIP), :] for k in range(tiles)] for s in (0, -1, 1)]
-        for k, found in enumerate(own_source(*parts, active)):
-            built[k, c * STRIP : (c + 1) * STRIP, :] = found
-        for k in range(tiles):
-            built[k, pl.ds(c * STRIP + spot, 1), :] = other_a[k, pl.ds(line, 1), :]
-            built[k, pl.ds(c * STRIP + spot + 1, 1), :] = other_b[k, pl.ds(line, 1), :]
-        for t in range(STRIP // 8):
-            lane = 4 * (chans * t + c)
-            at = pl.ds(start + 8 * t, 8)
-            packed = jnp.where(eight == lane, roll(other_a[0, at, :], lane), packed)
-            packed = jnp.where(eight == lane + 1, roll(other_b[0, at, :], lane + 1), packed)
-            packed = jnp.where(eight == lane + 2, roll(other_a[tiles - 1, at, :], lane + 3), packed)
-            packed = jnp.where(eight == lane + 3, roll(other_b[tiles - 1, at, :], lane + 4), packed)
-    built[0, chans * STRIP :, :] = packed
-    for k in range(1, tiles):
-        built[k, chans * STRIP :, :] = jnp.where(eight < HALF, active, marked)
-
-    by_odd = top == even_at("group")
-
-    @pl.when(by_odd)
-    def _():
-        odd_ref[...] = built[...]
-
-    @pl.when(jnp.logical_not(by_odd))
-    def _():
-        even_ref[...] = built[...]
+            for edge in (7, 8 + rows):
+                picked[k, edge : edge + 1, :] = jnp.zeros((1, LANES), jnp.float32)
+        packed = jnp.zeros((8, LANES), jnp.float32)
+        for c in range(chans):
+            for k in range(tiles):
+                at = pl.ds(k * LANES, LANES)
+                for r, n in spans(0, rows):
+                    x = x_ref[c, r : r + n, at]
+                    from_a, from_b = a_ref[c, r : r + n, at] - x, b_ref[c, r : r + n, at] - x
+                    other_a[k, r : r + n, :], other_b[k, r : r + n, :] = from_a, from_b
+                    picked[k, 8 + r : 8 + r + n, :] = jnp.where(second, from_b, from_a)
+            start = pl.multiple_of(low, 8)
+            parts = [[picked[k, pl.ds(start + 8 + s, STRIP), :] for k in range(tiles)] for s in (0, -1, 1)]
+            for k, found in enumerate(own_source(*parts, active)):
+                built[k, c * STRIP : (c + 1) * STRIP, :] = found
+            for k in range(tiles):
+                built[k, pl.ds(c * STRIP + spot, 1), :] = other_a[k, pl.ds(line, 1), :]
+                built[k, pl.ds(c * STRIP + spot + 1, 1), :] = other_b[k, pl.ds(line, 1), :]
+            for t in range(STRIP // 8):
+                lane = 4 * (chans * t + c)
+                at = pl.ds(start + 8 * t, 8)
+                packed = jnp.where(eight == lane, roll(other_a[0, at, :], lane), packed)
+                packed = jnp.where(eight == lane + 1, roll(other_b[0, at, :], lane + 1), packed)
+                packed = jnp.where(eight == lane + 2, roll(other_a[tiles - 1, at, :], lane + 3), packed)
+                packed = jnp.where(eight == lane + 3, roll(other_b[tiles - 1, at, :], lane + 4), packed)
+        built[0, chans * STRIP :, :] = packed
+        for k in range(1, tiles):
+            built[k, chans * STRIP :, :] = jnp.where(eight < HALF, active, marked)
+
+        by_odd = top == even_at("group")
+
+        @pl.when(by_odd)
+        def _():
+            odd_ref[...] = built[...]
+
+        @pl.when(jnp.logical_not(by_odd))
+        def _():
+            even_ref[...] = built[...]
+
+    lax.fori_loop(0, 2, one_side, 0)
 
 
 def inside(a_ref, b_ref, x_ref, cover_ref, label_ref, source_ref, once_ref, seam_ref, coarse_ref, da, db, rest):
@@ -383,8 +409,8 @@
 
 
 def cycle(
-    source_in, once_in, seam_in, coarse_in, sent_even, got_even, got_odd, x_ref, out_ref,
-    right_ref, left_ref, seam_source, seam_once, seam_rest, fine, fine_two, *bufs,
+    source_in, once_in, seam_in, coarse_in, sent_even, got_even, got_odd, x_ref, out_hbm,
+    out_ref, sems, right_ref, left_ref, seam_source, seam_once, seam_rest, fine, fine_two, *bufs,
 ):
     chans, own_tiles, height, _ = source_in.shape
     rows = height - 2 * HALO
@@ -636,9 +662,15 @@
 
         staggered(spans(low, high), lambda piece: turn(fine, 1, 8 + piece[0], piece[1]), first, 0)
         staggered(spans(HALO, HALO + rows), lambda piece: turn(fine_two, 1, 8 + piece[0], piece[1]), last, 0)
+        leave(c).start()
         return 0
 
+    def leave(c):
+        return pltpu.make_async_copy(out_ref.at[c], out_hbm.at[c], sems.at[c])
+
     lax.fori_loop(0, chans, finish, 0)
+    for c in range(chans):
+        leave(c).wait()
 
 
 def swaps(count, odd):
@@ -652,6 +684,7 @@
     height = rows + 2 * HALO
     vmem = pl.BlockSpec(memory_space=pltpu.VMEM)
     smem = pl.BlockSpec(memory_space=pltpu.SMEM)
+    hbm = pl.BlockSpec(memory_space=pltpu.HBM)
     f32 = jnp.float32
     sds = functools.partial(jax.ShapeDtypeStruct, dtype=f32)
     params = pltpu.CompilerParams(vmem_limit_bytes=40 * 1024 * 1024)
@@ -662,18 +695,16 @@
     upright = sds((tiles, chans * STRIP + 8, LANES))
     beside = sds((sum(message_rows(chans, height)) + 8, LANES))
 
-    last = rows // HALO - 1
-    block = pl.BlockSpec((chans, HALO, cols), lambda i: (0, i * last, 0))
-    whole = pl.BlockSpec(upright.shape, lambda i: (0, 0, 0))
     sent_even, sent_odd = pl.pallas_call(
         strips,
-        grid=(2,),
         out_shape=(upright, upright),
-        in_specs=[block, block, block, smem, smem],
-        out_specs=(whole, whole),
-        scratch_shapes=[pltpu.VMEM((tiles, HALO + 16, LANES), f32)] + [pltpu.VMEM((tiles, HALO, LANES), f32)] * 2
-        + [pltpu.VMEM(upright.shape, f32)],
-        compiler_params=params,
+        in_specs=[hbm, hbm, hbm, smem, smem],
+        out_specs=(vmem, vmem),
+        scratch_shapes=[pltpu.VMEM((2, chans, HALO, cols), f32)] * 3
+        + [pltpu.VMEM((tiles, HALO + 16, LANES), f32)]
+        + [pltpu.VMEM((tiles, HALO, LANES), f32)] * 2
+        + [pltpu.VMEM(upright.shape, f32), pltpu.SemaphoreType.DMA((3, 2))],
+        compiler_params=pltpu.CompilerParams(vmem_limit_bytes=56_000_000),
         name="strips",
     )(image_a, image_b, initial, coverage, seam_label)
     got_even = lax.ppermute(sent_even, "group", swaps(group, 0))
@@ -706,7 +737,8 @@
     got_even = lax.ppermute(sent_even, "blk", swaps(blk, 0))
     got_odd = lax.ppermute(sent_odd, "blk", swaps(blk, 1))
 
-    scratch = [pltpu.VMEM(beside.shape, f32)] * 2 + [pltpu.VMEM((chans, 1, height, LANES), f32)] * 3
+    scratch = [pltpu.VMEM(image_a.shape, f32), pltpu.SemaphoreType.DMA((chans,))]
+    scratch += [pltpu.VMEM(beside.shape, f32)] * 2 + [pltpu.VMEM((chans, 1, height, LANES), f32)] * 3
     scratch += [pltpu.VMEM((tiles + 1, height + 16, LANES), f32)] * 2
     for depth in range(1, LEVELS):
         fields = chans if depth == 1 else 1
@@ -715,7 +747,7 @@
         cycle,
         out_shape=sds((chans, rows, cols)),
         in_specs=[vmem] * 8,
-        out_specs=vmem,
+        out_specs=hbm,
         scratch_shapes=scratch,
         compiler_params=params,
         name="cycle",

time: 35.1 us -> 32.7 us (0.932)
  local copies, waits for them, and re-layouts: 3.4 us -> 0.01 us
  Pallas kernels: 16.2 us -> 17.2 us
    unnamed x8 -> x6, local copies, waits for them, and re-layouts: 3.4 us -> 0.01 us
    pallas_call x1, Pallas kernels: 0.8 us -> 1.99 us  [shards(): pl.pallas_call(strips, out_shape=(upright, upright), in_specs=[hbm, hbm,...]
  transfers between devices with their start and end apart: 4 -> 4, of which waited for: 2 -> 2; matrix products, arithmetic and copies ran while one was open for 0% -> 0% of each run, Pallas kernels for 8% -> 9%
where the time goes in v3:
time: 32.7 us; the launch traced here: 32.4 us
  Pallas kernels  17.2 us (53%)
  starting transfers between devices  8.69 us (27%)
  waiting for transfers between devices  5.07 us (16%)
  between operations  1.39 us (4%)
    pallas_call x1, Pallas kernels, shards(): pl.pallas_call(cycle, out_shape=sds((chans, rows, cols)), in_specs=[vmem]...  11 us
    ppermute x1, starting transfers between devices, shards(): got_odd = lax.ppermute(sent_odd, 'group', swaps(group, 1))  4.6 us
    ppermute x1, waiting for transfers between devices, shards(): got_odd = lax.ppermute(sent_odd, 'blk', swaps(blk, 1))  3.75 us
    pallas_call x1, Pallas kernels, shards(): pl.pallas_call(inside, out_shape=(central, central, column, coarse), in_s...  2.89 us
    pallas_call x1, Pallas kernels, shards(): pl.pallas_call(strips, out_shape=(upright, upright), in_specs=[hbm, hbm,...  1.99 us
    ppermute x1, starting transfers between devices, shards(): got_odd = lax.ppermute(sent_odd, 'blk', swaps(blk, 1))  1.94 us
    ppermute x1, starting transfers between devices, shards(): got_even = lax.ppermute(sent_even, 'blk', swaps(blk, 0))  1.64 us
    ppermute x1, waiting for transfers between devices, shards(): got_odd = lax.ppermute(sent_odd, 'group', swaps(group, 1))  1.32 us
  transfers between devices with their start and end apart: 4, of which 2 were waited for; matrix products, arithmetic and copies ran while one was open for 0% of the time, Pallas kernels for 9%

profile of v3, /device:TPU:12, one launch (start us, length us, event | category | flops | bytes accessed | tf_op | source)
XLA Modules:
  0.0 32.4 jit_solution(15171382640925277199)
XLA Ops:
  1.3 0.0 copy-start
  1.3 0.0 copy-start.1
  1.3 0.0 copy-start.2
  1.3 2.0 %strips.1 = (f32[2,176,128]{2,1,0:T(8,128)S(1)}, f32[2,176,128]{2,1,0:T(8,128)S(1)}) custom-call(f32[3,256,256]{2,1,0:T(8,128)} %a_hbm.1, f32[3,256,256]{2,1,0:T(8,128)} %b_hbm.1, f32[3,256,256]{2,1,0:T(8,128)} %x_ref.3, s32[1,1]{1,0:T(1,128)S(6)} %copy.14.cover_ref, s32[1,1]{1,0:T(1,128)S(6)} %copy.15.label_ref), custom_call_target="tpu_custom_call" | custom-call | tf_op jit(solution)/shard_map/strips/pallas_call | solution.py:698
  3.3 0.5 %collective-permute-start = (f32[2,176,128]{2,1,0:T(8,128)S(1)}, f32[2,176,128]{2,1,0:T(8,128)S(1)}, u32[]{:S(2)}, u32[]{:S(2)}) collective-permute-start(f32[2,176,128]{2,1,0:T(8,128)S(1)} %get-tuple-element.21.sent_even), channel_id=1, source_target_pairs={{0,8},{16,24},{8,0},{24,16},{1,9},{17,25},{9,1},{25,17},{2,10},{18... | collective-permute-start | bytes 540680 | tf_op jit(solution)/shard_map/ppermute | solution.py:710
  3.8 4.6 %collective-permute-start.1 = (f32[2,176,128]{2,1,0:T(8,128)S(1)}, f32[2,176,128]{2,1,0:T(8,128)S(1)}, u32[]{:S(2)}, u32[]{:S(2)}) collective-permute-start(f32[2,176,128]{2,1,0:T(8,128)S(1)} %get-tuple-element.22.sent_odd), channel_id=1, source_target_pairs={{8,16},{16,8},{9,17},{17,9},{10,18},{18,10},{11,19},{19,11},{12,20... | collective-permute-start | bytes 540680 | tf_op jit(solution)/shard_map/ppermute | solution.py:711
  8.4 0.0 copy-done
  8.5 0.0 copy-done.1
  8.5 0.0 copy-done.2
  8.5 2.9 %inside.1 = (f32[3,2,384,128]{3,2,1,0:T(8,128)S(1)}, f32[3,2,384,128]{3,2,1,0:T(8,128)S(1)}, f32[3,384,128]{2,1,0:T(8,128)S(1)}, f32[3,2,192,128]{3,2,1,0:T(8,128)S(1)}) custom-call(f32[3,256,256]{2,1,0:T(8,128)S(1)} %copy-done.1, f32[3,256,256]{2,1,0:T(8,128)S(1)} %copy-done.2, f32[3,256,256]{2,1,0:T(8,128)S(1)} %copy-done, s32[1,1]{1,0:T(1,128)S(6)} %copy.14.cover_ref, ...), custom_call_target="tpu_custom_call" | custom-call | flops 200000000 | bytes 4000000 | tf_op jit(solution)/shard_map/inside/pallas_call | solution.py:713
  11.4 0.0 collective-permute-done.got_even
  11.4 1.3 %collective-permute-done.1.got_odd = f32[2,176,128]{2,1,0:T(8,128)S(1)} collective-permute-done((f32[2,176,128]{2,1,0:T(8,128)S(1)}, f32[2,176,128]{2,1,0:T(8,128)S(1)}, u32[]{:S(2)}, u32[]{:S(2)}) %collective-permute-start.1) | collective-permute-done | bytes 180256 | tf_op jit(solution)/shard_map/ppermute | solution.py:711
  12.7 1.3 %join_rows.1 = (f32[3,2,384,128]{3,2,1,0:T(8,128)S(1)}, f32[3,2,384,128]{3,2,1,0:T(8,128)S(1)}, f32[3,384,128]{2,1,0:T(8,128)S(1)}, f32[3,2,192,128]{3,2,1,0:T(8...) custom-call(f32[3,2,384,128]{3,2,1,0:T(8,128)S(1)} %get-tuple-elemen, ...), custom_call_target="tpu_custom_call", output_to_operand_aliasing={{0}: (0, {}), {1}: (1, {}), {2}: (2, {}), {3}: (3, {})} | custom-call | tf_op jit(solution)/shard_map/join_rows/pallas_call | solution.py:724
  14.0 1.9 %collective-permute-start.3 = (f32[224,128]{1,0:T(8,128)S(1)}, f32[224,128]{1,0:T(8,128)S(1)}, u32[]{:S(2)}, u32[]{:S(2)}) collective-permute-start(f32[224,128]{1,0:T(8,128)S(1)} %get-tuple-element.28), channel_id=1, source_target_pairs={{1,2},{3,4},{5,6},{2,1},{4,3},{6,5},{9,10},{11,12},{13,14},{10,9},... | collective-permute-start | bytes 344072 | tf_op jit(solution)/shard_map/ppermute | solution.py:738
  15.9 1.6 %collective-permute-start.2 = (f32[224,128]{1,0:T(8,128)S(1)}, f32[224,128]{1,0:T(8,128)S(1)}, u32[]{:S(2)}, u32[]{:S(2)}) collective-permute-start(f32[224,128]{1,0:T(8,128)S(1)} %get-tuple-element.27.sent_even), channel_id=1, source_target_pairs={{0,1},{2,3},{4,5},{6,7},{1,0},{3,2},{5,4},{7,6},{8,9},{10,11},{12,... | collective-permute-start | bytes 344072 | tf_op jit(solution)/shard_map/ppermute | solution.py:737
  17.6 3.7 %collective-permute-done.3.got_odd = f32[224,128]{1,0:T(8,128)S(1)} collective-permute-done((f32[224,128]{1,0:T(8,128)S(1)}, f32[224,128]{1,0:T(8,128)S(1)}, u32[]{:S(2)}, u32[]{:S(2)}) %collective-permute-start.3) | collective-permute-done | bytes 114720 | tf_op jit(solution)/shard_map/ppermute | solution.py:738
  21.3 0.0 collective-permute-done.2.got_even
  21.3 11.0 %cycle.1 = f32[3,256,256]{2,1,0:T(8,128)} custom-call(f32[3,2,384,128]{3,2,1,0:T(8,128)S(1)} %get-tuple-element.23.source_in, f32[3,2,384,128]{3,2,1,0:T(8,128)S(1)} %get-tuple-element.24.once_in, f32[3,384,128]{2,1,0:T(8,128)S(1)} %get-tuple-element.25.seam_in, f32[3,2,192,128]{3,2,1,0:T(8,128)S(1)} %get-tuple-element.26.coarse_in, ...), custom_call_target="tpu_custom_call" | custom-call | tf_op jit(solution)/shard_map/cycle/pallas_call | solution.py:746
Async XLA Ops:
  1.3 7.2 %copy-start = (f32[3,256,256]{2,1,0:T(8,128)S(1)}, f32[3,256,256]{2,1,0:T(8,128)}, u32[]{:S(2)}) copy-start(f32[3,256,256]{2,1,0:T(8,128)} %x_ref.3) | copy-start | bytes 2359300
  1.3 7.2 %copy-start.1 = (f32[3,256,256]{2,1,0:T(8,128)S(1)}, f32[3,256,256]{2,1,0:T(8,128)}, u32[]{:S(2)}) copy-start(f32[3,256,256]{2,1,0:T(8,128)} %a_hbm.1) | copy-start | bytes 2359300
  1.3 7.2 %copy-start.2 = (f32[3,256,256]{2,1,0:T(8,128)S(1)}, f32[3,256,256]{2,1,0:T(8,128)}, u32[]{:S(2)}) copy-start(f32[3,256,256]{2,1,0:T(8,128)} %b_hbm.1) | copy-start | bytes 2359300
  3.3 8.1 %collective-permute-start = (f32[2,176,128]{2,1,0:T(8,128)S(1)}, f32[2,176,128]{2,1,0:T(8,128)S(1)}, u32[]{:S(2)}, u32[]{:S(2)}) collective-permute-start(f32[2,176,128]{2,1,0:T(8,128)S(1)} %get-tuple-element.21.sent_even), channel_id=1, source_target_pairs={{0,8},{16,24},{8,0},{24,16},{1,9},{17,25},{9,1},{25,17},{2,10},{18... | collective-permute-start | bytes 540680 | tf_op jit(solution)/shard_map/ppermute | solution.py:710
  3.8 8.9 %collective-permute-start.1 = (f32[2,176,128]{2,1,0:T(8,128)S(1)}, f32[2,176,128]{2,1,0:T(8,128)S(1)}, u32[]{:S(2)}, u32[]{:S(2)}) collective-permute-start(f32[2,176,128]{2,1,0:T(8,128)S(1)} %get-tuple-element.22.sent_odd), channel_id=1, source_target_pairs={{8,16},{16,8},{9,17},{17,9},{10,18},{18,10},{11,19},{19,11},{12,20... | collective-permute-start | bytes 540680 | tf_op jit(solution)/shard_map/ppermute | solution.py:711
  14.0 7.3 %collective-permute-start.3 = (f32[224,128]{1,0:T(8,128)S(1)}, f32[224,128]{1,0:T(8,128)S(1)}, u32[]{:S(2)}, u32[]{:S(2)}) collective-permute-start(f32[224,128]{1,0:T(8,128)S(1)} %get-tuple-element.28), channel_id=1, source_target_pairs={{1,2},{3,4},{5,6},{2,1},{4,3},{6,5},{9,10},{11,12},{13,14},{10,9},... | collective-permute-start | bytes 344072 | tf_op jit(solution)/shard_map/ppermute | solution.py:738
  15.9 5.4 %collective-permute-start.2 = (f32[224,128]{1,0:T(8,128)S(1)}, f32[224,128]{1,0:T(8,128)S(1)}, u32[]{:S(2)}, u32[]{:S(2)}) collective-permute-start(f32[224,128]{1,0:T(8,128)S(1)} %get-tuple-element.27.sent_even), channel_id=1, source_target_pairs={{0,1},{2,3},{4,5},{6,7},{1,0},{3,2},{5,4},{7,6},{8,9},{10,11},{12,... | collective-permute-start | bytes 344072 | tf_op jit(solution)/shard_map/ppermute | solution.py:737

commit v4 on v3

--- a/solution.py
+++ b/solution.py
@@ -35,6 +35,8 @@
 FIRST = HALO - STRIP
 RIM = 8
 SEAM = 6
+QUARTER = LANES // 4
+LEFT, RIGHT = 8, 24
 
 
 def lane_ids(rows):
@@ -163,10 +165,10 @@
                 built[k, pl.ds(c * STRIP + spot, 1), :] = other_a[k, pl.ds(line, 1), :]
                 built[k, pl.ds(c * STRIP + spot + 1, 1), :] = other_b[k, pl.ds(line, 1), :]
             for t in range(STRIP // 8):
-                lane = 4 * (chans * t + c)
+                lane = QUARTER * c + 4 * t
                 at = pl.ds(start + 8 * t, 8)
-                packed = jnp.where(eight == lane, roll(other_a[0, at, :], lane), packed)
-                packed = jnp.where(eight == lane + 1, roll(other_b[0, at, :], lane + 1), packed)
+                packed = jnp.where(eight == lane, roll(other_b[0, at, :], lane), packed)
+                packed = jnp.where(eight == lane + 1, roll(other_a[0, at, :], lane + 1), packed)
                 packed = jnp.where(eight == lane + 2, roll(other_a[tiles - 1, at, :], lane + 3), packed)
                 packed = jnp.where(eight == lane + 3, roll(other_b[tiles - 1, at, :], lane + 4), packed)
         built[0, chans * STRIP :, :] = packed
@@ -201,6 +203,8 @@
     def pick(k, low, n):
         return jnp.where(second, db[k, low : low + n, :], da[k, low : low + n, :])
 
+    seam_ref[...] = jnp.zeros(seam_ref.shape, jnp.float32)
+
     def channel(c, _):
         for k in range(tiles):
             at = pl.ds(k * LANES, LANES)
@@ -214,12 +218,22 @@
             for k in range(tiles):
                 source_ref[c, k, top + r : top + r + n, :] = found[k]
             ids = lane_ids(n)
-            seam = jnp.where(ids < SEAM, found[0], roll(found[tiles - 1], HALF))
+            base = QUARTER * c
             at = pl.ds(8 + r, n)
-            seam = jnp.where(ids == HALF, roll(da[tiles - 1, at, :], HALF + 1), seam)
-            seam = jnp.where(ids == HALF + 1, roll(db[tiles - 1, at, :], HALF + 2), seam)
-            seam = jnp.where(ids == LANES - 1, roll(da[0, at, :], -1), seam)
-            seam_ref[c, top + r : top + r + n, :] = jnp.where(ids == LANES - 2, roll(db[0, at, :], -2), seam)
+            seam = pltpu.roll(found[0], base + LEFT, 1)
+            for source, cell, lane in (
+                (found[tiles - 1], LANES - SEAM, RIGHT - SEAM),
+                (da[0, at, :], 0, LEFT - 1),
+                (db[0, at, :], 0, LEFT - 2),
+                (da[tiles - 1, at, :], LANES - 1, RIGHT),
+                (db[tiles - 1, at, :], LANES - 1, RIGHT + 1),
+            ):
+                spot = (ids >= base + lane) & (ids < base + lane + (SEAM if cell == LANES - SEAM else 1))
+                seam = jnp.where(spot, pltpu.roll(source, base + lane + (LANES - cell) % LANES, 1), seam)
+            at = pl.ds(top + r, n)
+            mine = (ids >= base + LEFT - 2) & (ids < base + RIGHT + 2)
+            mine = mine & ((ids < base + LEFT + SEAM) | (ids >= base + RIGHT - SEAM))
+            seam_ref[at, :] = jnp.where(mine, seam, seam_ref[at, :])
         source, once = source_ref.at[c], once_ref.at[c]
 
         def first(piece, turned):
@@ -244,17 +258,15 @@
     lax.fori_loop(0, chans, channel, 0)
 
 
-def seam_units(chans, height):
-    tiles_of = (height - 2 * FIRST) // 8
-    for unit in range(chans * tiles_of):
-        yield unit // tiles_of, FIRST + 8 * (unit % tiles_of), unit // 16, 8 * (unit % 16)
+def seam_units(height):
+    for t in range((height - 2 * FIRST) // 8):
+        yield FIRST + 8 * t, t // 4, t % 4
 
 
 def message_rows(chans, height):
     quarter = height // 2
     cells = (chans // 2 * quarter + chans % 2 * quarter // 2) // 2
-    units = -(-chans * ((height - 2 * FIRST) // 8) // 16) * 8
-    return cells, units
+    return cells, -(-(height - 2 * FIRST) // 32) * 8
 
 
 def column_rows(chans, height):
@@ -276,6 +288,8 @@
     active = cover_ref[0, 0].astype(jnp.float32)
     marked = label_ref[0, 0].astype(jnp.float32)
     eight = lane_ids(8)
+
+    place = eight & (QUARTER - 1)
 
     def take(top, got):
         low = FIRST if top else HALO + rows
@@ -301,19 +315,23 @@
                 for_theirs = NEAR * their_active * jnp.where(their_mark == 1.0, my_b, my_a)
                 source_ref[c, k, edge : edge + 1, :] = source_ref[c, k, edge : edge + 1, :] - for_mine
                 source_ref[c, k, other : other + 1, :] = source_ref[c, k, other : other + 1, :] - for_theirs
-            for t in range(STRIP // 8):
-                lane = 4 * (chans * t + c)
-                last = roll(packed, HALF - lane - 2)
-                once_a, once_b = roll(packed, LANES - 1 - lane), roll(packed, LANES - 2 - lane - 1)
-                cells = jnp.where(eight == LANES - 1, once_a, jnp.where(eight == LANES - 2, once_b, last))
-                r = low + 8 * t
-                cells = jnp.where(eight < SEAM, source_ref[c, 0, r : r + 8, :], cells)
-                end = roll(source_ref[c, tiles - 1, r : r + 8, :], HALF)
-                seam_ref[c, r : r + 8, :] = jnp.where((eight >= HALF - SEAM) & (eight < HALF), end, cells)
-            r = edge // 8 * 8
-            cells = jnp.where(eight < SEAM, source_ref[c, 0, r : r + 8, :], seam_ref[c, r : r + 8, :])
-            end = roll(source_ref[c, tiles - 1, r : r + 8, :], HALF)
-            seam_ref[c, r : r + 8, :] = jnp.where((eight >= HALF - SEAM) & (eight < HALF), end, cells)
+
+        def seam_of(r, cells):
+            for c in range(chans):
+                base = QUARTER * c
+                spot = (eight >= base + LEFT) & (eight < base + LEFT + SEAM)
+                cells = jnp.where(spot, roll(source_ref[c, 0, r : r + 8, :], base + LEFT), cells)
+                spot = (eight >= base + RIGHT - SEAM) & (eight < base + RIGHT)
+                cells = jnp.where(spot, roll(source_ref[c, tiles - 1, r : r + 8, :], base + RIGHT), cells)
+            seam_ref[r : r + 8, :] = cells
+
+        for t in range(STRIP // 8):
+            firsts, lasts = roll(packed, LEFT - 2 - 4 * t), roll(packed, RIGHT - 2 - 4 * t)
+            cells = jnp.where((place == LEFT - 2) | (place == LEFT - 1), firsts, 0.0)
+            cells = jnp.where((place == RIGHT) | (place == RIGHT + 1), lasts, cells)
+            seam_of(low + 8 * t, jnp.where(eight < QUARTER * chans, cells, 0.0))
+        r = edge // 8 * 8
+        seam_of(r, seam_ref[r : r + 8, :])
 
     def arrange(upper, lower, mine_up, mine_low):
         upper_got[...] = upper[...]
@@ -380,18 +398,13 @@
             left[8 * t : 8 * t + 8, :] = jnp.where(first_half, upper, roll(lower, HALF))
             right[8 * t : 8 * t + 8, :] = jnp.where(first_half, roll(upper, HALF), lower)
         lefts = rights = jnp.zeros((8, LANES), jnp.float32)
-        last = None
-        for c, r, tile, lane in [*seam_units(chans, height), (None, None, -1, 0)]:
-            if tile != last and last is not None:
-                at = cells + 8 * last
-                left[at : at + 8, :], right[at : at + 8, :] = lefts, rights
-            last = tile
-            if c is None:
-                break
-            value = seam_ref[c, r : r + 8, :]
-            spot = (eight >= lane) & (eight < lane + 8)
-            lefts = jnp.where(spot, roll(value, lane + 2), lefts)
-            rights = jnp.where(spot, roll(value, lane - (HALF - SEAM)), rights)
+        for r, tile, slot in seam_units(height):
+            value = seam_ref[r : r + 8, :]
+            spot = (place >> 3) == slot
+            lefts = jnp.where(spot, roll(value, 8 * slot - (LEFT - 2)), lefts)
+            rights = jnp.where(spot, roll(value, 8 * slot - (RIGHT - SEAM)), rights)
+            at = cells + 8 * tile
+            left[at : at + 8, :], right[at : at + 8, :] = lefts, rights
         for out in (left, right):
             out[cells + units : cells + units + 8, :] = marks_ref[...]
 
@@ -410,7 +423,7 @@
 
 def cycle(
     source_in, once_in, seam_in, coarse_in, sent_even, got_even, got_odd, x_ref, out_hbm,
-    out_ref, sems, right_ref, left_ref, seam_source, seam_once, seam_rest, fine, fine_two, *bufs,
+    out_ref, sems, right_ref, left_ref, seam_source, seam_once, seam_rest, fine, fine_two, fix, *bufs,
 ):
     chans, own_tiles, height, _ = source_in.shape
     rows = height - 2 * HALO
@@ -437,13 +450,13 @@
     own = [mark(sent_even, i) for i in range(6)]
     right = [mark(right_ref, i) for i in range(6)]
     left = [mark(left_ref, i) for i in range(6)]
-    quarter3 = eight < HALF + HALF // 2
     first_half = eight < HALF
+    place = eight & (QUARTER - 1)
 
     def mixed(i):
-        return jnp.where(first_half, own[i], jnp.where(quarter3, right[i], left[i]))
-
-    seam_scale = [mixed(i) * NEAR for i in range(3)]
+        return jnp.where(place < LEFT, left[i], jnp.where(place < RIGHT, own[i], right[i]))
+
+    seam_scale = [jnp.where(eight < QUARTER * chans, mixed(i), 0.0) * NEAR for i in range(3)]
     seam_mark = [mixed(i + 3) == 1.0 for i in range(3)]
     own_scale = [own[i] * NEAR for i in range(3)]
     side_scale = [jnp.where(first_half, right[i], left[i]) * NEAR for i in range(3)]
@@ -461,56 +474,49 @@
     def scales(depth, r, n):
         return [over_rows(own_scale, depth, r, n)] * own_tiles + [over_rows(side_scale, depth, r, n)]
 
-    inner = (eight < SEAM) | ((eight >= HALF - SEAM) & (eight < HALF))
-    outer = ((eight >= HALF) & (eight < HALF + SEAM)) | (eight >= LANES - SEAM)
-    from_near = (eight == 0) | (eight == HALF - 1)
-    from_own = (eight == HALF) | (eight == LANES - 1)
-    up_one = (eight == HALF - 1) | (eight == LANES - 1)
-    near_b = (eight == HALF - 2) | (eight == 1)
-    right_unit = (eight >= HALF - 2) & (eight < HALF + SEAM)
+    inner = ((place >= LEFT) & (place < LEFT + SEAM)) | ((place >= RIGHT - SEAM) & (place < RIGHT))
+    outer = ((place >= LEFT - SEAM) & (place < LEFT)) | ((place >= RIGHT) & (place < RIGHT + SEAM))
+    from_near = (place == LEFT) | (place == RIGHT - 1)
+    from_own = (place == LEFT - 1) | (place == RIGHT)
+    up_one = (place == LEFT - 1) | (place == RIGHT - 1)
+    near_b = (place == LEFT + 1) | (place == RIGHT - 2)
+    right_unit = place >= RIGHT - 2
+
     def unpack(unit):
-        c, r, tile, lane = unit
-        rights = roll(right_ref[cells + 8 * tile : cells + 8 * tile + 8, :], HALF - 2 - lane)
-        lefts = roll(left_ref[cells + 8 * tile : cells + 8 * tile + 8, :], LANES - SEAM - lane)
+        r, tile, slot = unit
+        rights = roll(right_ref[cells + 8 * tile : cells + 8 * tile + 8, :], RIGHT - 2 - 8 * slot)
+        lefts = roll(left_ref[cells + 8 * tile : cells + 8 * tile + 8, :], LEFT - SEAM - 8 * slot)
         return rights, lefts
 
     def keep_near(unit, turned):
-        c, r, _, _ = unit
-        seam_rest[c, 0, r : r + 8, :] = jnp.where(right_unit, *turned)
+        r = unit[0]
+        seam_rest[0, r : r + 8, :] = jnp.where(right_unit, *turned)
 
     def second_cells(unit):
-        c, r, _, _ = unit
-        cells_b = jnp.where(near_b, seam_rest[c, 0, r : r + 8, :], seam_in[c, r : r + 8, :])
+        r = unit[0]
+        cells_b = jnp.where(near_b, seam_rest[0, r : r + 8, :], seam_in[r : r + 8, :])
         return roll(cells_b, 1), roll(cells_b, -1)
 
     def put_seam(unit, turned):
-        c, r, _, _ = unit
+        r = unit[0]
         band = 0 if r < HALO else 1 if r < HALO + rows else 2
-        near, mine = seam_rest[c, 0, r : r + 8, :], seam_in[c, r : r + 8, :]
+        near, mine = seam_rest[0, r : r + 8, :], seam_in[r : r + 8, :]
         value = jnp.where(inner, mine, jnp.where(outer, near, 0.0))
         border = jnp.where(seam_mark[band], jnp.where(up_one, *turned), jnp.where(from_near, near, mine))
         border = jnp.where(from_near | from_own, border, 0.0)
-        seam_source[c, 0, r : r + 8, :] = value - seam_scale[band] * border
-
-    units_of = list(seam_units(chans, height))
-    staggered(units_of, unpack, keep_near, 24)
-    staggered(units_of, second_cells, put_seam, 24)
-    spots = [(c, r, n) for c in range(chans) for r, n in spans(FIRST, height - FIRST, 2 * STEP)]
-
-    def seam_first(spot, turned):
-        c, r, n = spot
-        source = seam_source.at[c]
-        _, found = swept(source, source, [over_rows(seam_scale, 0, r, n)], 1, r, n, True, turned)
-        seam_once[c, 0, r : r + n, :] = found[0]
-
-    def seam_second(spot, turned):
-        c, r, n = spot
-        scale = [over_rows(seam_scale, 0, r, n)]
-        mids, found = swept(seam_once.at[c], seam_source.at[c], scale, 1, r, n, True, turned)
-        seam_rest[c, 0, r : r + n, :] = found[0] - mids[0]
-
-    staggered(spots, lambda spot: turn(seam_source.at[spot[0]], 1, *spot[1:]), seam_first, 0)
-    staggered(spots, lambda spot: turn(seam_once.at[spot[0]], 1, *spot[1:]), seam_second, 0)
+        seam_source[0, r : r + 8, :] = value - seam_scale[band] * border
+
+    staggered(seam_units(height), unpack, keep_near, 24)
+    staggered(seam_units(height), second_cells, put_seam, 24)
+    for r, n in spans(FIRST, height - FIRST, height):
+        _, found = swept(
+            seam_source, seam_source, [over_rows(seam_scale, 0, r, n)], 1, r, n, True, turn(seam_source, 1, r, n)
+        )
+        seam_once[0, r : r + n, :] = found[0]
+        mids, found = swept(
+            seam_once, seam_source, [over_rows(seam_scale, 0, r, n)], 1, r, n, True, turn(seam_once, 1, r, n)
+        )
+        seam_rest[0, r : r + n, :] = found[0] - mids[0]
 
     one_src, one_once, one_two = bufs[0:3]
     half_rows = height // 2
@@ -524,21 +530,34 @@
             value = jnp.where(first_half, from_right, roll(from_left, HALF))
         else:
             value = jnp.where(first_half, roll(from_right, HALF), from_left)
-        one_src[c, own_tiles, 8 + r : 16 + r, :] = jnp.where(even_lane, value, roll(value, 1))
-        one_src[d, own_tiles, 8 + s : 16 + s, :] = jnp.where(even_lane, roll(value, -1), value)
-    for c in range(chans):
+        if c == d:
+            one_src[c // 2, own_tiles, 8 + r : 16 + r, :] = jnp.where(even_lane, value, roll(value, 1))
+            one_src[c // 2, own_tiles, 8 + s : 16 + s, :] = jnp.where(even_lane, roll(value, -1), value)
+        else:
+            one_src[c // 2, own_tiles, 8 + r : 16 + r, :] = value
+
+    pairs = [(c, min(c + 1, chans - 1)) for c in range(0, chans, 2)]
+
+    def paired(of, pair, n):
+        first, second = pair
+        return of(first) if first == second else jnp.where((lane_ids(n) & 1) == 0, of(first), of(second))
+
+    for f, pair in enumerate(pairs):
         for r, n in spans(0, half_rows):
             for k in range(own_tiles):
-                one_src[c, k, 8 + r : 8 + r + n, :] = coarse_in[c, k, r : r + n, :]
-        for r, n in spans(FIRST // 2, half_rows - FIRST // 2):
-            ids = lane_ids(n)
-            seam = restricted(seam_rest.at[c], 0, 2 * r, n, 1)
-            turned = roll(seam, HALF)
-            at = pl.ds(8 + r, n)
-            one_src[c, 0, at, :] = jnp.where(ids < 4, seam, one_src[c, 0, at, :])
-            one_src[c, own_tiles - 1, at, :] = jnp.where(ids >= LANES - 4, turned, one_src[c, own_tiles - 1, at, :])
-            side = jnp.where(ids < 4, turned, one_src[c, own_tiles, at, :])
-            one_src[c, own_tiles, at, :] = jnp.where(ids >= LANES - 4, seam, side)
+                one_src[f, k, 8 + r : 8 + r + n, :] = paired(lambda c: coarse_in[c, k, r : r + n, :], pair, n)
+    for r, n in spans(FIRST // 2, half_rows - FIRST // 2):
+        ids = lane_ids(n)
+        seam = restricted(seam_rest, 0, 2 * r, n, 1)
+        at = pl.ds(8 + r, n)
+        for f, pair in enumerate(pairs):
+            by_left = paired(lambda c: roll(seam, -QUARTER * c - LEFT), pair, n)
+            by_right = paired(lambda c: roll(seam, -QUARTER * c - RIGHT), pair, n)
+            one_src[f, 0, at, :] = jnp.where(ids < 4, by_left, one_src[f, 0, at, :])
+            inner_end = one_src[f, own_tiles - 1, at, :]
+            one_src[f, own_tiles - 1, at, :] = jnp.where(ids >= LANES - 4, by_right, inner_end)
+            side = jnp.where(ids < 4, by_right, one_src[f, own_tiles, at, :])
+            one_src[f, own_tiles, at, :] = jnp.where(ids >= LANES - 4, by_left, side)
 
     def smooth(src, once, fields, depth, into, minus=False):
         def one_sweep(spot, turned):
@@ -571,16 +590,13 @@
 
     assert chans <= 4 and LEVELS >= 3
 
-    def spread_channel(value, f):
-        ids = lane_ids(value.shape[0])
-        odd = (ids & 1) == 1
-        pair = jnp.where(odd, value, roll(value, -1)) if f & 1 else jnp.where(odd, roll(value, 1), value)
-        high = (ids & 2) == 2
-        return jnp.where(high, pair, roll(pair, -2)) if f & 2 else jnp.where(high, roll(pair, 2), pair)
+    def spread_pair(value, f):
+        high = (lane_ids(value.shape[0]) & 2) == 2
+        return jnp.where(high, value, roll(value, -2)) if f else jnp.where(high, roll(value, 2), value)
 
     def level(depth):
         src, once, two = bufs[3 * (depth - 1) : 3 * depth]
-        fields = chans if depth == 1 else 1
+        fields = len(pairs) if depth == 1 else 1
         if depth == LEVELS - 1:
             held = src
             for sweep in range(1, COARSE):
@@ -593,34 +609,49 @@
         below = bufs[3 * depth]
         shift = 1 << depth
         for r, n in spans(0, height >> (depth + 1)):
-            ids = lane_ids(n) & 3
+            half = (lane_ids(n) & 2) >> 1
             for k in range(tiles):
                 value = None
                 for f in range(fields):
                     total = restricted(two.at[f], k, 8 + 2 * r, n, shift)
-                    value = total if value is None else jnp.where(ids == f, total, value)
+                    value = total if value is None else jnp.where(half == f, total, value)
                 below[0, k, 8 + r : 8 + r + n, :] = value
         fix = level(depth + 1)
-        expand(fix, fields, depth, two, 0, height >> (depth + 1), spread_channel if depth == 1 else None)
+        expand(fix, fields, depth, two, 0, height >> (depth + 1), spread_pair if depth == 1 else None)
         add_fix(once, two, fields, depth, once)
         smooth(src, once, fields, depth, two)
         smooth(src, two, fields, depth, once)
         return once
 
-    fix = level(1)
+    paired_fix = level(1)
     low, high = HALO - RIM, HALO + rows + RIM
+    for f, (even, odd) in enumerate(pairs):
+        for r, n in spans(low // 2, high // 2):
+            at = pl.ds(8 + r, n)
+            odd_lane = (lane_ids(n) & 1) == 1
+            for k in range(tiles):
+                value = paired_fix[f, k, at, :]
+                if even == odd:
+                    fix[even, k, at, :] = value
+                else:
+                    fix[even, k, at, :] = jnp.where(odd_lane, roll(value, 1), value)
+                    fix[odd, k, at, :] = jnp.where(odd_lane, value, roll(value, -1))
+
+    def at_borders(seam, c):
+        base = QUARTER * c
+        return pltpu.roll(seam, LANES - LEFT - base, 1), pltpu.roll(seam, LANES - RIGHT - base, 1)
 
     def fine_source(c):
         def tile(k, r, n):
             ids = lane_ids(n)
-            seam = seam_source[c, 0, r : r + n, :]
+            by_left, by_right = at_borders(seam_source[0, r : r + n, :], c)
             if k == own_tiles:
-                return jnp.where(ids < HALF, roll(seam, HALF), seam)
+                return jnp.where(ids < HALF, by_right, by_left)
             value = source_in[c, k, r : r + n, :]
             if k == 0:
-                value = jnp.where(ids == 0, seam, value)
+                value = jnp.where(ids == 0, by_left, value)
             if k == own_tiles - 1:
-                value = jnp.where(ids == LANES - 1, roll(seam, HALF), value)
+                value = jnp.where(ids == LANES - 1, by_right, value)
             return value
 
         return tile
@@ -634,17 +665,16 @@
                 fine[k, pl.ds(9 + 2 * r, n, stride=2), :] = value
         for r, n in spans(low, high):
             ids = lane_ids(n)
-            seam = seam_once[c, 0, r : r + n, :]
-            turned = roll(seam, HALF)
+            by_left, by_right = at_borders(seam_once[0, r : r + n, :], c)
             at = pl.ds(8 + r, n)
             for k in range(own_tiles):
                 value = once_in[c, k, r : r + n, :]
                 if k == 0:
-                    value = jnp.where(ids < 2, seam, value)
+                    value = jnp.where(ids < 2, by_left, value)
                 if k == own_tiles - 1:
-                    value = jnp.where(ids >= LANES - 2, turned, value)
+                    value = jnp.where(ids >= LANES - 2, by_right, value)
                 fine[k, at, :] = fine[k, at, :] + value
-            fine[own_tiles, at, :] = fine[own_tiles, at, :] + jnp.where(ids < HALF, turned, seam)
+            fine[own_tiles, at, :] = fine[own_tiles, at, :] + jnp.where(ids < HALF, by_right, by_left)
         add = fine_source(c)
 
         def first(piece, turned):
@@ -690,7 +720,8 @@
     params = pltpu.CompilerParams(vmem_limit_bytes=40 * 1024 * 1024)
     group, blk = lax.axis_size("group"), lax.axis_size("blk")
     central = sds((chans, tiles, height, LANES))
-    column = sds((chans, height, LANES))
+    assert chans <= 4
+    column = sds((height, LANES))
     coarse = sds((chans, tiles, height // 2, LANES))
     upright = sds((tiles, chans * STRIP + 8, LANES))
     beside = sds((sum(message_rows(chans, height)) + 8, LANES))
@@ -738,10 +769,11 @@
     got_odd = lax.ppermute(sent_odd, "blk", swaps(blk, 1))
 
     scratch = [pltpu.VMEM(image_a.shape, f32), pltpu.SemaphoreType.DMA((chans,))]
-    scratch += [pltpu.VMEM(beside.shape, f32)] * 2 + [pltpu.VMEM((chans, 1, height, LANES), f32)] * 3
+    scratch += [pltpu.VMEM(beside.shape, f32)] * 2 + [pltpu.VMEM((1, height, LANES), f32)] * 3
     scratch += [pltpu.VMEM((tiles + 1, height + 16, LANES), f32)] * 2
+    scratch += [pltpu.VMEM((chans, tiles + 1, height // 2 + 16, LANES), f32)]
     for depth in range(1, LEVELS):
-        fields = chans if depth == 1 else 1
+        fields = (chans + 1) // 2 if depth == 1 else 1
         scratch += [pltpu.VMEM((fields, tiles + 1, (height >> depth) + 16, LANES), f32)] * 3
     return pl.pallas_call(
         cycle,

time: 32.7 us -> 29 us (0.89)
  Pallas kernels: 17.2 us -> 13.4 us
    pallas_call x1, Pallas kernels: 11 us -> 7.38 us  [shards(): pl.pallas_call(cycle, out_shape=sds((chans, rows, cols)), in_specs=[vmem]...]
  transfers between devices with their start and end apart: 4 -> 4, of which waited for: 2 -> 2; matrix products, arithmetic and copies ran while one was open for 0% -> 0% of each run, Pallas kernels for 9% -> 11%
where the time goes in v4:
time: 29 us; the launch traced here: 28.7 us
  Pallas kernels  13.4 us (46%)
  starting transfers between devices  8.69 us (30%)
  waiting for transfers between devices  5.17 us (18%)
  between operations  1.39 us (5%)
    pallas_call x1, Pallas kernels, shards(): pl.pallas_call(cycle, out_shape=sds((chans, rows, cols)), in_specs=[vmem]...  7.38 us
    ppermute x1, starting transfers between devices, shards(): got_odd = lax.ppermute(sent_odd, 'group', swaps(group, 1))  4.6 us
    ppermute x1, waiting for transfers between devices, shards(): got_odd = lax.ppermute(sent_odd, 'blk', swaps(blk, 1))  4.01 us
    pallas_call x1, Pallas kernels, shards(): pl.pallas_call(inside, out_shape=(central, central, column, coarse), in_s...  3.05 us
    pallas_call x1, Pallas kernels, shards(): pl.pallas_call(strips, out_shape=(upright, upright), in_specs=[hbm, hbm,...  1.97 us
    ppermute x1, starting transfers between devices, shards(): got_odd = lax.ppermute(sent_odd, 'blk', swaps(blk, 1))  1.93 us
    ppermute x1, starting transfers between devices, shards(): got_even = lax.ppermute(sent_even, 'blk', swaps(blk, 0))  1.65 us
    ppermute x1, waiting for transfers between devices, shards(): got_odd = lax.ppermute(sent_odd, 'group', swaps(group, 1))  1.16 us
  transfers between devices with their start and end apart: 4, of which 2 were waited for; matrix products, arithmetic and copies ran while one was open for 0% of the time, Pallas kernels for 11%

profile of v4, /device:TPU:12, one launch (start us, length us, event | category | flops | bytes accessed | tf_op | source)
XLA Modules:
  0.0 28.7 jit_solution(17244465978331342374)
XLA Ops:
  1.3 0.0 copy-start
  1.3 0.0 copy-start.1
  1.3 0.0 copy-start.2
  1.3 2.0 %strips.1 = (f32[2,176,128]{2,1,0:T(8,128)S(1)}, f32[2,176,128]{2,1,0:T(8,128)S(1)}) custom-call(f32[3,256,256]{2,1,0:T(8,128)} %a_hbm.1, f32[3,256,256]{2,1,0:T(8,128)} %b_hbm.1, f32[3,256,256]{2,1,0:T(8,128)} %x_ref.3, s32[1,1]{1,0:T(1,128)S(6)} %copy.14.cover_ref, s32[1,1]{1,0:T(1,128)S(6)} %copy.15.label_ref), custom_call_target="tpu_custom_call" | custom-call | tf_op jit(solution)/shard_map/strips/pallas_call | solution.py:729
  3.3 0.5 %collective-permute-start = (f32[2,176,128]{2,1,0:T(8,128)S(1)}, f32[2,176,128]{2,1,0:T(8,128)S(1)}, u32[]{:S(2)}, u32[]{:S(2)}) collective-permute-start(f32[2,176,128]{2,1,0:T(8,128)S(1)} %get-tuple-element.21.sent_even), channel_id=1, source_target_pairs={{0,8},{16,24},{8,0},{24,16},{1,9},{17,25},{9,1},{25,17},{2,10},{18... | collective-permute-start | bytes 540680 | tf_op jit(solution)/shard_map/ppermute | solution.py:741
  3.8 4.6 %collective-permute-start.1 = (f32[2,176,128]{2,1,0:T(8,128)S(1)}, f32[2,176,128]{2,1,0:T(8,128)S(1)}, u32[]{:S(2)}, u32[]{:S(2)}) collective-permute-start(f32[2,176,128]{2,1,0:T(8,128)S(1)} %get-tuple-element.22.sent_odd), channel_id=1, source_target_pairs={{8,16},{16,8},{9,17},{17,9},{10,18},{18,10},{11,19},{19,11},{12,20... | collective-permute-start | bytes 540680 | tf_op jit(solution)/shard_map/ppermute | solution.py:742
  8.4 0.0 copy-done
  8.4 0.0 copy-done.1
  8.4 0.0 copy-done.2
  8.5 3.0 %inside.1 = (f32[3,2,384,128]{3,2,1,0:T(8,128)S(1)}, f32[3,2,384,128]{3,2,1,0:T(8,128)S(1)}, f32[384,128]{1,0:T(8,128)S(1)}, f32[3,2,192,128]{3,2,1,0:T(8,128)S(1)}) custom-call(f32[3,256,256]{2,1,0:T(8,128)S(1)} %copy-done.1, f32[3,256,256]{2,1,0:T(8,128)S(1)} %copy-done.2, f32[3,256,256]{2,1,0:T(8,128)S(1)} %copy-done, s32[1,1]{1,0:T(1,128)S(6)} %copy.14.cover_ref, ...), custom_call_target="tpu_custom_call" | custom-call | flops 200000000 | bytes 4000000 | tf_op jit(solution)/shard_map/inside/pallas_call | solution.py:744
  11.5 0.0 collective-permute-done.got_even
  11.5 1.2 %collective-permute-done.1.got_odd = f32[2,176,128]{2,1,0:T(8,128)S(1)} collective-permute-done((f32[2,176,128]{2,1,0:T(8,128)S(1)}, f32[2,176,128]{2,1,0:T(8,128)S(1)}, u32[]{:S(2)}, u32[]{:S(2)}) %collective-permute-start.1) | collective-permute-done | bytes 180256 | tf_op jit(solution)/shard_map/ppermute | solution.py:742
  12.7 1.0 %join_rows.1 = (f32[3,2,384,128]{3,2,1,0:T(8,128)S(1)}, f32[3,2,384,128]{3,2,1,0:T(8,128)S(1)}, f32[384,128]{1,0:T(8,128)S(1)}, f32[3,2,192,128]{3,2,1,0:T(8,128...) custom-call(f32[3,2,384,128]{3,2,1,0:T(8,128)S(1)} %get-tuple-elemen, ...), custom_call_target="tpu_custom_call", output_to_operand_aliasing={{0}: (0, {}), {1}: (1, {}), {2}: (2, {}), {3}: (3, {})} | custom-call | tf_op jit(solution)/shard_map/join_rows/pallas_call | solution.py:755
  13.7 1.9 %collective-permute-start.3 = (f32[248,128]{1,0:T(8,128)S(1)}, f32[248,128]{1,0:T(8,128)S(1)}, u32[]{:S(2)}, u32[]{:S(2)}) collective-permute-start(f32[248,128]{1,0:T(8,128)S(1)} %get-tuple-element.28), channel_id=1, source_target_pairs={{1,2},{3,4},{5,6},{2,1},{4,3},{6,5},{9,10},{11,12},{13,14},{10,9},... | collective-permute-start | bytes 380936 | tf_op jit(solution)/shard_map/ppermute | solution.py:769
  15.6 1.6 %collective-permute-start.2 = (f32[248,128]{1,0:T(8,128)S(1)}, f32[248,128]{1,0:T(8,128)S(1)}, u32[]{:S(2)}, u32[]{:S(2)}) collective-permute-start(f32[248,128]{1,0:T(8,128)S(1)} %get-tuple-element.27.sent_even), channel_id=1, source_target_pairs={{0,1},{2,3},{4,5},{6,7},{1,0},{3,2},{5,4},{7,6},{8,9},{10,11},{12,... | collective-permute-start | bytes 380936 | tf_op jit(solution)/shard_map/ppermute | solution.py:768
  17.3 4.0 %collective-permute-done.3.got_odd = f32[248,128]{1,0:T(8,128)S(1)} collective-permute-done((f32[248,128]{1,0:T(8,128)S(1)}, f32[248,128]{1,0:T(8,128)S(1)}, u32[]{:S(2)}, u32[]{:S(2)}) %collective-permute-start.3) | collective-permute-done | bytes 127008 | tf_op jit(solution)/shard_map/ppermute | solution.py:769
  21.3 0.0 collective-permute-done.2.got_even
  21.3 7.4 %cycle.1 = f32[3,256,256]{2,1,0:T(8,128)} custom-call(f32[3,2,384,128]{3,2,1,0:T(8,128)S(1)} %get-tuple-element.23.source_in, f32[3,2,384,128]{3,2,1,0:T(8,128)S(1)} %get-tuple-element.24.once_in, f32[384,128]{1,0:T(8,128)S(1)} %get-tuple-element.25.seam_in, f32[3,2,192,128]{3,2,1,0:T(8,128)S(1)} %get-tuple-element.26.coarse_in, ...), custom_call_target="tpu_custom_call" | custom-call | tf_op jit(solution)/shard_map/cycle/pallas_call | solution.py:778
Async XLA Ops:
  1.3 7.1 %copy-start = (f32[3,256,256]{2,1,0:T(8,128)S(1)}, f32[3,256,256]{2,1,0:T(8,128)}, u32[]{:S(2)}) copy-start(f32[3,256,256]{2,1,0:T(8,128)} %x_ref.3) | copy-start | bytes 2359300
  1.3 7.1 %copy-start.1 = (f32[3,256,256]{2,1,0:T(8,128)S(1)}, f32[3,256,256]{2,1,0:T(8,128)}, u32[]{:S(2)}) copy-start(f32[3,256,256]{2,1,0:T(8,128)} %a_hbm.1) | copy-start | bytes 2359300
  1.3 7.1 %copy-start.2 = (f32[3,256,256]{2,1,0:T(8,128)S(1)}, f32[3,256,256]{2,1,0:T(8,128)}, u32[]{:S(2)}) copy-start(f32[3,256,256]{2,1,0:T(8,128)} %b_hbm.1) | copy-start | bytes 2359300
  3.3 8.2 %collective-permute-start = (f32[2,176,128]{2,1,0:T(8,128)S(1)}, f32[2,176,128]{2,1,0:T(8,128)S(1)}, u32[]{:S(2)}, u32[]{:S(2)}) collective-permute-start(f32[2,176,128]{2,1,0:T(8,128)S(1)} %get-tuple-element.21.sent_even), channel_id=1, source_target_pairs={{0,8},{16,24},{8,0},{24,16},{1,9},{17,25},{9,1},{25,17},{2,10},{18... | collective-permute-start | bytes 540680 | tf_op jit(solution)/shard_map/ppermute | solution.py:741
  3.8 8.9 %collective-permute-start.1 = (f32[2,176,128]{2,1,0:T(8,128)S(1)}, f32[2,176,128]{2,1,0:T(8,128)S(1)}, u32[]{:S(2)}, u32[]{:S(2)}) collective-permute-start(f32[2,176,128]{2,1,0:T(8,128)S(1)} %get-tuple-element.22.sent_odd), channel_id=1, source_target_pairs={{8,16},{16,8},{9,17},{17,9},{10,18},{18,10},{11,19},{19,11},{12,20... | collective-permute-start | bytes 540680 | tf_op jit(solution)/shard_map/ppermute | solution.py:742
  13.7 7.6 %collective-permute-start.3 = (f32[248,128]{1,0:T(8,128)S(1)}, f32[248,128]{1,0:T(8,128)S(1)}, u32[]{:S(2)}, u32[]{:S(2)}) collective-permute-start(f32[248,128]{1,0:T(8,128)S(1)} %get-tuple-element.28), channel_id=1, source_target_pairs={{1,2},{3,4},{5,6},{2,1},{4,3},{6,5},{9,10},{11,12},{13,14},{10,9},... | collective-permute-start | bytes 380936 | tf_op jit(solution)/shard_map/ppermute | solution.py:769
  15.6 5.7 %collective-permute-start.2 = (f32[248,128]{1,0:T(8,128)S(1)}, f32[248,128]{1,0:T(8,128)S(1)}, u32[]{:S(2)}, u32[]{:S(2)}) collective-permute-start(f32[248,128]{1,0:T(8,128)S(1)} %get-tuple-element.27.sent_even), channel_id=1, source_target_pairs={{0,1},{2,3},{4,5},{6,7},{1,0},{3,2},{5,4},{7,6},{8,9},{10,11},{12,... | collective-permute-start | bytes 380936 | tf_op jit(solution)/shard_map/ppermute | solution.py:768

commit v5 on v4

--- a/solution.py
+++ b/solution.py
@@ -109,9 +109,16 @@
     return total + jnp.where(even, roll(total, -shift), roll(total, shift))
 
 
+def strip_rows(chans, tiles):
+    assert tiles == 2 and 2 * chans + 2 <= 8
+    at_coarse = 8 * tiles * chans
+    at_seam = at_coarse + chans * (HALO // 2)
+    return at_coarse, at_seam, at_seam + 8 * -(-STRIP // 16)
+
+
 def strips(
     a_hbm, b_hbm, x_hbm, cover_ref, label_ref, even_ref, odd_ref,
-    a_both, b_both, x_both, picked, other_a, other_b, built, sems,
+    a_both, b_both, x_both, picked, other_a, other_b, source, once, rest, built, sems,
 ):
     chans, block, cols = a_hbm.shape
     rows = HALO
@@ -142,38 +149,72 @@
 
     def message(step, a_ref, b_ref, x_ref):
         top = step == 0
-        low = jnp.where(top, 0, rows - STRIP)
+        start = pl.multiple_of(jnp.where(top, 0, rows - STRIP), 8)
+        near = pl.multiple_of(jnp.where(top, 8, rows), 8)
         line = jnp.where(top, 0, rows - 1)
-        spot = jnp.where(top, STRIP - 2, 0)
+        at_coarse, at_seam, at_marks = strip_rows(chans, tiles)
+        scale = [active * NEAR] * tiles
+        place = eight & (QUARTER - 1)
+        seams = [jnp.zeros((8, LANES), jnp.float32) for _ in range(STRIP // 8)]
+        channels = range(chans)
+        for c in channels:
+            for k in range(tiles):
+                for edge in (7, 8 + rows):
+                    picked[c, k, edge : edge + 1, :] = jnp.zeros((1, LANES), jnp.float32)
+                at = pl.ds(k * LANES, LANES)
+                x = x_ref[c, :, at]
+                from_a, from_b = a_ref[c, :, at] - x, b_ref[c, :, at] - x
+                other_a[c, k], other_b[c, k] = from_a, from_b
+                picked[c, k, 8 : 8 + rows, :] = jnp.where(second, from_b, from_a)
+        for c in channels:
+            parts = [[picked[c, k, 8 + s : 8 + s + rows, :] for k in range(tiles)] for s in (0, -1, 1)]
+            for k, found in enumerate(own_source(*parts, active)):
+                source[c, k, 8 : 8 + rows, :] = found
+        for c in channels:
+            src = source.at[c]
+            _, found = swept(src, src, scale, 1, 8, rows, False, turn(src, 1, 8, rows))
+            for k in range(tiles):
+                once[c, k, 8 : 8 + rows, :] = found[k]
+        for c in channels:
+            mids, found = swept(once.at[c], source.at[c], scale, 1, 8, rows, False, turn(once.at[c], 1, 8, rows))
+            for k in range(tiles):
+                rest[c, k, 8 : 8 + rows, :] = found[k] - mids[k]
+        for c in channels:
+            first, last = (restricted(rest.at[c], k, 8, rows // 2, 1) for k in range(tiles))
+            low = at_coarse + c * (rows // 2)
+            built[low : low + rows // 2, :] = jnp.where((lane_ids(rows // 2) & 1) == 0, first, last)
+            for k in range(tiles):
+                low = 8 * (tiles * c + k)
+                built[low : low + 8, :] = source[c, k, pl.ds(near, 8), :]
+                low = at_marks + 8 * k + 2 * c
+                built[low : low + 1, :] = other_a[c, k, pl.ds(line, 1), :]
+                built[low + 1 : low + 2, :] = other_b[c, k, pl.ds(line, 1), :]
+            base = QUARTER * c
+            for t in range(STRIP // 8):
+                at, own_at = pl.ds(start + 8 * t, 8), pl.ds(8 + start + 8 * t, 8)
+                seam = seams[t]
+                for cells, cell, lane, width in (
+                    (source[c, 0, own_at, :], 0, LEFT, SEAM),
+                    (source[c, tiles - 1, own_at, :], LANES - SEAM, RIGHT - SEAM, SEAM),
+                    (other_a[c, 0, at, :], 0, LEFT - 1, 1),
+                    (other_b[c, 0, at, :], 0, LEFT - 2, 1),
+                    (other_a[c, tiles - 1, at, :], LANES - 1, RIGHT, 1),
+                    (other_b[c, tiles - 1, at, :], LANES - 1, RIGHT + 1, 1),
+                ):
+                    spot = (eight >= base + lane) & (eight < base + lane + width)
+                    seam = jnp.where(spot, roll(cells, base + lane - cell), seam)
+                seams[t] = seam
+        for t in range(STRIP // 8):
+            slot = 2 * (t & 1)
+            if slot == 0:
+                packed = jnp.zeros((8, LANES), jnp.float32)
+            packed = jnp.where((place >> 3) == slot, roll(seams[t], 8 * slot - (LEFT - 2)), packed)
+            packed = jnp.where((place >> 3) == slot + 1, roll(seams[t], 8 * slot + 8 - (RIGHT - SEAM)), packed)
+            built[at_seam + 8 * (t // 2) : at_seam + 8 * (t // 2) + 8, :] = packed
         for k in range(tiles):
-            for edge in (7, 8 + rows):
-                picked[k, edge : edge + 1, :] = jnp.zeros((1, LANES), jnp.float32)
-        packed = jnp.zeros((8, LANES), jnp.float32)
-        for c in range(chans):
-            for k in range(tiles):
-                at = pl.ds(k * LANES, LANES)
-                for r, n in spans(0, rows):
-                    x = x_ref[c, r : r + n, at]
-                    from_a, from_b = a_ref[c, r : r + n, at] - x, b_ref[c, r : r + n, at] - x
-                    other_a[k, r : r + n, :], other_b[k, r : r + n, :] = from_a, from_b
-                    picked[k, 8 + r : 8 + r + n, :] = jnp.where(second, from_b, from_a)
-            start = pl.multiple_of(low, 8)
-            parts = [[picked[k, pl.ds(start + 8 + s, STRIP), :] for k in range(tiles)] for s in (0, -1, 1)]
-            for k, found in enumerate(own_source(*parts, active)):
-                built[k, c * STRIP : (c + 1) * STRIP, :] = found
-            for k in range(tiles):
-                built[k, pl.ds(c * STRIP + spot, 1), :] = other_a[k, pl.ds(line, 1), :]
-                built[k, pl.ds(c * STRIP + spot + 1, 1), :] = other_b[k, pl.ds(line, 1), :]
-            for t in range(STRIP // 8):
-                lane = QUARTER * c + 4 * t
-                at = pl.ds(start + 8 * t, 8)
-                packed = jnp.where(eight == lane, roll(other_b[0, at, :], lane), packed)
-                packed = jnp.where(eight == lane + 1, roll(other_a[0, at, :], lane + 1), packed)
-                packed = jnp.where(eight == lane + 2, roll(other_a[tiles - 1, at, :], lane + 3), packed)
-                packed = jnp.where(eight == lane + 3, roll(other_b[tiles - 1, at, :], lane + 4), packed)
-        built[0, chans * STRIP :, :] = packed
-        for k in range(1, tiles):
-            built[k, chans * STRIP :, :] = jnp.where(eight < HALF, active, marked)
+            low = at_marks + 8 * k + 2 * chans
+            built[low : low + 1, :] = jnp.full((1, LANES), active)
+            built[low + 1 : low + 2, :] = jnp.full((1, LANES), marked)
 
         by_odd = top == even_at("group")
 
@@ -283,7 +324,6 @@
 ):
     chans, tiles, height, _ = source_ref.shape
     rows = height - 2 * HALO
-    tail = chans * STRIP
     row_even, col_even = even_at("group"), even_at("blk")
     active = cover_ref[0, 0].astype(jnp.float32)
     marked = label_ref[0, 0].astype(jnp.float32)
@@ -291,26 +331,31 @@
 
     place = eight & (QUARTER - 1)
 
+    at_coarse, at_seam, at_marks = strip_rows(chans, tiles)
+
     def take(top, got):
-        low = FIRST if top else HALO + rows
-        their_spot = 0 if top else STRIP - 2
-        my_spot = 0 if top else 2
+        near = HALO - 8 if top else HALO + rows
+        mine = lines[0 if top else 1]
         edge = HALO if top else HALO + rows - 1
         other = edge - 1 if top else edge + 1
-        packed = got[0, tail:, :]
-        marks = got[1, tail:, :]
-        their_active = jnp.broadcast_to(marks[0:1, 0:1], (1, LANES))
-        their_mark = jnp.broadcast_to(marks[0:1, HALF : HALF + 1], (1, LANES))
+        their_active = got[at_marks + 2 * chans : at_marks + 2 * chans + 1, :]
+        their_mark = got[at_marks + 2 * chans + 1 : at_marks + 2 * chans + 2, :]
         band = 0 if top else 2
         marks_ref[band : band + 1, :] = their_active
         marks_ref[band + 3 : band + 4, :] = their_mark
+        half_halo = HALO // 2
+        coarse_at = 0 if top else (height - HALO) // 2
+        even_cell = (lane_ids(half_halo) & 1) == 0
         for c in range(chans):
-            for k in range(tiles):
-                source_ref[c, k, low : low + STRIP, :] = got[k, c * STRIP : (c + 1) * STRIP, :]
-                their_a = got[k, c * STRIP + their_spot : c * STRIP + their_spot + 1, :]
-                their_b = got[k, c * STRIP + their_spot + 1 : c * STRIP + their_spot + 2, :]
-                my_a = lines[k, 4 * c + my_spot : 4 * c + my_spot + 1, :]
-                my_b = lines[k, 4 * c + my_spot + 1 : 4 * c + my_spot + 2, :]
+            cells = got[at_coarse + c * half_halo : at_coarse + (c + 1) * half_halo, :]
+            at = pl.ds(coarse_at, half_halo)
+            coarse_ref[c, 0, at, :] = jnp.where(even_cell, cells, roll(cells, 1))
+            coarse_ref[c, 1, at, :] = jnp.where(even_cell, roll(cells, -1), cells)
+            for k in range(tiles):
+                source_ref[c, k, near : near + 8, :] = got[8 * (tiles * c + k) : 8 * (tiles * c + k) + 8, :]
+                low = at_marks + 8 * k + 2 * c
+                their_a, their_b = got[low : low + 1, :], got[low + 1 : low + 2, :]
+                my_a, my_b = mine[k, 2 * c : 2 * c + 1, :], mine[k, 2 * c + 1 : 2 * c + 2, :]
                 for_mine = NEAR * active * jnp.where(marked == 1.0, their_b, their_a)
                 for_theirs = NEAR * their_active * jnp.where(their_mark == 1.0, my_b, my_a)
                 source_ref[c, k, edge : edge + 1, :] = source_ref[c, k, edge : edge + 1, :] - for_mine
@@ -325,21 +370,28 @@
                 cells = jnp.where(spot, roll(source_ref[c, tiles - 1, r : r + 8, :], base + RIGHT), cells)
             seam_ref[r : r + 8, :] = cells
 
+        in_left = (place >= LEFT - 2) & (place < LEFT + SEAM)
+        in_right = (place >= RIGHT - SEAM) & (place < RIGHT + 2)
         for t in range(STRIP // 8):
-            firsts, lasts = roll(packed, LEFT - 2 - 4 * t), roll(packed, RIGHT - 2 - 4 * t)
-            cells = jnp.where((place == LEFT - 2) | (place == LEFT - 1), firsts, 0.0)
-            cells = jnp.where((place == RIGHT) | (place == RIGHT + 1), lasts, cells)
-            seam_of(low + 8 * t, jnp.where(eight < QUARTER * chans, cells, 0.0))
+            packed = got[at_seam + 8 * (t // 2) : at_seam + 8 * (t // 2) + 8, :]
+            slot = 2 * (t & 1)
+            firsts = jnp.where(in_left, roll(packed, LEFT - 2 - 8 * slot), 0.0)
+            cells = jnp.where(in_right, roll(packed, RIGHT - SEAM - 8 * slot - 8), firsts)
+            cells = jnp.where(eight < QUARTER * chans, cells, 0.0)
+            r = (FIRST if top else HALO + rows) + 8 * t
+            if r == near:
+                seam_of(r, cells)
+            else:
+                seam_ref[r : r + 8, :] = cells
         r = edge // 8 * 8
         seam_of(r, seam_ref[r : r + 8, :])
 
     def arrange(upper, lower, mine_up, mine_low):
         upper_got[...] = upper[...]
         lower_got[...] = lower[...]
-        for c in range(chans):
-            for k in range(tiles):
-                lines[k, 4 * c : 4 * c + 2, :] = mine_up[k, (c + 1) * STRIP - 2 : (c + 1) * STRIP, :]
-                lines[k, 4 * c + 2 : 4 * c + 4, :] = mine_low[k, c * STRIP : c * STRIP + 2, :]
+        for k in range(tiles):
+            at = pl.ds(at_marks + 8 * k, 8)
+            lines[0, k], lines[1, k] = mine_up[at, :], mine_low[at, :]
 
     @pl.when(row_even)
     def _():
@@ -355,7 +407,8 @@
     marks_ref[4:5, :] = jnp.full((1, LANES), marked)
     marks_ref[6:8, :] = jnp.zeros((2, LANES), jnp.float32)
 
-    edges = ((FIRST, HALO, 0), (HALO, HALO + RIM, 1), (HALO + rows - RIM, HALO + rows, 1), (HALO + rows, height - FIRST, 2))
+    bottom = HALO + rows
+    edges = ((HALO - 8, HALO, 0), (HALO, HALO + RIM, 1), (bottom - RIM, bottom, 1), (bottom, bottom + 8, 2))
     spots = [(c, band, r, n) for c in range(chans) for low, high, band in edges for r, n in spans(low, high)]
     for stage in range(2):
         held = (source_ref, once_ref)[stage]
@@ -372,13 +425,9 @@
 
         staggered(spots, lambda spot: turn(held.at[spot[0]], 1, *spot[2:]), edge_sweep, 0)
     for c in range(chans):
-        for low, high in ((FIRST, HALO + RIM), (HALO + rows - RIM, height - FIRST)):
+        for low, high in ((HALO - 4, HALO + RIM), (bottom - RIM, bottom + 4)):
             for k in range(tiles):
                 coarse_ref[c, k, low // 2 : high // 2, :] = restricted(rest.at[c], k, low, (high - low) // 2, 1)
-            zeros = jnp.zeros((FIRST // 2, LANES), jnp.float32)
-        for k in range(tiles):
-            coarse_ref[c, k, 0 : FIRST // 2, :] = zeros
-            coarse_ref[c, k, (height - FIRST) // 2 : height // 2, :] = zeros
 
     cells, units = message_rows(chans, height)
     first_half = eight < HALF
@@ -723,7 +772,7 @@
     assert chans <= 4
     column = sds((height, LANES))
     coarse = sds((chans, tiles, height // 2, LANES))
-    upright = sds((tiles, chans * STRIP + 8, LANES))
+    upright = sds((strip_rows(chans, tiles)[2] + 8 * tiles, LANES))
     beside = sds((sum(message_rows(chans, height)) + 8, LANES))
 
     sent_even, sent_odd = pl.pallas_call(
@@ -732,8 +781,9 @@
         in_specs=[hbm, hbm, hbm, smem, smem],
         out_specs=(vmem, vmem),
         scratch_shapes=[pltpu.VMEM((2, chans, HALO, cols), f32)] * 3
-        + [pltpu.VMEM((tiles, HALO + 16, LANES), f32)]
-        + [pltpu.VMEM((tiles, HALO, LANES), f32)] * 2
+        + [pltpu.VMEM((chans, tiles, HALO + 16, LANES), f32)]
+        + [pltpu.VMEM((chans, tiles, HALO, LANES), f32)] * 2
+        + [pltpu.VMEM((chans, tiles, HALO + 16, LANES), f32)] * 3
         + [pltpu.VMEM(upright.shape, f32), pltpu.SemaphoreType.DMA((3, 2))],
         compiler_params=pltpu.CompilerParams(vmem_limit_bytes=56_000_000),
         name="strips",
@@ -760,7 +810,7 @@
         input_output_aliases={0: 0, 1: 1, 2: 2, 3: 3},
         scratch_shapes=[pltpu.VMEM(central.shape, f32), pltpu.VMEM((8, LANES), f32)]
         + [pltpu.VMEM(upright.shape, f32)] * 2
-        + [pltpu.VMEM((tiles, 4 * chans, LANES), f32)]
+        + [pltpu.VMEM((2, tiles, 8, LANES), f32)]
         + [pltpu.VMEM(beside.shape, f32)] * 2,
         compiler_params=params,
         name="join_rows",

time: 29 us -> 28 us (0.966)
  waiting for transfers between devices: 5.17 us -> 4.02 us
  Pallas kernels: 13.4 us -> 13.7 us
    ppermute x1, waiting for transfers between devices: 1.16 us -> 0.01 us  [shards(): got_odd = lax.ppermute(sent_odd, 'group', swaps(group, 1))]
    pallas_call x1, Pallas kernels: 1.97 us -> 2.64 us  [shards(): pl.pallas_call(strips, out_shape=(upright, upright), in_specs=[hbm, hbm,...]
    pallas_call x1, Pallas kernels: 1.02 us -> 0.63 us  [shards(): pl.pallas_call(join_rows, out_shape=(central, central, column, coarse, be...]
    ppermute x1, starting transfers between devices: 1.93 us -> 2.23 us  [shards(): got_odd = lax.ppermute(sent_odd, 'blk', swaps(blk, 1))]
    ppermute x1, starting transfers between devices: 1.65 us -> 1.35 us  [shards(): got_even = lax.ppermute(sent_even, 'blk', swaps(blk, 0))]
  transfers between devices with their start and end apart: 4 -> 4, of which waited for: 2 -> 1; matrix products, arithmetic and copies ran while one was open for 0% -> 0% of each run, Pallas kernels for 11% -> 11%
where the time goes in v5:
time: 28 us; the launch traced here: 27.8 us
  Pallas kernels  13.7 us (49%)
  starting transfers between devices  8.69 us (31%)
  waiting for transfers between devices  4.02 us (14%)
  between operations  1.4 us (5%)
    pallas_call x1, Pallas kernels, shards(): pl.pallas_call(cycle, out_shape=sds((chans, rows, cols)), in_specs=[vmem]...  7.38 us
    ppermute x1, starting transfers between devices, shards(): got_odd = lax.ppermute(sent_odd, 'group', swaps(group, 1))  4.6 us
    ppermute x1, waiting for transfers between devices, shards(): got_odd = lax.ppermute(sent_odd, 'blk', swaps(blk, 1))  4.01 us
    pallas_call x1, Pallas kernels, shards(): pl.pallas_call(inside, out_shape=(central, central, column, coarse), in_s...  3.05 us
    pallas_call x1, Pallas kernels, shards(): pl.pallas_call(strips, out_shape=(upright, upright), in_specs=[hbm, hbm,...  2.64 us
    ppermute x1, starting transfers between devices, shards(): got_odd = lax.ppermute(sent_odd, 'blk', swaps(blk, 1))  2.23 us
    ppermute x1, starting transfers between devices, shards(): got_even = lax.ppermute(sent_even, 'blk', swaps(blk, 0))  1.35 us
    pallas_call x1, Pallas kernels, shards(): pl.pallas_call(join_rows, out_shape=(central, central, column, coarse, be...  0.63 us
  transfers between devices with their start and end apart: 4, of which 1 were waited for; matrix products, arithmetic and copies ran while one was open for 0% of the time, Pallas kernels for 11%

profile of v5, /device:TPU:12, one launch (start us, length us, event | category | flops | bytes accessed | tf_op | source)
XLA Modules:
  0.0 27.8 jit_solution(4089620993620340336)
XLA Ops:
  1.3 0.0 copy-start
  1.3 0.0 copy-start.1
  1.3 0.0 copy-start.2
  1.3 2.6 %strips.1 = (f32[192,128]{1,0:T(8,128)S(1)}, f32[192,128]{1,0:T(8,128)S(1)}) custom-call(f32[3,256,256]{2,1,0:T(8,128)} %a_hbm.1, f32[3,256,256]{2,1,0:T(8,128)} %b_hbm.1, f32[3,256,256]{2,1,0:T(8,128)} %x_ref.3, s32[1,1]{1,0:T(1,128)S(6)} %copy.14.cover_ref, s32[1,1]{1,0:T(1,128)S(6)} %copy.15.label_ref), custom_call_target="tpu_custom_call" | custom-call | tf_op jit(solution)/shard_map/strips/pallas_call | solution.py:778
  4.0 0.5 %collective-permute-start = (f32[192,128]{1,0:T(8,128)S(1)}, f32[192,128]{1,0:T(8,128)S(1)}, u32[]{:S(2)}, u32[]{:S(2)}) collective-permute-start(f32[192,128]{1,0:T(8,128)S(1)} %get-tuple-element.21.sent_even), channel_id=1, source_target_pairs={{0,8},{16,24},{8,0},{24,16},{1,9},{17,25},{9,1},{25,17},{2,10},{18... | collective-permute-start | bytes 294920 | tf_op jit(solution)/shard_map/ppermute | solution.py:791
  4.5 4.6 %collective-permute-start.1 = (f32[192,128]{1,0:T(8,128)S(1)}, f32[192,128]{1,0:T(8,128)S(1)}, u32[]{:S(2)}, u32[]{:S(2)}) collective-permute-start(f32[192,128]{1,0:T(8,128)S(1)} %get-tuple-element.22.sent_odd), channel_id=1, source_target_pairs={{8,16},{16,8},{9,17},{17,9},{10,18},{18,10},{11,19},{19,11},{12,20... | collective-permute-start | bytes 294920 | tf_op jit(solution)/shard_map/ppermute | solution.py:792
  9.1 0.0 copy-done
  9.1 0.0 copy-done.1
  9.1 0.0 copy-done.2
  9.1 3.0 %inside.1 = (f32[3,2,384,128]{3,2,1,0:T(8,128)S(1)}, f32[3,2,384,128]{3,2,1,0:T(8,128)S(1)}, f32[384,128]{1,0:T(8,128)S(1)}, f32[3,2,192,128]{3,2,1,0:T(8,128)S(1)}) custom-call(f32[3,256,256]{2,1,0:T(8,128)S(1)} %copy-done.1, f32[3,256,256]{2,1,0:T(8,128)S(1)} %copy-done.2, f32[3,256,256]{2,1,0:T(8,128)S(1)} %copy-done, s32[1,1]{1,0:T(1,128)S(6)} %copy.14.cover_ref, ...), custom_call_target="tpu_custom_call" | custom-call | flops 200000000 | bytes 4000000 | tf_op jit(solution)/shard_map/inside/pallas_call | solution.py:794
  12.2 0.0 collective-permute-done.got_even
  12.2 0.0 collective-permute-done.1.got_odd
  12.2 0.6 %join_rows.1 = (f32[3,2,384,128]{3,2,1,0:T(8,128)S(1)}, f32[3,2,384,128]{3,2,1,0:T(8,128)S(1)}, f32[384,128]{1,0:T(8,128)S(1)}, f32[3,2,192,128]{3,2,1,0:T(8,128...) custom-call(f32[3,2,384,128]{3,2,1,0:T(8,128)S(1)} %get-tuple-elemen, ...), custom_call_target="tpu_custom_call", output_to_operand_aliasing={{0}: (0, {}), {1}: (1, {}), {2}: (2, {}), {3}: (3, {})} | custom-call | tf_op jit(solution)/shard_map/join_rows/pallas_call | solution.py:805
  12.8 2.2 %collective-permute-start.3 = (f32[248,128]{1,0:T(8,128)S(1)}, f32[248,128]{1,0:T(8,128)S(1)}, u32[]{:S(2)}, u32[]{:S(2)}) collective-permute-start(f32[248,128]{1,0:T(8,128)S(1)} %get-tuple-element.28), channel_id=1, source_target_pairs={{1,2},{3,4},{5,6},{2,1},{4,3},{6,5},{9,10},{11,12},{13,14},{10,9},... | collective-permute-start | bytes 380936 | tf_op jit(solution)/shard_map/ppermute | solution.py:819
  15.1 1.4 %collective-permute-start.2 = (f32[248,128]{1,0:T(8,128)S(1)}, f32[248,128]{1,0:T(8,128)S(1)}, u32[]{:S(2)}, u32[]{:S(2)}) collective-permute-start(f32[248,128]{1,0:T(8,128)S(1)} %get-tuple-element.27.sent_even), channel_id=1, source_target_pairs={{0,1},{2,3},{4,5},{6,7},{1,0},{3,2},{5,4},{7,6},{8,9},{10,11},{12,... | collective-permute-start | bytes 380936 | tf_op jit(solution)/shard_map/ppermute | solution.py:818
  16.4 4.0 %collective-permute-done.3.got_odd = f32[248,128]{1,0:T(8,128)S(1)} collective-permute-done((f32[248,128]{1,0:T(8,128)S(1)}, f32[248,128]{1,0:T(8,128)S(1)}, u32[]{:S(2)}, u32[]{:S(2)}) %collective-permute-start.3) | collective-permute-done | bytes 127008 | tf_op jit(solution)/shard_map/ppermute | solution.py:819
  20.4 0.0 collective-permute-done.2.got_even
  20.4 7.4 %cycle.1 = f32[3,256,256]{2,1,0:T(8,128)} custom-call(f32[3,2,384,128]{3,2,1,0:T(8,128)S(1)} %get-tuple-element.23.source_in, f32[3,2,384,128]{3,2,1,0:T(8,128)S(1)} %get-tuple-element.24.once_in, f32[384,128]{1,0:T(8,128)S(1)} %get-tuple-element.25.seam_in, f32[3,2,192,128]{3,2,1,0:T(8,128)S(1)} %get-tuple-element.26.coarse_in, ...), custom_call_target="tpu_custom_call" | custom-call | tf_op jit(solution)/shard_map/cycle/pallas_call | solution.py:828
Async XLA Ops:
  1.3 7.8 %copy-start = (f32[3,256,256]{2,1,0:T(8,128)S(1)}, f32[3,256,256]{2,1,0:T(8,128)}, u32[]{:S(2)}) copy-start(f32[3,256,256]{2,1,0:T(8,128)} %x_ref.3) | copy-start | bytes 2359300
  1.3 7.8 %copy-start.1 = (f32[3,256,256]{2,1,0:T(8,128)S(1)}, f32[3,256,256]{2,1,0:T(8,128)}, u32[]{:S(2)}) copy-start(f32[3,256,256]{2,1,0:T(8,128)} %a_hbm.1) | copy-start | bytes 2359300
  1.3 7.8 %copy-start.2 = (f32[3,256,256]{2,1,0:T(8,128)S(1)}, f32[3,256,256]{2,1,0:T(8,128)}, u32[]{:S(2)}) copy-start(f32[3,256,256]{2,1,0:T(8,128)} %b_hbm.1) | copy-start | bytes 2359300
  4.0 8.2 %collective-permute-start = (f32[192,128]{1,0:T(8,128)S(1)}, f32[192,128]{1,0:T(8,128)S(1)}, u32[]{:S(2)}, u32[]{:S(2)}) collective-permute-start(f32[192,128]{1,0:T(8,128)S(1)} %get-tuple-element.21.sent_even), channel_id=1, source_target_pairs={{0,8},{16,24},{8,0},{24,16},{1,9},{17,25},{9,1},{25,17},{2,10},{18... | collective-permute-start | bytes 294920 | tf_op jit(solution)/shard_map/ppermute | solution.py:791
  4.5 7.7 %collective-permute-start.1 = (f32[192,128]{1,0:T(8,128)S(1)}, f32[192,128]{1,0:T(8,128)S(1)}, u32[]{:S(2)}, u32[]{:S(2)}) collective-permute-start(f32[192,128]{1,0:T(8,128)S(1)} %get-tuple-element.22.sent_odd), channel_id=1, source_target_pairs={{8,16},{16,8},{9,17},{17,9},{10,18},{18,10},{11,19},{19,11},{12,20... | collective-permute-start | bytes 294920 | tf_op jit(solution)/shard_map/ppermute | solution.py:792
  12.8 7.6 %collective-permute-start.3 = (f32[248,128]{1,0:T(8,128)S(1)}, f32[248,128]{1,0:T(8,128)S(1)}, u32[]{:S(2)}, u32[]{:S(2)}) collective-permute-start(f32[248,128]{1,0:T(8,128)S(1)} %get-tuple-element.28), channel_id=1, source_target_pairs={{1,2},{3,4},{5,6},{2,1},{4,3},{6,5},{9,10},{11,12},{13,14},{10,9},... | collective-permute-start | bytes 380936 | tf_op jit(solution)/shard_map/ppermute | solution.py:819
  15.1 5.4 %collective-permute-start.2 = (f32[248,128]{1,0:T(8,128)S(1)}, f32[248,128]{1,0:T(8,128)S(1)}, u32[]{:S(2)}, u32[]{:S(2)}) collective-permute-start(f32[248,128]{1,0:T(8,128)S(1)} %get-tuple-element.27.sent_even), channel_id=1, source_target_pairs={{0,1},{2,3},{4,5},{6,7},{1,0},{3,2},{5,4},{7,6},{8,9},{10,11},{12,... | collective-permute-start | bytes 380936 | tf_op jit(solution)/shard_map/ppermute | solution.py:818

commit v6 on v5

--- a/solution.py
+++ b/solution.py
@@ -705,13 +705,14 @@
 
         return tile
 
-    def finish(c, _):
+    for c in range(chans):
         for r, n in spans(low // 2, high // 2):
             scale = scales(1, r, n)
             for k in range(tiles):
                 value = fix[c, k, 8 + r : 8 + r + n, :] * (scale[k] * (1.0 / NEAR))
-                fine[k, pl.ds(8 + 2 * r, n, stride=2), :] = value
-                fine[k, pl.ds(9 + 2 * r, n, stride=2), :] = value
+                fine[c, k, pl.ds(8 + 2 * r, n, stride=2), :] = value
+                fine[c, k, pl.ds(9 + 2 * r, n, stride=2), :] = value
+    for c in range(chans):
         for r, n in spans(low, high):
             ids = lane_ids(n)
             by_left, by_right = at_borders(seam_once[0, r : r + n, :], c)
@@ -722,32 +723,26 @@
                     value = jnp.where(ids < 2, by_left, value)
                 if k == own_tiles - 1:
                     value = jnp.where(ids >= LANES - 2, by_right, value)
-                fine[k, at, :] = fine[k, at, :] + value
-            fine[own_tiles, at, :] = fine[own_tiles, at, :] + jnp.where(ids < HALF, by_right, by_left)
-        add = fine_source(c)
-
-        def first(piece, turned):
-            r, n = piece
-            _, found = swept(fine, add, scales(0, r, n), 1, 8 + r, n, True, turned)
-            for k in range(tiles):
-                fine_two[k, 8 + r : 8 + r + n, :] = found[k]
-
-        def last(piece, turned):
-            r, n = piece
-            _, found = swept(fine_two, add, scales(0, r, n), 1, 8 + r, n, True, turned, own_tiles)
+                fine[c, k, at, :] = fine[c, k, at, :] + value
+            fine[c, own_tiles, at, :] = fine[c, own_tiles, at, :] + jnp.where(ids < HALF, by_right, by_left)
+    for c in range(chans):
+        add, src = fine_source(c), fine.at[c]
+        for r, n in spans(low, high):
+            _, found = swept(src, add, scales(0, r, n), 1, 8 + r, n, True, turn(src, 1, 8 + r, n))
+            for k in range(tiles):
+                fine_two[c, k, 8 + r : 8 + r + n, :] = found[k]
+
+    def leave(c):
+        return pltpu.make_async_copy(out_ref.at[c], out_hbm.at[c], sems.at[c])
+
+    for c in range(chans):
+        add, src = fine_source(c), fine_two.at[c]
+        for r, n in spans(HALO, HALO + rows):
+            _, found = swept(src, add, scales(0, r, n), 1, 8 + r, n, True, turn(src, 1, 8 + r, n), own_tiles)
             for k in range(own_tiles):
                 at = pl.ds(k * LANES, LANES)
                 out_ref[c, r - HALO : r - HALO + n, at] = x_ref[c, r - HALO : r - HALO + n, at] + found[k]
-
-        staggered(spans(low, high), lambda piece: turn(fine, 1, 8 + piece[0], piece[1]), first, 0)
-        staggered(spans(HALO, HALO + rows), lambda piece: turn(fine_two, 1, 8 + piece[0], piece[1]), last, 0)
         leave(c).start()
-        return 0
-
-    def leave(c):
-        return pltpu.make_async_copy(out_ref.at[c], out_hbm.at[c], sems.at[c])
-
-    lax.fori_loop(0, chans, finish, 0)
     for c in range(chans):
         leave(c).wait()
 
@@ -820,7 +815,7 @@
 
     scratch = [pltpu.VMEM(image_a.shape, f32), pltpu.SemaphoreType.DMA((chans,))]
     scratch += [pltpu.VMEM(beside.shape, f32)] * 2 + [pltpu.VMEM((1, height, LANES), f32)] * 3
-    scratch += [pltpu.VMEM((tiles + 1, height + 16, LANES), f32)] * 2
+    scratch += [pltpu.VMEM((chans, tiles + 1, height + 16, LANES), f32)] * 2
     scratch += [pltpu.VMEM((chans, tiles + 1, height // 2 + 16, LANES), f32)]
     for depth in range(1, LEVELS):
         fields = (chans + 1) // 2 if depth == 1 else 1

time: 28 us -> 27.8 us (level)
  no operation moved by 1% of the time
where the time goes in v6:
time: 27.8 us; the launch traced here: 27.7 us
  Pallas kernels  13.5 us (49%)
  starting transfers between devices  8.69 us (31%)
  waiting for transfers between devices  4.02 us (14%)
  between operations  1.4 us (5%)
    pallas_call x1, Pallas kernels, shards(): pl.pallas_call(cycle, out_shape=sds((chans, rows, cols)), in_specs=[vmem]...  7.21 us
    ppermute x1, starting transfers between devices, shards(): got_odd = lax.ppermute(sent_odd, 'group', swaps(group, 1))  4.6 us
    ppermute x1, waiting for transfers between devices, shards(): got_odd = lax.ppermute(sent_odd, 'blk', swaps(blk, 1))  4.01 us
    pallas_call x1, Pallas kernels, shards(): pl.pallas_call(inside, out_shape=(central, central, column, coarse), in_s...  3.05 us
    pallas_call x1, Pallas kernels, shards(): pl.pallas_call(strips, out_shape=(upright, upright), in_specs=[hbm, hbm,...  2.64 us
    ppermute x1, starting transfers between devices, shards(): got_odd = lax.ppermute(sent_odd, 'blk', swaps(blk, 1))  2.23 us
    ppermute x1, starting transfers between devices, shards(): got_even = lax.ppermute(sent_even, 'blk', swaps(blk, 0))  1.35 us
    pallas_call x1, Pallas kernels, shards(): pl.pallas_call(join_rows, out_shape=(central, central, column, coarse, be...  0.63 us
  transfers between devices with their start and end apart: 4, of which 1 were waited for; matrix products, arithmetic and copies ran while one was open for 0% of the time, Pallas kernels for 11%

profile of v6, /device:TPU:12, one launch (start us, length us, event | category | flops | bytes accessed | tf_op | source)
XLA Modules:
  0.0 27.7 jit_solution(8273940612337902602)
XLA Ops:
  1.3 0.0 copy-start
  1.3 0.0 copy-start.1
  1.3 0.0 copy-start.2
  1.3 2.6 %strips.1 = (f32[192,128]{1,0:T(8,128)S(1)}, f32[192,128]{1,0:T(8,128)S(1)}) custom-call(f32[3,256,256]{2,1,0:T(8,128)} %a_hbm.1, f32[3,256,256]{2,1,0:T(8,128)} %b_hbm.1, f32[3,256,256]{2,1,0:T(8,128)} %x_ref.3, s32[1,1]{1,0:T(1,128)S(6)} %copy.14.cover_ref, s32[1,1]{1,0:T(1,128)S(6)} %copy.15.label_ref), custom_call_target="tpu_custom_call" | custom-call | tf_op jit(solution)/shard_map/strips/pallas_call | solution.py:773
  4.0 0.5 %collective-permute-start = (f32[192,128]{1,0:T(8,128)S(1)}, f32[192,128]{1,0:T(8,128)S(1)}, u32[]{:S(2)}, u32[]{:S(2)}) collective-permute-start(f32[192,128]{1,0:T(8,128)S(1)} %get-tuple-element.21.sent_even), channel_id=1, source_target_pairs={{0,8},{16,24},{8,0},{24,16},{1,9},{17,25},{9,1},{25,17},{2,10},{18... | collective-permute-start | bytes 294920 | tf_op jit(solution)/shard_map/ppermute | solution.py:786
  4.5 4.6 %collective-permute-start.1 = (f32[192,128]{1,0:T(8,128)S(1)}, f32[192,128]{1,0:T(8,128)S(1)}, u32[]{:S(2)}, u32[]{:S(2)}) collective-permute-start(f32[192,128]{1,0:T(8,128)S(1)} %get-tuple-element.22.sent_odd), channel_id=1, source_target_pairs={{8,16},{16,8},{9,17},{17,9},{10,18},{18,10},{11,19},{19,11},{12,20... | collective-permute-start | bytes 294920 | tf_op jit(solution)/shard_map/ppermute | solution.py:787
  9.1 0.0 copy-done
  9.1 0.0 copy-done.1
  9.1 0.0 copy-done.2
  9.1 3.0 %inside.1 = (f32[3,2,384,128]{3,2,1,0:T(8,128)S(1)}, f32[3,2,384,128]{3,2,1,0:T(8,128)S(1)}, f32[384,128]{1,0:T(8,128)S(1)}, f32[3,2,192,128]{3,2,1,0:T(8,128)S(1)}) custom-call(f32[3,256,256]{2,1,0:T(8,128)S(1)} %copy-done.1, f32[3,256,256]{2,1,0:T(8,128)S(1)} %copy-done.2, f32[3,256,256]{2,1,0:T(8,128)S(1)} %copy-done, s32[1,1]{1,0:T(1,128)S(6)} %copy.14.cover_ref, ...), custom_call_target="tpu_custom_call" | custom-call | flops 200000000 | bytes 4000000 | tf_op jit(solution)/shard_map/inside/pallas_call | solution.py:789
  12.2 0.0 collective-permute-done.got_even
  12.2 0.0 collective-permute-done.1.got_odd
  12.2 0.6 %join_rows.1 = (f32[3,2,384,128]{3,2,1,0:T(8,128)S(1)}, f32[3,2,384,128]{3,2,1,0:T(8,128)S(1)}, f32[384,128]{1,0:T(8,128)S(1)}, f32[3,2,192,128]{3,2,1,0:T(8,128...) custom-call(f32[3,2,384,128]{3,2,1,0:T(8,128)S(1)} %get-tuple-elemen, ...), custom_call_target="tpu_custom_call", output_to_operand_aliasing={{0}: (0, {}), {1}: (1, {}), {2}: (2, {}), {3}: (3, {})} | custom-call | tf_op jit(solution)/shard_map/join_rows/pallas_call | solution.py:800
  12.8 2.2 %collective-permute-start.3 = (f32[248,128]{1,0:T(8,128)S(1)}, f32[248,128]{1,0:T(8,128)S(1)}, u32[]{:S(2)}, u32[]{:S(2)}) collective-permute-start(f32[248,128]{1,0:T(8,128)S(1)} %get-tuple-element.28), channel_id=1, source_target_pairs={{1,2},{3,4},{5,6},{2,1},{4,3},{6,5},{9,10},{11,12},{13,14},{10,9},... | collective-permute-start | bytes 380936 | tf_op jit(solution)/shard_map/ppermute | solution.py:814
  15.1 1.4 %collective-permute-start.2 = (f32[248,128]{1,0:T(8,128)S(1)}, f32[248,128]{1,0:T(8,128)S(1)}, u32[]{:S(2)}, u32[]{:S(2)}) collective-permute-start(f32[248,128]{1,0:T(8,128)S(1)} %get-tuple-element.27.sent_even), channel_id=1, source_target_pairs={{0,1},{2,3},{4,5},{6,7},{1,0},{3,2},{5,4},{7,6},{8,9},{10,11},{12,... | collective-permute-start | bytes 380936 | tf_op jit(solution)/shard_map/ppermute | solution.py:813
  16.4 4.0 %collective-permute-done.3.got_odd = f32[248,128]{1,0:T(8,128)S(1)} collective-permute-done((f32[248,128]{1,0:T(8,128)S(1)}, f32[248,128]{1,0:T(8,128)S(1)}, u32[]{:S(2)}, u32[]{:S(2)}) %collective-permute-start.3) | collective-permute-done | bytes 127008 | tf_op jit(solution)/shard_map/ppermute | solution.py:814
  20.4 0.0 collective-permute-done.2.got_even
  20.4 7.2 %cycle.1 = f32[3,256,256]{2,1,0:T(8,128)} custom-call(f32[3,2,384,128]{3,2,1,0:T(8,128)S(1)} %get-tuple-element.23.source_in, f32[3,2,384,128]{3,2,1,0:T(8,128)S(1)} %get-tuple-element.24.once_in, f32[384,128]{1,0:T(8,128)S(1)} %get-tuple-element.25.seam_in, f32[3,2,192,128]{3,2,1,0:T(8,128)S(1)} %get-tuple-element.26.coarse_in, ...), custom_call_target="tpu_custom_call" | custom-call | tf_op jit(solution)/shard_map/cycle/pallas_call | solution.py:823
Async XLA Ops:
  1.3 7.8 %copy-start = (f32[3,256,256]{2,1,0:T(8,128)S(1)}, f32[3,256,256]{2,1,0:T(8,128)}, u32[]{:S(2)}) copy-start(f32[3,256,256]{2,1,0:T(8,128)} %x_ref.3) | copy-start | bytes 2359300
  1.3 7.8 %copy-start.1 = (f32[3,256,256]{2,1,0:T(8,128)S(1)}, f32[3,256,256]{2,1,0:T(8,128)}, u32[]{:S(2)}) copy-start(f32[3,256,256]{2,1,0:T(8,128)} %a_hbm.1) | copy-start | bytes 2359300
  1.3 7.8 %copy-start.2 = (f32[3,256,256]{2,1,0:T(8,128)S(1)}, f32[3,256,256]{2,1,0:T(8,128)}, u32[]{:S(2)}) copy-start(f32[3,256,256]{2,1,0:T(8,128)} %b_hbm.1) | copy-start | bytes 2359300
  4.0 8.2 %collective-permute-start = (f32[192,128]{1,0:T(8,128)S(1)}, f32[192,128]{1,0:T(8,128)S(1)}, u32[]{:S(2)}, u32[]{:S(2)}) collective-permute-start(f32[192,128]{1,0:T(8,128)S(1)} %get-tuple-element.21.sent_even), channel_id=1, source_target_pairs={{0,8},{16,24},{8,0},{24,16},{1,9},{17,25},{9,1},{25,17},{2,10},{18... | collective-permute-start | bytes 294920 | tf_op jit(solution)/shard_map/ppermute | solution.py:786
  4.5 7.7 %collective-permute-start.1 = (f32[192,128]{1,0:T(8,128)S(1)}, f32[192,128]{1,0:T(8,128)S(1)}, u32[]{:S(2)}, u32[]{:S(2)}) collective-permute-start(f32[192,128]{1,0:T(8,128)S(1)} %get-tuple-element.22.sent_odd), channel_id=1, source_target_pairs={{8,16},{16,8},{9,17},{17,9},{10,18},{18,10},{11,19},{19,11},{12,20... | collective-permute-start | bytes 294920 | tf_op jit(solution)/shard_map/ppermute | solution.py:787
  12.8 7.6 %collective-permute-start.3 = (f32[248,128]{1,0:T(8,128)S(1)}, f32[248,128]{1,0:T(8,128)S(1)}, u32[]{:S(2)}, u32[]{:S(2)}) collective-permute-start(f32[248,128]{1,0:T(8,128)S(1)} %get-tuple-element.28), channel_id=1, source_target_pairs={{1,2},{3,4},{5,6},{2,1},{4,3},{6,5},{9,10},{11,12},{13,14},{10,9},... | collective-permute-start | bytes 380936 | tf_op jit(solution)/shard_map/ppermute | solution.py:814
  15.1 5.4 %collective-permute-start.2 = (f32[248,128]{1,0:T(8,128)S(1)}, f32[248,128]{1,0:T(8,128)S(1)}, u32[]{:S(2)}, u32[]{:S(2)}) collective-permute-start(f32[248,128]{1,0:T(8,128)S(1)} %get-tuple-element.27.sent_even), channel_id=1, source_target_pairs={{0,1},{2,3},{4,5},{6,7},{1,0},{3,2},{5,4},{7,6},{8,9},{10,11},{12,... | collective-permute-start | bytes 380936 | tf_op jit(solution)/shard_map/ppermute | solution.py:813

commit v7 on v6

--- a/solution.py
+++ b/solution.py
@@ -455,7 +455,7 @@
             at = cells + 8 * tile
             left[at : at + 8, :], right[at : at + 8, :] = lefts, rights
         for out in (left, right):
-            out[cells + units : cells + units + 8, :] = marks_ref[...]
+            out[cells : cells + 8, :] = jnp.where(eight < LANES - QUARTER, out[cells : cells + 8, :], marks_ref[...])
 
     pack(left_out, right_out)
 
@@ -491,10 +491,9 @@
         right_ref[...] = got_odd[...]
         left_ref[...] = got_even[...]
 
-    at = cells + units
-
     def mark(ref, row):
-        return jnp.broadcast_to(ref[at + row : at + row + 1, :], (8, LANES))
+        cell = ref[cells + row : cells + row + 1, LANES - 1 : LANES]
+        return jnp.broadcast_to(cell, (8, LANES))
 
     own = [mark(sent_even, i) for i in range(6)]
     right = [mark(right_ref, i) for i in range(6)]
@@ -764,11 +763,11 @@
     params = pltpu.CompilerParams(vmem_limit_bytes=40 * 1024 * 1024)
     group, blk = lax.axis_size("group"), lax.axis_size("blk")
     central = sds((chans, tiles, height, LANES))
-    assert chans <= 4
+    assert chans <= 3
     column = sds((height, LANES))
     coarse = sds((chans, tiles, height // 2, LANES))
     upright = sds((strip_rows(chans, tiles)[2] + 8 * tiles, LANES))
-    beside = sds((sum(message_rows(chans, height)) + 8, LANES))
+    beside = sds((sum(message_rows(chans, height)), LANES))
 
     sent_even, sent_odd = pl.pallas_call(
         strips,

time: 27.8 us -> 27.7 us (level)
  no operation moved by 1% of the time
where the time goes in v7:
time: 27.7 us; the launch traced here: 27.5 us
  Pallas kernels  13.5 us (49%)
  starting transfers between devices  8.69 us (31%)
  waiting for transfers between devices  3.93 us (14%)
  between operations  1.4 us (5%)
    pallas_call x1, Pallas kernels, shards(): pl.pallas_call(cycle, out_shape=sds((chans, rows, cols)), in_specs=[vmem]...  7.16 us
    ppermute x1, starting transfers between devices, shards(): got_odd = lax.ppermute(sent_odd, 'group', swaps(group, 1))  4.6 us
    ppermute x1, waiting for transfers between devices, shards(): got_odd = lax.ppermute(sent_odd, 'blk', swaps(blk, 1))  3.92 us
    pallas_call x1, Pallas kernels, shards(): pl.pallas_call(inside, out_shape=(central, central, column, coarse), in_s...  3.05 us
    pallas_call x1, Pallas kernels, shards(): pl.pallas_call(strips, out_shape=(upright, upright), in_specs=[hbm, hbm,...  2.64 us
    ppermute x1, starting transfers between devices, shards(): got_odd = lax.ppermute(sent_odd, 'blk', swaps(blk, 1))  2.23 us
    ppermute x1, starting transfers between devices, shards(): got_even = lax.ppermute(sent_even, 'blk', swaps(blk, 0))  1.35 us
    pallas_call x1, Pallas kernels, shards(): pl.pallas_call(join_rows, out_shape=(central, central, column, coarse, be...  0.63 us
  transfers between devices with their start and end apart: 4, of which 1 were waited for; matrix products, arithmetic and copies ran while one was open for 0% of the time, Pallas kernels for 11%

profile of v7, /device:TPU:12, one launch (start us, length us, event | category | flops | bytes accessed | tf_op | source)
XLA Modules:
  0.0 27.5 jit_solution(4128486842920137839)
XLA Ops:
  1.3 0.0 copy-start
  1.3 0.0 copy-start.1
  1.3 0.0 copy-start.2
  1.3 2.6 %strips.1 = (f32[192,128]{1,0:T(8,128)S(1)}, f32[192,128]{1,0:T(8,128)S(1)}) custom-call(f32[3,256,256]{2,1,0:T(8,128)} %a_hbm.1, f32[3,256,256]{2,1,0:T(8,128)} %b_hbm.1, f32[3,256,256]{2,1,0:T(8,128)} %x_ref.3, s32[1,1]{1,0:T(1,128)S(6)} %copy.14.cover_ref, s32[1,1]{1,0:T(1,128)S(6)} %copy.15.label_ref), custom_call_target="tpu_custom_call" | custom-call | tf_op jit(solution)/shard_map/strips/pallas_call | solution.py:772
  4.0 0.5 %collective-permute-start = (f32[192,128]{1,0:T(8,128)S(1)}, f32[192,128]{1,0:T(8,128)S(1)}, u32[]{:S(2)}, u32[]{:S(2)}) collective-permute-start(f32[192,128]{1,0:T(8,128)S(1)} %get-tuple-element.21.sent_even), channel_id=1, source_target_pairs={{0,8},{16,24},{8,0},{24,16},{1,9},{17,25},{9,1},{25,17},{2,10},{18... | collective-permute-start | bytes 294920 | tf_op jit(solution)/shard_map/ppermute | solution.py:785
  4.5 4.6 %collective-permute-start.1 = (f32[192,128]{1,0:T(8,128)S(1)}, f32[192,128]{1,0:T(8,128)S(1)}, u32[]{:S(2)}, u32[]{:S(2)}) collective-permute-start(f32[192,128]{1,0:T(8,128)S(1)} %get-tuple-element.22.sent_odd), channel_id=1, source_target_pairs={{8,16},{16,8},{9,17},{17,9},{10,18},{18,10},{11,19},{19,11},{12,20... | collective-permute-start | bytes 294920 | tf_op jit(solution)/shard_map/ppermute | solution.py:786
  9.1 0.0 copy-done
  9.1 0.0 copy-done.1
  9.1 0.0 copy-done.2
  9.1 3.0 %inside.1 = (f32[3,2,384,128]{3,2,1,0:T(8,128)S(1)}, f32[3,2,384,128]{3,2,1,0:T(8,128)S(1)}, f32[384,128]{1,0:T(8,128)S(1)}, f32[3,2,192,128]{3,2,1,0:T(8,128)S(1)}) custom-call(f32[3,256,256]{2,1,0:T(8,128)S(1)} %copy-done.1, f32[3,256,256]{2,1,0:T(8,128)S(1)} %copy-done.2, f32[3,256,256]{2,1,0:T(8,128)S(1)} %copy-done, s32[1,1]{1,0:T(1,128)S(6)} %copy.14.cover_ref, ...), custom_call_target="tpu_custom_call" | custom-call | flops 200000000 | bytes 4000000 | tf_op jit(solution)/shard_map/inside/pallas_call | solution.py:788
  12.2 0.0 collective-permute-done.got_even
  12.2 0.0 collective-permute-done.1.got_odd
  12.2 0.6 %join_rows.1 = (f32[3,2,384,128]{3,2,1,0:T(8,128)S(1)}, f32[3,2,384,128]{3,2,1,0:T(8,128)S(1)}, f32[384,128]{1,0:T(8,128)S(1)}, f32[3,2,192,128]{3,2,1,0:T(8,128...) custom-call(f32[3,2,384,128]{3,2,1,0:T(8,128)S(1)} %get-tuple-elemen, ...), custom_call_target="tpu_custom_call", output_to_operand_aliasing={{0}: (0, {}), {1}: (1, {}), {2}: (2, {}), {3}: (3, {})} | custom-call | tf_op jit(solution)/shard_map/join_rows/pallas_call | solution.py:799
  12.8 2.2 %collective-permute-start.3 = (f32[240,128]{1,0:T(8,128)S(1)}, f32[240,128]{1,0:T(8,128)S(1)}, u32[]{:S(2)}, u32[]{:S(2)}) collective-permute-start(f32[240,128]{1,0:T(8,128)S(1)} %get-tuple-element.28), channel_id=1, source_target_pairs={{1,2},{3,4},{5,6},{2,1},{4,3},{6,5},{9,10},{11,12},{13,14},{10,9},... | collective-permute-start | bytes 368648 | tf_op jit(solution)/shard_map/ppermute | solution.py:813
  15.1 1.4 %collective-permute-start.2 = (f32[240,128]{1,0:T(8,128)S(1)}, f32[240,128]{1,0:T(8,128)S(1)}, u32[]{:S(2)}, u32[]{:S(2)}) collective-permute-start(f32[240,128]{1,0:T(8,128)S(1)} %get-tuple-element.27.sent_even), channel_id=1, source_target_pairs={{0,1},{2,3},{4,5},{6,7},{1,0},{3,2},{5,4},{7,6},{8,9},{10,11},{12,... | collective-permute-start | bytes 368648 | tf_op jit(solution)/shard_map/ppermute | solution.py:812
  16.4 3.9 %collective-permute-done.3.got_odd = f32[240,128]{1,0:T(8,128)S(1)} collective-permute-done((f32[240,128]{1,0:T(8,128)S(1)}, f32[240,128]{1,0:T(8,128)S(1)}, u32[]{:S(2)}, u32[]{:S(2)}) %collective-permute-start.3) | collective-permute-done | bytes 122912 | tf_op jit(solution)/shard_map/ppermute | solution.py:813
  20.4 0.0 collective-permute-done.2.got_even
  20.4 7.2 %cycle.1 = f32[3,256,256]{2,1,0:T(8,128)} custom-call(f32[3,2,384,128]{3,2,1,0:T(8,128)S(1)} %get-tuple-element.23.source_in, f32[3,2,384,128]{3,2,1,0:T(8,128)S(1)} %get-tuple-element.24.once_in, f32[384,128]{1,0:T(8,128)S(1)} %get-tuple-element.25.seam_in, f32[3,2,192,128]{3,2,1,0:T(8,128)S(1)} %get-tuple-element.26.coarse_in, ...), custom_call_target="tpu_custom_call" | custom-call | tf_op jit(solution)/shard_map/cycle/pallas_call | solution.py:822
Async XLA Ops:
  1.3 7.8 %copy-start = (f32[3,256,256]{2,1,0:T(8,128)S(1)}, f32[3,256,256]{2,1,0:T(8,128)}, u32[]{:S(2)}) copy-start(f32[3,256,256]{2,1,0:T(8,128)} %x_ref.3) | copy-start | bytes 2359300
  1.3 7.8 %copy-start.1 = (f32[3,256,256]{2,1,0:T(8,128)S(1)}, f32[3,256,256]{2,1,0:T(8,128)}, u32[]{:S(2)}) copy-start(f32[3,256,256]{2,1,0:T(8,128)} %a_hbm.1) | copy-start | bytes 2359300
  1.3 7.8 %copy-start.2 = (f32[3,256,256]{2,1,0:T(8,128)S(1)}, f32[3,256,256]{2,1,0:T(8,128)}, u32[]{:S(2)}) copy-start(f32[3,256,256]{2,1,0:T(8,128)} %b_hbm.1) | copy-start | bytes 2359300
  4.0 8.2 %collective-permute-start = (f32[192,128]{1,0:T(8,128)S(1)}, f32[192,128]{1,0:T(8,128)S(1)}, u32[]{:S(2)}, u32[]{:S(2)}) collective-permute-start(f32[192,128]{1,0:T(8,128)S(1)} %get-tuple-element.21.sent_even), channel_id=1, source_target_pairs={{0,8},{16,24},{8,0},{24,16},{1,9},{17,25},{9,1},{25,17},{2,10},{18... | collective-permute-start | bytes 294920 | tf_op jit(solution)/shard_map/ppermute | solution.py:785
  4.5 7.7 %collective-permute-start.1 = (f32[192,128]{1,0:T(8,128)S(1)}, f32[192,128]{1,0:T(8,128)S(1)}, u32[]{:S(2)}, u32[]{:S(2)}) collective-permute-start(f32[192,128]{1,0:T(8,128)S(1)} %get-tuple-element.22.sent_odd), channel_id=1, source_target_pairs={{8,16},{16,8},{9,17},{17,9},{10,18},{18,10},{11,19},{19,11},{12,20... | collective-permute-start | bytes 294920 | tf_op jit(solution)/shard_map/ppermute | solution.py:786
  12.8 7.5 %collective-permute-start.3 = (f32[240,128]{1,0:T(8,128)S(1)}, f32[240,128]{1,0:T(8,128)S(1)}, u32[]{:S(2)}, u32[]{:S(2)}) collective-permute-start(f32[240,128]{1,0:T(8,128)S(1)} %get-tuple-element.28), channel_id=1, source_target_pairs={{1,2},{3,4},{5,6},{2,1},{4,3},{6,5},{9,10},{11,12},{13,14},{10,9},... | collective-permute-start | bytes 368648 | tf_op jit(solution)/shard_map/ppermute | solution.py:813
  15.1 5.3 %collective-permute-start.2 = (f32[240,128]{1,0:T(8,128)S(1)}, f32[240,128]{1,0:T(8,128)S(1)}, u32[]{:S(2)}, u32[]{:S(2)}) collective-permute-start(f32[240,128]{1,0:T(8,128)S(1)} %get-tuple-element.27.sent_even), channel_id=1, source_target_pairs={{0,1},{2,3},{4,5},{6,7},{1,0},{3,2},{5,4},{7,6},{8,9},{10,11},{12,... | collective-permute-start | bytes 368648 | tf_op jit(solution)/shard_map/ppermute | solution.py:812
